TPU v7x, 128 devices: a whole 4x4x4 slice. The times are simulated.
128 devices in a mesh: seq: 32 (over x, z, core), mp: 4 (over y).
Axes of the slice: x: 4, y: 4, z: 4, core: 2. Of those that a mesh axis runs over, the one named last changes fastest.
Arguments:
- layer_in: bfloat16 [24576, 2560], P('seq'), may hold values from -6 to 6
- ssm_input: bfloat16 [24576, 5120], P('seq', 'mp'), may hold values from -6 to 6
- b_matrix: bfloat16 [24576, 128], P('seq'), may hold values from -1.796875 to 1.796875
- c_matrix: bfloat16 [24576, 128], P('seq'), may hold values from -1.796875 to 1.796875
- dt_raw: float32 [24576, 80], P('seq', 'mp'), may hold values from -2.8 to 2.8
- dt_bias: float32 [80], P('mp'), may hold values from -7 to 0
- a_log: float32 [80], P('mp'), may hold values from -8 to 3
- d_skip: float32 [80], P('mp'), may hold values from 0.5 to 1.5
- grad_out: bfloat16 [24576, 5120], P('seq', 'mp'), may hold values from -1 to 1
Outputs:
- grad_wx: float32 [2560, 5120], P('seq', 'mp')
- grad_wbc: float32 [2560, 256], P('seq', 'mp')
- grad_alog: float32 [80], P('mp')
- grad_dtbias: float32 [80], P('mp')
- grad_dskip: float32 [80], P('mp')
All inputs are finite; a program needn't handle non-finite values.
Results may differ from a plain program's by a relative error of at most 0.0063.
Values sent between devices are 32-bit elements; how exact they have to be, the bound alone decides.
A program may use at most 192 MiB of HBM per device.

v0:
```python
from functools import partial

import jax
import jax.numpy as jnp
from jax import lax
from jax.sharding import Mesh
from jax.sharding import PartitionSpec as P

GROUP = 256
SEQ = ("seq_0", "seq_1", "seq_2")


def neutral_like(array, identity):
    return jax.tree.map(
        lambda part, zero: jnp.zeros_like(part) + jnp.asarray(zero, part.dtype), array, identity
    )


def carried_in(array, axes, combine, identity, reverse):
    before = start = neutral_like(array, identity)
    subtotal = array
    for axis in reversed(axes):
        devices, mine = (lax.axis_size(axis), lax.axis_index(axis))
        pieces = jax.tree.map(lambda part: lax.all_gather(part, axis), subtotal)
        inside, subtotal = (start, start)
        for k in reversed(range(devices)) if reverse else range(devices):
            passed = k > mine if reverse else k < mine
            subtotal = combine(subtotal, jax.tree.map(lambda part: part[k], pieces))
            inside = jax.tree.map(lambda new, old: jnp.where(passed, new, old), subtotal, inside)
        before = combine(inside, before)
    return before


def in_blocks(array, dim, devices):
    dims = array.shape
    pieces = array.reshape(*dims[:dim], devices, dims[dim] // devices, *dims[dim + 1 :])
    return jnp.moveaxis(pieces, dim, 0)


def sent_and_summed(array, axis, dim):
    pieces = in_blocks(array, dim, lax.axis_size(axis))
    arrived = lax.all_to_all(pieces, axis, split_axis=0, concat_axis=0, tiled=True)
    return arrived.sum(axis=0)


def together(arrays, axis):
    flat, at, done = (jnp.concatenate([a.reshape(-1) for a in arrays]), 0, [])
    subtotal = lax.psum(flat, axis)
    for a in arrays:
        done.append(subtotal[at : at + a.size].reshape(a.shape))
        at += a.size
    return tuple(done)


def contract(form, left, right):
    return jnp.einsum(form, left, right, preferred_element_type=jnp.float32)


def matmul(left, right):
    return jnp.dot(left, right, preferred_element_type=jnp.float32)


def inner_first(left, right):
    return lax.dot_general(
        left, right, (((0,), (0,)), ((), ())), preferred_element_type=jnp.float32
    )


def inner_last(left, right):
    return lax.dot_general(
        left, right, (((1,), (1,)), ((), ())), preferred_element_type=jnp.float32
    )


def reverse_sum(values):
    return jnp.flip(jnp.cumsum(jnp.flip(values, 0), axis=0), 0)


def exclusive_sum(values):
    return jnp.cumsum(values, axis=0) - values


def head_rates(dt_raw, dt_bias, a_log):
    shifted = dt_raw + dt_bias[None, :]
    dt_step = jax.nn.softplus(shifted)
    gate_slope = jax.nn.sigmoid(shifted)
    decay_rate = -jnp.exp(a_log)
    return (dt_step, gate_slope, decay_rate, dt_step * decay_rate[None, :])


def block_states(ssm_input, grad_out, b_matrix, c_matrix, dt_step, log_step):
    tok_count, head_count = dt_step.shape
    head_dim = ssm_input.shape[1] // head_count
    state_width = b_matrix.shape[1]
    groups = tok_count // GROUP
    within = jnp.cumsum(log_step.reshape(groups, GROUP, head_count), axis=1)
    totals = within[:, -1, :]
    group_steps = dt_step.reshape(groups, GROUP, head_count)
    x_four = ssm_input.reshape(groups, GROUP, head_count, head_dim)
    dy_four = grad_out.reshape(groups, GROUP, head_count, head_dim)
    x_scaled = (x_four * (group_steps * jnp.exp(totals[:, None, :] - within))[..., None]).astype(
        jnp.bfloat16
    )
    y_scaled = (dy_four * jnp.exp(within)[..., None]).astype(jnp.bfloat16)
    b_three = b_matrix.reshape(groups, GROUP, state_width)
    c_three = c_matrix.reshape(groups, GROUP, state_width)
    state_parts = contract("kqhp,kqn->khpn", x_scaled, b_three)
    grad_parts = contract("kqhp,kqn->khpn", y_scaled, c_three)
    carry_state = jnp.zeros((head_count, head_dim, state_width), jnp.float32)
    starts = []
    for group_id in range(groups):
        starts.append(carry_state)
        carry_state = jnp.exp(totals[group_id])[:, None, None] * carry_state + state_parts[group_id]
    carry_grad = jnp.zeros((head_count, head_dim, state_width), jnp.float32)
    end_grads = [carry_grad] * groups
    for group_id in range(groups - 1, -1, -1):
        end_grads[group_id] = carry_grad
        carry_grad = grad_parts[group_id] + jnp.exp(totals[group_id])[:, None, None] * carry_grad
    cumulative = jnp.cumsum(log_step, axis=0)
    block_decay = jnp.exp(cumulative[-1])
    packed = (
        within,
        totals,
        x_scaled,
        y_scaled,
        jnp.stack(starts),
        jnp.stack(end_grads),
        cumulative,
    )
    return (block_decay, carry_state, carry_grad, packed)


def one_group(d_skip, group_item):
    x_c, dy_c, b_c, c_c, dt_c, within_c, total_c, start_c, end_c, xw_c, yw_c = group_item
    size_q = x_c.shape[0]
    state_width = b_c.shape[1]
    cross_bc = inner_last(c_c, b_c)
    positions = jnp.arange(size_q)
    lower_mask = positions[:, None] >= positions[None, :]
    strict = positions[:, None] > positions[None, :]
    lagged = within_c.T[:, :, None] - within_c.T[:, None, :]
    decayed = jnp.where(lower_mask[None], jnp.exp(jnp.where(lower_mask[None], lagged, 0.0)), 0.0)
    mix_matrix = (cross_bc[None] * decayed).astype(jnp.bfloat16)
    gb_intra = contract("hrs,rhp->shp", mix_matrix, dy_c)
    paired = contract("rhp,shp->hrs", dy_c, x_c) * decayed
    paired_dt = paired * dt_c.T[:, None, :]
    mixed_sum = jnp.sum(paired_dt, axis=0).astype(jnp.bfloat16)
    box_terms = jnp.where(strict[None], cross_bc[None] * paired_dt, 0.0)
    box_flow = jnp.sum(box_terms, axis=1) - jnp.sum(box_terms, axis=2)
    da_intra = (jnp.cumsum(box_flow, axis=1) - box_flow).T
    start_low = start_c.astype(jnp.bfloat16)
    end_low = end_c.astype(jnp.bfloat16)
    y_start = contract("hpn,qn->qhp", start_low, c_c) * jnp.exp(within_c)[:, :, None]
    gb_end = (
        contract("hpn,qn->qhp", end_low, b_c) * jnp.exp(total_c[None, :] - within_c)[:, :, None]
    )
    gb_local = gb_intra + gb_end
    dx_local = (dt_c[:, :, None] * gb_local + d_skip[None, :, None] * dy_c).astype(jnp.bfloat16)
    x_wide = x_c.astype(jnp.float32)
    dy_wide = dy_c.astype(jnp.float32)
    x_gb = jnp.sum(x_wide * gb_local, axis=2)
    backward_part = jnp.sum(dy_wide * y_start, axis=2)
    forward_part = dt_c * jnp.sum(x_wide * gb_end, axis=2)
    meeting = jnp.exp(total_c) * jnp.sum(end_c * start_c, axis=(1, 2))
    da_local = (
        da_intra + reverse_sum(backward_part) + exclusive_sum(forward_part) + meeting[None, :]
    )
    dc_part = matmul(mixed_sum, b_c) + matmul(
        yw_c.reshape(size_q, -1), start_low.reshape(-1, state_width)
    )
    db_part = inner_first(mixed_sum, c_c) + matmul(
        xw_c.reshape(size_q, -1), end_low.reshape(-1, state_width)
    )
    return (dx_local, jnp.concatenate([db_part, dc_part], axis=1), x_gb, da_local)


def group_local(ssm_input, grad_out, b_matrix, c_matrix, dt_step, d_skip, packed):
    within, totals, x_scaled, y_scaled, starts, end_grads, cumulative = packed
    tok_count, head_count = dt_step.shape
    groups = within.shape[0]
    head_dim = ssm_input.shape[1] // head_count
    group_items = (
        ssm_input.reshape(groups, GROUP, head_count, head_dim),
        grad_out.reshape(groups, GROUP, head_count, head_dim),
        b_matrix.reshape(groups, GROUP, -1),
        c_matrix.reshape(groups, GROUP, -1),
        dt_step.reshape(groups, GROUP, head_count),
        within,
        totals,
        starts,
        end_grads,
        x_scaled,
        y_scaled,
    )
    dx_local, dbc_local, x_gb, da_local = lax.map(partial(one_group, d_skip), group_items)
    return (
        dx_local.reshape(tok_count, -1),
        dbc_local.reshape(tok_count, -1),
        x_gb.reshape(tok_count, head_count),
        da_local.reshape(tok_count, head_count),
    )


def device_terms(ssm_input, grad_out, b_matrix, c_matrix, dt_step, cumulative, state_in, grad_in):
    tok_count, head_count = dt_step.shape
    head_dim = ssm_input.shape[1] // head_count
    state_width = b_matrix.shape[1]
    block_end = cumulative[-1]
    state_low = state_in.astype(jnp.bfloat16)
    grad_low = grad_in.astype(jnp.bfloat16)
    rise_factor = jnp.exp(cumulative)
    fall_factor = jnp.exp(block_end[None, :] - cumulative)
    x_three = ssm_input.reshape(tok_count, head_count, head_dim)
    dy_three = grad_out.reshape(tok_count, head_count, head_dim)
    y_dev = contract("hpn,tn->thp", state_low, c_matrix) * rise_factor[:, :, None]
    gb_dev = contract("hpn,tn->thp", grad_low, b_matrix) * fall_factor[:, :, None]
    dx_carry = (dt_step[:, :, None] * gb_dev).astype(jnp.bfloat16).reshape(tok_count, -1)
    x_gb = jnp.sum(x_three.astype(jnp.float32) * gb_dev, axis=2)
    backward_part = jnp.sum(dy_three.astype(jnp.float32) * y_dev, axis=2)
    forward_part = dt_step * x_gb
    meeting = jnp.exp(block_end) * jnp.sum(grad_in * state_in, axis=(1, 2))
    da_dev = reverse_sum(backward_part) + exclusive_sum(forward_part) + meeting[None, :]
    y_rise = (dy_three * rise_factor[:, :, None]).astype(jnp.bfloat16).reshape(tok_count, -1)
    x_fall = (
        (x_three * (dt_step * fall_factor)[:, :, None]).astype(jnp.bfloat16).reshape(tok_count, -1)
    )
    dc_dev = matmul(y_rise, state_low.reshape(-1, state_width))
    db_dev = matmul(x_fall, grad_low.reshape(-1, state_width))
    return (dx_carry, jnp.concatenate([db_dev, dc_dev], axis=1), x_gb, da_dev)


def head_totals(ssm_input, grad_out, dt_step, gate_slope, decay_rate, x_gb, da_all):
    tok_count, head_count = dt_step.shape
    derivative = x_gb + decay_rate[None, :] * da_all
    skip_terms = jnp.sum(
        (ssm_input.astype(jnp.float32) * grad_out.astype(jnp.float32)).reshape(
            tok_count, head_count, -1
        ),
        axis=2,
    )
    return (
        jnp.sum(dt_step * da_all, axis=0),
        jnp.sum(gate_slope * derivative, axis=0),
        jnp.sum(skip_terms, axis=0),
    )


def join_carry(earlier, later):
    return (earlier[0] * later[0], later[0][:, None, None] * earlier[1] + later[1])


def carries(block_decay, block_state, block_grad):
    identity = (jnp.ones_like(block_decay), jnp.zeros_like(block_state))
    state_in = carried_in((block_decay, block_state), SEQ, join_carry, identity, False)[1]
    grad_in = carried_in((block_decay, block_grad), SEQ, join_carry, identity, True)[1]
    return (state_in, grad_in)


def projection_term(layer_in, grads):
    running = inner_first(layer_in, grads[0])
    for extra_grad in grads[1:]:
        running = running + inner_first(layer_in, extra_grad)
    return running


def on_device(layer_in, ssm_input, b_matrix, c_matrix, dt_raw, dt_bias, a_log, d_skip, grad_out):
    dt_step, gate_slope, decay_rate, log_step = head_rates(dt_raw, dt_bias, a_log)
    block_decay, block_state, block_grad, packed = block_states(
        ssm_input, grad_out, b_matrix, c_matrix, dt_step, log_step
    )
    state_in, grad_in = carries(block_decay, block_state, block_grad)
    local_part = group_local(ssm_input, grad_out, b_matrix, c_matrix, dt_step, d_skip, packed)
    carried = device_terms(
        ssm_input, grad_out, b_matrix, c_matrix, dt_step, packed[6], state_in, grad_in
    )
    grad_wx = lax.psum_scatter(
        projection_term(layer_in, (local_part[0], carried[0])), SEQ, scatter_dimension=0, tiled=True
    )
    dbc_all = local_part[1] + carried[1]
    owned_cols = lax.psum_scatter(dbc_all, "mp", scatter_dimension=1, tiled=True).astype(
        jnp.bfloat16
    )
    grad_wbc = sent_and_summed(projection_term(layer_in, (owned_cols,)), SEQ, 0)
    stat_terms = head_totals(
        ssm_input,
        grad_out,
        dt_step,
        gate_slope,
        decay_rate,
        local_part[2] + carried[2],
        local_part[3] + carried[3],
    )
    rate_sum, bias_sum, skip_sum = together((stat_terms[0], stat_terms[1], stat_terms[2]), SEQ)
    return (grad_wx, grad_wbc, decay_rate * rate_sum, bias_sum, skip_sum)


def solution(mesh):
    split = Mesh(mesh.devices.reshape(4, 4, 2, mesh.shape["mp"]), ("seq_0", "seq_1", "seq_2", "mp"))
    in_specs = (
        P(SEQ, None),
        P(SEQ, "mp"),
        P(SEQ, None),
        P(SEQ, None),
        P(SEQ, "mp"),
        P("mp"),
        P("mp"),
        P("mp"),
        P(SEQ, "mp"),
    )
    out_specs = (P(SEQ, "mp"), P(SEQ, "mp"), P("mp"), P("mp"), P("mp"))
    return jax.shard_map(
        on_device, mesh=split, in_specs=in_specs, out_specs=out_specs, check_vma=False
    )
```

profile of v0, /device:TPU:0, one launch (start us, length us, event | category | flops | bytes accessed | tf_op | source)
XLA Modules:
  0.0 422.1 jit_solution(3671476360436188882)
XLA Ops:
  9.0 1.7 reduce-window.52
  12.1 4.0 copy.151
  16.1 2.7 copy.144
  20.1 2.9 reshape.366
  23.0 5.2 %reshape.372 = bf16[3,256,20,64]{1,0,3,2:T(4,128)(2,1)S(1)} reshape(bf16[768,1280]{0,1:T(8,128)(2,1)} %copy.151) | data formatting | bytes 3932160 | tf_op jit(solution)/shard_map/reshape | solution.py:183
  28.3 4.4 %multiply_convert_fusion.6 = (bf16[3,256,20,64]{1,0,3,2:T(4,128)(2,1)S(1)}, bf16[3,256,20,64]{1,0,3,2:T(4,128)(2,1)S(1)}) fusion(bf16[3,256,20,64]{1,0,3,2:T(4,128)(2,1)S(1)} %reshape.372, f32[3,256,20]{1,0,2:T(4,128)S(1)} %get-tuple-element.291, f32[3,256,20]{1,0,2:T(4,128)S(1)} %get-tuple-element.292, bf16[3,256,20,64]{1,0,3,2:T(4,128)(2,1)} %reshape.366), kind=kLoop, calls=%fused_computation.103 | loop fusion | flops 5898240 | bytes 7987200 | tf_op jit(solution)/shard_map/convert_element_type | solution.py:101
  36.1 2.2 slice_add_fusion
  39.8 3.3 reduce-window.56
  43.6 1.8 all-gather
  45.4 11.1 %all-gather.1 = f32[4,1,20]{2,1,0:T(1,128)S(1)} all-gather(f32[1,1,20]{2,1,0:T(1,128)S(1)} %get-tuple-element.316), channel_id=1, replica_groups=mesh['seq_0'=4,'seq_1'=4,'seq_2'=2,'mp'=4] {'seq_1'}, dimensions={0}, use_global_device_ids=true | all-gather | bytes 400 | tf_op jit(solution)/shard_map/all_gather | solution.py:24
  57.1 2.3 multiply_add_fusion.7
  59.5 8.8 %all-gather.17.cloned.1.call-done = f32[2,20,64,128]{3,2,1,0:T(8,128)} async-done(((f32[1,20,64,128]{3,2,1,0:T(8,128)}), f32[2,20,64,128]{3,2,1,0:T(8,128)}) %all-gather.17.cloned.1.call-update) | async-done | bytes 1310736 | tf_op jit(solution)/shard_map/all_gather | solution.py:24
  68.2 2.3 multiply_add_fusion.3
  70.7 36.0 %all-gather.13.cloned.1.call-done = f32[4,20,64,128]{3,2,1,0:T(8,128)} async-done(((f32[1,20,64,128]{3,2,1,0:T(8,128)}), f32[4,20,64,128]{3,2,1,0:T(8,128)}) %all-gather.13.cloned.1.call-update) | async-done | bytes 2621456 | tf_op jit(solution)/shard_map/all_gather | solution.py:24
  106.6 36.8 %all-gather.19.cloned.1.call-done = f32[4,20,64,128]{3,2,1,0:T(8,128)} async-done(((f32[1,20,64,128]{3,2,1,0:T(8,128)}), f32[4,20,64,128]{3,2,1,0:T(8,128)}) %all-gather.19.cloned.1.call-update) | async-done | bytes 2621456 | tf_op jit(solution)/shard_map/all_gather | solution.py:24
  143.5 4.0 multiply_add_fusion.4
  147.6 3.5 copy.155
  151.1 1.7 copy.157
  153.4 1.8 pad_maximum_fusion.1
  155.5 75.9 %while.16 = (s32[]{:T(128)}, bf16[3,256,20,64]{1,3,2,0:T(8,128)(2,1)}, f32[3,256,256]{2,1,0:T(8,128)}, f32[3,256,20]{1,0,2:T(4,128)}, f32[3,256,20]{1,0,2:T(4,12...) while((s32[]{:T(128)}, ...), condition=%wide.region_16.17_spmd, body=%wide.region_2.16_spmd.sunk | while | flops 748835008 | bytes 29963108 | solution.py:195
  157.1 1.7 fusion.178
  163.5 4.9 %fusion.175 = (f32[20,256]{1,0:T(8,128)}, f32[20,256]{1,0:T(8,128)}, bf16[256,256]{1,0:T(8,128)(2,1)S(1)}) fusion(f32[256,256]{1,0:T(8,128)S(1)} %fusion.173, pred[256,256]{1,0:T(8,128)(4,1)S(1)} %get-tuple-element.456, f32[20,256]{1,0:T(8,128)S(1)} %bitcast.599, f32[20,256]{1,0:T(8,128)S(1)} %bitcast.601, ...), kind=kOutput, calls=%fused_computation.4.clone.1 | convolution fusion | flops 180803584 | bytes 1950720 | tf_op jit(solution)/shard_map/while/body/eval_jaxpr/rhp,shp->hrs/dot_general | solution.py:56
  171.6 3.3 fusion.174
  182.4 1.7 fusion.178
  188.7 4.9 %fusion.175 = (f32[20,256]{1,0:T(8,128)}, f32[20,256]{1,0:T(8,128)}, bf16[256,256]{1,0:T(8,128)(2,1)S(1)}) fusion(f32[256,256]{1,0:T(8,128)S(1)} %fusion.173, pred[256,256]{1,0:T(8,128)(4,1)S(1)} %get-tuple-element.456, f32[20,256]{1,0:T(8,128)S(1)} %bitcast.599, f32[20,256]{1,0:T(8,128)S(1)} %bitcast.601, ...), kind=kOutput, calls=%fused_computation.4.clone.1 | convolution fusion | flops 180803584 | bytes 1950720 | tf_op jit(solution)/shard_map/while/body/eval_jaxpr/rhp,shp->hrs/dot_general | solution.py:56
  196.9 3.3 fusion.174
  202.9 1.6 dynamic_update_slice.24
  207.7 1.7 fusion.178
  214.0 4.9 %fusion.175 = (f32[20,256]{1,0:T(8,128)}, f32[20,256]{1,0:T(8,128)}, bf16[256,256]{1,0:T(8,128)(2,1)S(1)}) fusion(f32[256,256]{1,0:T(8,128)S(1)} %fusion.173, pred[256,256]{1,0:T(8,128)(4,1)S(1)} %get-tuple-element.456, f32[20,256]{1,0:T(8,128)S(1)} %bitcast.599, f32[20,256]{1,0:T(8,128)S(1)} %bitcast.601, ...), kind=kOutput, calls=%fused_computation.4.clone.1 | convolution fusion | flops 180803584 | bytes 1950720 | tf_op jit(solution)/shard_map/while/body/eval_jaxpr/rhp,shp->hrs/dot_general | solution.py:56
  222.1 3.3 fusion.174
  231.4 2.3 copy.166
  233.7 3.3 copy.160
  237.5 9.8 %all-gather.2 = f32[4,1,20]{2,1,0:T(1,128)S(1)} all-gather(f32[1,1,20]{2,1,0:T(1,128)S(1)} %get-tuple-element.298), channel_id=1, replica_groups=mesh['seq_0'=4,'seq_1'=4,'seq_2'=2,'mp'=4] {'seq_0'}, dimensions={0}, use_global_device_ids=true | all-gather | bytes 400 | tf_op jit(solution)/shard_map/all_gather | solution.py:24
  247.3 7.2 %all-gather.3 = f32[4,1,20]{2,1,0:T(1,128)S(1)} all-gather(f32[1,1,20]{2,1,0:T(1,128)S(1)} %get-tuple-element.299), channel_id=1, replica_groups=mesh['seq_0'=4,'seq_1'=4,'seq_2'=2,'mp'=4] {'seq_0'}, dimensions={0}, use_global_device_ids=true | all-gather | bytes 400 | tf_op jit(solution)/shard_map/all_gather | solution.py:24
  254.7 8.5 %fusion.118 = f32[1280,2560]{1,0:T(8,128)} fusion(bf16[768,1280]{0,1:T(8,128)(2,1)S(1)} %bitcast.592, bf16[768,2560]{1,0:T(8,128)(2,1)S(1)} %copy-done.7), kind=kOutput, calls=%fused_computation.269 | convolution fusion | flops 5033164800 | bytes 19005440 | tf_op jit(solution)/shard_map/dot_general | solution.py:64
  263.3 6.9 %multiply_reduce_fusion.3 = (f32[20]{0:T(128)S(1)}, bf16[20,64,128]{2,1,0:T(8,128)(2,1)}, bf16[20,64,128]{2,1,0:T(8,128)(2,1)}) fusion(pred[]{:T(512)S(6)} %gt.48, f32[2,20,64,128]{3,2,1,0:T(8,128)} %all-gather.17.cloned.1.call-done, f32[20]{0:T(128)S(1)} %copy-done.42, f32[20]{0:T(128)S(1)} %copy-done.46, pred[]{:T(512)S(6)} %gt.47, pred[]{:T(512)S(6)} %gt.46, ...), kind=kLoop, calls=%fused_computation.162 | loop fusion | flops 10813420 | bytes 13764420 | tf_op jit(solution)/shard_map/reduce_sum | solution.py:221
  270.6 2.7 multiply_reduce_fusion.1
  273.3 3.6 convolution_bitcast_fusion.3
  276.9 3.5 convolution_bitcast_fusion.4
  281.8 2.7 multiply_reduce_fusion.2
  284.5 11.4 %fusion.68 = f32[2560,1280]{0,1:T(8,128)} fusion(f32[1280,2560]{1,0:T(8,128)} %fusion.118, bf16[768,1280]{0,1:T(8,128)(2,1)S(1)} %bitcast.626, bf16[768,2560]{1,0:T(8,128)(2,1)S(1)} %copy-done.8), kind=kOutput, calls=%fused_computation.102 | convolution fusion | flops 5036441600 | bytes 32112640 | tf_op jit(solution)/shard_map/dot_general | solution.py:64
  295.9 14.0 %copy.182 = f32[2560,1280]{1,0:T(8,128)} copy(f32[2560,1280]{0,1:T(8,128)} %fusion.68) | data formatting | bytes 26214400
  312.3 1.7 reduce-window.60
  314.9 1.7 reduce-window.62
  316.8 3.2 convolution_bitcast_fusion.2
  322.2 5.2 %all-to-all-start = ((f32[32,80,64]{1,2,0:T(8,128)}), f32[32,80,64]{1,2,0:T(8,128)S(1)}, u32[]{:S(2)}, u32[]{:S(2)}) async-start(f32[32,80,64]{1,2,0:T(8,128)} %copy.167), calls=%async_computation.1 | async-start | bytes 2097152 | tf_op jit(solution)/shard_map/all_to_all | solution.py:42
  328.1 72.0 %psum.7 = f32[60]{0:T(128)S(1)} all-reduce(f32[60]{0:T(128)S(1)} %pad_maximum_fusion.2), channel_id=1, replica_groups=mesh['seq_0'=4,'seq_1'=4,'seq_2'=2,'mp'=4] {'seq_0','seq_1','seq_2'}, use_global_device_ids=true, to_apply=%region_33.34 | all-reduce | flops 60 | bytes 480 | tf_op jit(solution)/shard_map/psum | solution.py:48
  401.4 13.9 %reduce-scatter.7.cloned.1.call-done = f32[80,1280]{1,0:T(8,128)} async-done(((f32[2560,1280]{1,0:T(8,128)}), f32[80,1280]{1,0:T(8,128)}) %reduce-scatter.7.cloned.1.call-update) | async-done | bytes 409616
  (424 shorter events, 64.8 us)
Async XLA Ops:
  7.2 49.9 %all-gather.11.cloned.1.call-start = ((), (), s32[]{:S(2)}) async-start(), calls=%async_computation.3 | async-start | bytes 1966080 | tf_op jit(solution)/shard_map/all_gather | solution.py:24
  38.3 29.9 %all-gather.17.cloned.1.call-start = ((), (), s32[]{:S(2)}) async-start(), calls=%async_computation.6 | async-start | bytes 1966080 | tf_op jit(solution)/shard_map/all_gather | solution.py:24
  39.1 67.5 %all-gather.13.cloned.1.call-start = ((), (), s32[]{:S(2)}) async-start(), calls=%async_computation.4 | async-start | bytes 3276800 | tf_op jit(solution)/shard_map/all_gather | solution.py:24
  43.4 27.1 %copy-start.26 = (f32[3,8,6,128]{3,1,2,0:T(8,128)}, f32[3,8,6,128]{3,1,2,0:T(8,128)S(1)}, u32[]{:S(2)}) copy-start(f32[3,8,6,128]{3,1,2,0:T(8,128)S(1)} %copy.212) | copy-start | bytes 221188
  45.4 25.1 %copy-start.33 = (f32[2,1,20]{2,1,0:T(1,128)}, f32[2,1,20]{2,1,0:T(1,128)S(1)}, u32[]{:S(2)}) copy-start(f32[2,1,20]{2,1,0:T(1,128)S(1)} %all-gather) | copy-start | bytes 484
  45.4 25.1 %copy-start.43 = (f32[20]{0:T(128)}, f32[20]{0:T(128)S(1)}, u32[]{:S(2)}) copy-start(f32[20]{0:T(128)S(1)} %get-tuple-element.314) | copy-start | bytes 244
  45.4 25.1 %copy-start.45 = (f32[20]{0:T(128)}, f32[20]{0:T(128)S(1)}, u32[]{:S(2)}) copy-start(f32[20]{0:T(128)S(1)} %get-tuple-element.315) | copy-start | bytes 244
  57.1 13.5 %copy-start.37 = (f32[20]{0:T(128)}, f32[20]{0:T(128)S(1)}, u32[]{:S(2)}) copy-start(f32[20]{0:T(128)S(1)} %get-tuple-element.313) | copy-start | bytes 244
  57.1 13.5 %copy-start.41 = (f32[20]{0:T(128)}, f32[20]{0:T(128)S(1)}, u32[]{:S(2)}) copy-start(f32[20]{0:T(128)S(1)} %get-tuple-element.312) | copy-start | bytes 244
  57.1 86.4 %copy-start.35 = (f32[20]{0:T(128)}, f32[20]{0:T(128)S(1)}, u32[]{:S(2)}) copy-start(f32[20]{0:T(128)S(1)} %get-tuple-element.301) | copy-start | bytes 244
  57.1 86.4 %copy-start.39 = (f32[20]{0:T(128)}, f32[20]{0:T(128)S(1)}, u32[]{:S(2)}) copy-start(f32[20]{0:T(128)S(1)} %get-tuple-element.300) | copy-start | bytes 244
  59.4 84.1 %all-gather.19.cloned.1.call-start = ((), (), s32[]{:S(2)}) async-start(), calls=%async_computation.7 | async-start | bytes 3276800 | tf_op jit(solution)/shard_map/all_gather | solution.py:24
  70.6 192.6 %all-gather.15.cloned.1.call-start = ((), (), s32[]{:S(2)}) async-start(), calls=%async_computation.5 | async-start | bytes 3276800 | tf_op jit(solution)/shard_map/all_gather | solution.py:24
  70.6 76.8 %copy-start.47 = (f32[20]{0:T(128)}, f32[20]{0:T(128)S(1)}, u32[]{:S(2)}) copy-start(f32[20]{0:T(128)S(1)} %get-tuple-element.303) | copy-start | bytes 244
  70.6 76.8 %copy-start.49 = (f32[20]{0:T(128)}, f32[20]{0:T(128)S(1)}, u32[]{:S(2)}) copy-start(f32[20]{0:T(128)S(1)} %get-tuple-element.304) | copy-start | bytes 244
  70.6 76.8 %copy-start.51 = (f32[20]{0:T(128)}, f32[20]{0:T(128)S(1)}, u32[]{:S(2)}) copy-start(f32[20]{0:T(128)S(1)} %get-tuple-element.302) | copy-start | bytes 244
  70.7 76.8 %copy-start.53 = (f32[20]{0:T(128)}, f32[20]{0:T(128)S(1)}, u32[]{:S(2)}) copy-start(f32[20]{0:T(128)S(1)} %get-tuple-element.305) | copy-start | bytes 244
  147.5 115.6 %all-gather.21.cloned.1.call-start = ((), (), s32[]{:S(2)}) async-start(), calls=%async_computation.8 | async-start | bytes 3276800 | tf_op jit(solution)/shard_map/all_gather | solution.py:24
  155.3 161.5 %reduce-scatter.5.cloned.1.call-start = ((), (), s32[]{:S(2)}) async-start(), calls=%async_computation.9 | async-start | bytes 983040 | tf_op jit(solution)/shard_map/reduce_scatter | solution.py:280
  155.5 6.2 %copy-start.20 = (f32[3,256,20]{1,0,2:T(4,128)}, f32[3,256,20]{1,0,2:T(4,128)S(1)}, u32[]{:S(2)}) copy-start(f32[3,256,20]{1,0,2:T(4,128)S(1)} %get-tuple-element.510) | copy-start | bytes 184324 | tf_op jit(solution)/shard_map/while
  157.0 6.4 %copy-start.22 = (f32[1,256,20]{1,2,0:T(8,128)}, f32[1,256,20]{1,2,0:T(8,128)S(1)}, u32[]{:S(2)}) copy-start(f32[1,256,20]{1,2,0:T(8,128)S(1)} %copy.255) | copy-start | bytes 61444 | tf_op jit(solution)/shard_map/while
  157.0 6.4 %copy-start.23 = (f32[1,256,20]{1,2,0:T(8,128)}, f32[1,256,20]{1,2,0:T(8,128)S(1)}, u32[]{:S(2)}) copy-start(f32[1,256,20]{1,2,0:T(8,128)S(1)} %copy.256) | copy-start | bytes 61444 | tf_op jit(solution)/shard_map/while
  182.3 6.4 %copy-start.22 = (f32[1,256,20]{1,2,0:T(8,128)}, f32[1,256,20]{1,2,0:T(8,128)S(1)}, u32[]{:S(2)}) copy-start(f32[1,256,20]{1,2,0:T(8,128)S(1)} %copy.255) | copy-start | bytes 61444 | tf_op jit(solution)/shard_map/while
  182.3 6.3 %copy-start.23 = (f32[1,256,20]{1,2,0:T(8,128)}, f32[1,256,20]{1,2,0:T(8,128)S(1)}, u32[]{:S(2)}) copy-start(f32[1,256,20]{1,2,0:T(8,128)S(1)} %copy.256) | copy-start | bytes 61444 | tf_op jit(solution)/shard_map/while
  207.6 6.4 %copy-start.22 = (f32[1,256,20]{1,2,0:T(8,128)}, f32[1,256,20]{1,2,0:T(8,128)S(1)}, u32[]{:S(2)}) copy-start(f32[1,256,20]{1,2,0:T(8,128)S(1)} %copy.255) | copy-start | bytes 61444 | tf_op jit(solution)/shard_map/while
  207.6 6.4 %copy-start.23 = (f32[1,256,20]{1,2,0:T(8,128)}, f32[1,256,20]{1,2,0:T(8,128)S(1)}, u32[]{:S(2)}) copy-start(f32[1,256,20]{1,2,0:T(8,128)S(1)} %copy.256) | copy-start | bytes 61444 | tf_op jit(solution)/shard_map/while
  236.9 17.6 %copy-start.34 = (f32[2,1,20]{2,1,0:T(1,128)S(1)}, f32[2,1,20]{2,1,0:T(1,128)}, u32[]{:S(2)}) copy-start(f32[2,1,20]{2,1,0:T(1,128)} %copy-done.33) | copy-start | bytes 484
  237.0 17.6 %copy-start.7 = (bf16[768,2560]{1,0:T(8,128)(2,1)S(1)}, bf16[768,2560]{1,0:T(8,128)(2,1)}, u32[]{:S(2)}) copy-start(bf16[768,2560]{1,0:T(8,128)(2,1)} %param.11) | copy-start | bytes 11796484
  254.6 8.6 %copy-start.36 = (f32[20]{0:T(128)S(1)}, f32[20]{0:T(128)}, u32[]{:S(2)}) copy-start(f32[20]{0:T(128)} %copy-done.35) | copy-start | bytes 244
  254.6 8.6 %copy-start.38 = (f32[20]{0:T(128)S(1)}, f32[20]{0:T(128)}, u32[]{:S(2)}) copy-start(f32[20]{0:T(128)} %copy-done.37) | copy-start | bytes 244
  254.6 8.6 %copy-start.40 = (f32[20]{0:T(128)S(1)}, f32[20]{0:T(128)}, u32[]{:S(2)}) copy-start(f32[20]{0:T(128)} %copy-done.39) | copy-start | bytes 244
  254.6 8.6 %copy-start.42 = (f32[20]{0:T(128)S(1)}, f32[20]{0:T(128)}, u32[]{:S(2)}) copy-start(f32[20]{0:T(128)} %copy-done.41) | copy-start | bytes 244
  254.6 8.6 %copy-start.44 = (f32[20]{0:T(128)S(1)}, f32[20]{0:T(128)}, u32[]{:S(2)}) copy-start(f32[20]{0:T(128)} %copy-done.43) | copy-start | bytes 244
  254.6 8.6 %copy-start.46 = (f32[20]{0:T(128)S(1)}, f32[20]{0:T(128)}, u32[]{:S(2)}) copy-start(f32[20]{0:T(128)} %copy-done.45) | copy-start | bytes 244
  254.6 8.6 %copy-start.48 = (f32[20]{0:T(128)S(1)}, f32[20]{0:T(128)}, u32[]{:S(2)}) copy-start(f32[20]{0:T(128)} %copy-done.47) | copy-start | bytes 244
  254.6 8.6 %copy-start.50 = (f32[20]{0:T(128)S(1)}, f32[20]{0:T(128)}, u32[]{:S(2)}) copy-start(f32[20]{0:T(128)} %copy-done.49) | copy-start | bytes 244
  254.6 8.6 %copy-start.52 = (f32[20]{0:T(128)S(1)}, f32[20]{0:T(128)}, u32[]{:S(2)}) copy-start(f32[20]{0:T(128)} %copy-done.51) | copy-start | bytes 244
  254.6 8.6 %copy-start.54 = (f32[20]{0:T(128)S(1)}, f32[20]{0:T(128)}, u32[]{:S(2)}) copy-start(f32[20]{0:T(128)} %copy-done.53) | copy-start | bytes 244
  254.7 8.6 %copy-start.58 = (f32[20]{0:T(128)S(1)}, f32[20]{0:T(128)}, u32[]{:S(2)}) copy-start(f32[20]{0:T(128)} %get-tuple-element.265) | copy-start | bytes 244
  254.7 8.6 %copy-start.59 = (f32[20]{0:T(128)S(1)}, f32[20]{0:T(128)}, u32[]{:S(2)}) copy-start(f32[20]{0:T(128)} %get-tuple-element.266) | copy-start | bytes 244
  263.3 7.0 %copy-start.27 = (f32[3,8,6,128]{3,1,2,0:T(8,128)S(1)}, f32[3,8,6,128]{3,1,2,0:T(8,128)}, u32[]{:S(2)}) copy-start(f32[3,8,6,128]{3,1,2,0:T(8,128)} %copy-done.26) | copy-start | bytes 221188
  263.3 7.3 %copy-start.3 = (bf16[768,1280]{0,1:T(8,128)(2,1)S(1)}, bf16[768,1280]{0,1:T(8,128)(2,1)}, u32[]{:S(2)}) copy-start(bf16[768,1280]{0,1:T(8,128)(2,1)} %copy-done.2) | copy-start | bytes 5898244
  281.5 133.8 %reduce-scatter.7.cloned.1.call-start = ((), (), s32[]{:S(2)}) async-start(), calls=%async_computation.10 | async-start | bytes 13516800
  320.6 7.2 %copy-start.30 = (f32[768,20]{0,1:T(8,128)S(1)}, f32[768,20]{0,1:T(8,128)}, u32[]{:S(2)}) copy-start(f32[768,20]{0,1:T(8,128)} %param.15) | copy-start | bytes 184324
  320.6 7.2 %copy-start.55 = (f32[20]{0:T(128)S(1)}, f32[20]{0:T(128)}, u32[]{:S(2)}) copy-start(f32[20]{0:T(128)} %param.16) | copy-start | bytes 244
  320.6 7.2 %copy-start.57 = (f32[20]{0:T(128)S(1)}, f32[20]{0:T(128)}, u32[]{:S(2)}) copy-start(f32[20]{0:T(128)} %copy-done.56) | copy-start | bytes 244
  322.2 77.9 %copy-start.60 = (f32[20]{0:T(128)S(1)}, f32[20]{0:T(128)}, u32[]{:S(2)}) copy-start(f32[20]{0:T(128)} %param.17) | copy-start | bytes 244
  322.2 78.5 %all-to-all-start = ((f32[32,80,64]{1,2,0:T(8,128)}), f32[32,80,64]{1,2,0:T(8,128)S(1)}, u32[]{:S(2)}, u32[]{:S(2)}) async-start(f32[32,80,64]{1,2,0:T(8,128)} %copy.167), calls=%async_computation.1 | async-start | bytes 2097152 | tf_op jit(solution)/shard_map/all_to_all | solution.py:42
  (39 other events, 92.0 us)
Sparse Core Ops, SparseCore 0:
  38.4 14.5 all-gather.10
  54.7 13.4 all-gather.16
  69.9 36.7 all-gather.12
  108.1 35.2 all-gather.18
  147.6 35.0 all-gather.14
  184.2 35.2 all-gather.20
  281.6 21.6 reduce-scatter.4
  310.1 105.1 reduce-scatter.6
where the time goes:
time: 425 us; the launch traced here: 422 us
  blocking collectives  102 us (24%)
  waiting for transfers between devices  96.3 us (23%)
  matrix products  76.6 us (18%)
  local copies, waits for them, and re-layouts  68.5 us (16%)
  other arithmetic  56.7 us (13%)
  between operations  15.2 us (4%)
  starting transfers between devices  6.01 us (1%)
    all_gather x6, waiting for transfers between devices, carried_in(): pieces = jax.tree.map(lambda part: lax.all_gather(part, axis), subtotal)  81.6 us
    psum x1, blocking collectives, together(): subtotal = lax.psum(flat, axis)  72 us
    dot_general x16, matrix products, contract(): return jnp.einsum(form, left, right, preferred_element_type=jnp.float32)  35.5 us
    all_gather x4, blocking collectives, carried_in(): pieces = jax.tree.map(lambda part: lax.all_gather(part, axis), subtotal)  29.9 us
    unnamed x122, local copies, waits for them, and re-layouts  25.6 us
    dot_general x6, matrix products, inner_first(): lax.dot_general(left, right, (((0,), (0,)), ((), ())), preferred_element_...  23.7 us
    dot_general x11, matrix products, matmul(): return jnp.dot(left, right, preferred_element_type=jnp.float32)  16.8 us
    another operation x44, other arithmetic  15.3 us
  transfers between devices with their start and end apart: 9, of which 4 were waited for; matrix products, arithmetic and copies ran while one was open for 34% of the time, Pallas kernels for 0%

commit v1 on v0

v1 whole, which is shorter than its diff:
```python
import functools
import math

import jax
import jax.numpy as jnp
from jax import lax
from jax.experimental import pallas as pl
from jax.experimental.pallas import tpu as pltpu
from jax.sharding import Mesh
from jax.sharding import PartitionSpec as P

GROUP = 256
HEAD_DIM = 64
STATE = 128
LOG2E = 1.0 / math.log(2.0)
SEQ = ("seq_0", "seq_1", "seq_2")
F32 = jnp.float32
BF16 = jnp.bfloat16
VMEM = pltpu.VMEM


def dot(left, right):
    return jnp.dot(left, right, preferred_element_type=F32)


def dot_nt(left, right):
    return lax.dot_general(left, right, (((1,), (1,)), ((), ())), preferred_element_type=F32)


def dot_tn(left, right):
    return lax.dot_general(left, right, (((0,), (0,)), ((), ())), preferred_element_type=F32)


def dot_exact(left, right):
    return jnp.dot(left, right, preferred_element_type=F32, precision=lax.Precision.HIGHEST)


def lane_iota(shape, dim):
    return lax.broadcasted_iota(jnp.int32, shape, dim)


def spread_matrix(heads, dtype):
    rows = lane_iota((heads, heads * HEAD_DIM), 0)
    cols = lane_iota((heads, heads * HEAD_DIM), 1)
    inside = (cols >= rows * HEAD_DIM) & (cols < (rows + 1) * HEAD_DIM)
    return jnp.where(inside, 1.0, 0.0).astype(dtype)


def gather_matrix(heads, dtype):
    rows = lane_iota((heads * HEAD_DIM, heads), 0)
    cols = lane_iota((heads * HEAD_DIM, heads), 1)
    inside = (rows >= cols * HEAD_DIM) & (rows < (cols + 1) * HEAD_DIM)
    return jnp.where(inside, 1.0, 0.0).astype(dtype)


def lower_ones(size):
    return jnp.where(lane_iota((size, size), 0) >= lane_iota((size, size), 1), 1.0, 0.0)


def spread(values, matrix):
    high = values.astype(BF16)
    low = (values - high.astype(F32)).astype(BF16)
    return dot(high, matrix) + dot(low, matrix)


def states_kernel(x_ref, dy_ref, b_ref, c_ref, dt_ref, a_ref, parts_ref, ends_ref, total_s, total_g):
    groups = x_ref.shape[0] // GROUP
    heads = dt_ref.shape[1]
    width = heads * HEAD_DIM
    tri = lower_ones(GROUP)
    spread_m = spread_matrix(heads, BF16)
    spread_e = spread_matrix(heads, F32)
    decays = []
    block_end = jnp.zeros((1, heads), F32)
    for g in range(groups):
        rows = slice(g * GROUP, (g + 1) * GROUP)
        within = dot_exact(tri, a_ref[rows, :])
        last = within[GROUP - 1 : GROUP, :]
        block_end = block_end + last
        decays.append(dot_exact(jnp.broadcast_to(jnp.exp(last), (8, heads)), spread_e)[0:1, :])
        fall = spread(dt_ref[rows, :] * jnp.exp(last - within), spread_m)
        xw = (x_ref[rows, :].astype(F32) * fall).astype(BF16)
        state = dot_tn(b_ref[rows, :], xw)
        rise = spread(jnp.exp(within), spread_m)
        yw = (dy_ref[rows, :].astype(F32) * rise).astype(BF16)
        grad = dot_tn(c_ref[rows, :], yw)
        if g < groups - 1:
            parts_ref[g] = state
        if g > 0:
            parts_ref[groups - 2 + g] = grad
        if g == 0:
            total_s[...] = state
            total_g[...] = grad
            gain = decays[0]
        else:
            total_s[...] = decays[g] * total_s[...] + state
            total_g[...] = total_g[...] + gain * grad
            gain = gain * decays[g]
    ends_ref[0:STATE, 0:width] = total_s[...]
    ends_ref[STATE : 2 * STATE, 0:width] = total_g[...]
    pad = jnp.concatenate([jnp.exp(block_end), jnp.zeros((1, 128 - heads), F32)], axis=1)
    ends_ref[:, width : width + 128] = jnp.broadcast_to(pad, (2 * STATE, 128))


def scan_kernel(half_ref, in_ref, out_ref, gain_ref):
    devices, rows, full = in_ref.shape
    width = full - 128
    heads = width // HEAD_DIM
    gains = in_ref[:, 0, width : width + 128][:, 0:heads]
    gain_ref[...] = dot_exact(gains, spread_matrix(heads, F32))
    backward = half_ref[0]

    def step(i, running):
        b = jnp.where(backward == 1, devices - 1 - i, i)
        out_ref[b] = running
        return gain_ref[pl.ds(b, 1), :] * running + in_ref[b, :, 0:width]

    lax.fori_loop(0, devices, step, jnp.zeros((rows, width), F32))


def intra_kernel(x_ref, dy_ref, b_ref, c_ref, dt_ref, slope_ref, a_ref, gi_ref, dbc_ref, stat_ref, v_ref, mix_ref):
    heads = dt_ref.shape[1]
    half = GROUP // 2
    tri = lower_ones(GROUP)
    dt = dt_ref[...]
    within = dot_exact(tri, a_ref[...])
    sums = dot_exact(tri, jnp.concatenate([dt, slope_ref[...]], axis=1))
    rise2 = within * LOG2E
    start2 = rise2 - jnp.log2(dt)
    rise_rows = jnp.transpose(rise2)
    sum_rows = jnp.transpose(sums)
    cross = dot_nt(b_ref[...], c_ref[...])
    v_ref[...] = jnp.zeros_like(v_ref)
    mix_ref[:, half:GROUP, 0:half] = jnp.zeros((2, half, half), BF16)
    strip = 64
    for pair in range(heads // 2):
        lanes = slice(pair * 128, (pair + 1) * 128)
        halves = []
        zs = []
        for sub in range(2):
            h = 2 * pair + sub
            cols = slice(h * HEAD_DIM, (h + 1) * HEAD_DIM)
            x_h = x_ref[:, cols]
            dy_h = dy_ref[:, cols]
            top = dot_nt(x_h[0:half], dy_h)
            low = dot_nt(x_h[half:GROUP], dy_h[half:GROUP])
            acc = [jnp.zeros((8, GROUP), F32) for _ in range(3)]
            z_strips = []
            for k in range(GROUP // strip):
                first = (k * strip // half) * half
                rows = slice(k * strip, (k + 1) * strip)
                wide = GROUP - first
                gap = rise_rows[h : h + 1, first:GROUP] - start2[rows, h : h + 1]
                reach = lane_iota((strip, wide), 1) + first >= lane_iota((strip, wide), 0) + k * strip
                decay = jnp.where(reach, jnp.exp2(gap), 0.0)
                bc = cross[rows, first:GROUP]
                mix_ref[sub, rows, first:GROUP] = (decay * bc).astype(BF16)
                pairs = top[rows, :] if first == 0 else low[k * strip - half : (k + 1) * strip - half, :]
                z = decay * pairs
                z_strips.append(z)
                box = z * bc
                w_dt = sums[rows, h : h + 1]
                w_sl = sums[rows, heads + h : heads + h + 1]
                for n, term in enumerate((box, box * w_dt, box * w_sl)):
                    part = jnp.sum(term.reshape(strip // 8, 8, wide), axis=0)
                    if first > 0:
                        acc[n] = jnp.concatenate([acc[n][:, 0:first], acc[n][:, first:GROUP] + part], axis=1)
                    else:
                        acc[n] = acc[n] + part
            zs.append(z_strips)
            halves.append(dot(mix_ref[sub], dy_h))
            flow_dt = acc[0] * sum_rows[h : h + 1, :] - acc[1]
            flow_sl = acc[0] * sum_rows[heads + h : heads + h + 1, :] - acc[2]
            stat_ref[0, h : h + 1, :] = jnp.sum(flow_dt, axis=0, keepdims=True)
            stat_ref[0, heads + h : heads + h + 1, :] = jnp.sum(flow_sl, axis=0, keepdims=True)
        for k in range(GROUP // strip):
            first = (k * strip // half) * half
            rows = slice(k * strip, (k + 1) * strip)
            v_ref[rows, first:GROUP] += zs[0][k] + zs[1][k]
        gi_ref[:, lanes] = jnp.concatenate(halves, axis=1).astype(BF16)
    mixed = v_ref[...].astype(BF16)
    dbc_ref[:, 0:STATE] = dot(mixed, c_ref[...])
    dbc_ref[:, STATE : 2 * STATE] = dot_tn(mixed, b_ref[...])


def final_kernel(x_ref, dy_ref, b_ref, c_ref, dt_ref, slope_ref, a_ref, skip_ref, rate_ref, gi_ref, dbc_ref,
                 flow_ref, parts_ref, carry_ref, dx_ref, dbc_out, stat_ref, sp_ref, gp_ref):
    heads = dt_ref.shape[1]
    groups = x_ref.shape[0] // GROUP
    tri = lower_ones(GROUP)
    spread_m = spread_matrix(heads, BF16)
    spread_e = spread_matrix(heads, F32)
    gather_m = gather_matrix(heads, BF16)
    gather_e = gather_matrix(heads, F32)
    rate = rate_ref[...]
    within, last, decays = [], [], []
    for g in range(groups):
        rows = slice(g * GROUP, (g + 1) * GROUP)
        within.append(dot_exact(tri, a_ref[rows, :]))
        last.append(within[g][GROUP - 1 : GROUP, :])
        decays.append(dot_exact(jnp.broadcast_to(jnp.exp(last[g]), (8, heads)), spread_e)[0:1, :])
    sp_ref[0] = carry_ref[0:STATE, :]
    gp_ref[groups - 1] = carry_ref[STATE : 2 * STATE, :]
    for g in range(groups - 1):
        sp_ref[g + 1] = decays[g] * sp_ref[g] + parts_ref[g]
    for g in range(groups - 1, 0, -1):
        gp_ref[g - 1] = parts_ref[groups - 2 + g] + decays[g] * gp_ref[g]
    flow_dt_all = jnp.zeros((1, heads), F32)
    flow_sl_all = jnp.zeros((1, heads), F32)
    bias_all = jnp.zeros((1, heads), F32)
    skip_all = jnp.zeros((1, heads), F32)
    for g in range(groups):
        rows = slice(g * GROUP, (g + 1) * GROUP)
        dt = dt_ref[rows, :]
        slope = slope_ref[rows, :]
        rise = jnp.exp(within[g])
        fall = dt * jnp.exp(last[g] - within[g])
        x = x_ref[rows, :].astype(F32)
        dy = dy_ref[rows, :].astype(F32)
        b = b_ref[rows, :]
        c = c_ref[rows, :]
        sp = sp_ref[g]
        gp = gp_ref[g]
        sp_low = sp.astype(BF16)
        gp_low = gp.astype(BF16)
        fall_wide = spread(fall, spread_m)
        xw = (x * fall_wide).astype(BF16)
        from_end = dot(b, gp_low)
        dx_raw = gi_ref[rows, :].astype(F32) + fall_wide * from_end
        dx_ref[rows, :] = (dx_raw + skip_ref[...] * dy).astype(BF16)
        x_gb = dot((x * dx_raw).astype(BF16), gather_m)
        fore = fall * dot((x * from_end).astype(BF16), gather_m)
        skips = dot((x * dy).astype(BF16), gather_m)
        rise_wide = spread(rise, spread_m)
        yw = (dy * rise_wide).astype(BF16)
        from_start = dot(c, sp_low)
        back = rise * dot((dy * from_start).astype(BF16), gather_m)
        dbc_out[rows, 0:STATE] = dbc_ref[rows, 0:STATE] + dot_nt(xw, gp_low)
        dbc_out[rows, STATE : 2 * STATE] = dbc_ref[rows, STATE : 2 * STATE] + dot_nt(yw, sp_low)
        sum_dt = dot_exact(tri, dt)
        sum_sl = dot_exact(tri, slope)
        all_dt = sum_dt[GROUP - 1 : GROUP, :]
        all_sl = sum_sl[GROUP - 1 : GROUP, :]
        inner = jnp.sum(sp * gp, axis=0, keepdims=True)
        meet = jnp.exp(last[g]) * dot_exact(jnp.broadcast_to(inner, (8, inner.shape[1])), gather_e)[0:1, :]
        flow_dt_all += jnp.sum(back * sum_dt + fore * (all_dt - sum_dt), axis=0, keepdims=True) + meet * all_dt
        flow_sl_all += jnp.sum(back * sum_sl + fore * (all_sl - sum_sl), axis=0, keepdims=True) + meet * all_sl
        bias_all += jnp.sum(slope / dt * x_gb, axis=0, keepdims=True)
        skip_all += jnp.sum(skips, axis=0, keepdims=True)
    intra = flow_ref[0]
    for g in range(1, groups):
        intra = intra + flow_ref[g]
    totals = jnp.transpose(jnp.sum(intra, axis=1, keepdims=True) + jnp.zeros((2 * heads, 128), F32))[0:1, :]
    flow_dt_all += totals[:, 0:heads]
    flow_sl_all += totals[:, heads : 2 * heads]
    stat_ref[...] = jnp.zeros_like(stat_ref)
    stat_ref[0:1, 0:heads] = rate * flow_dt_all
    stat_ref[1:2, 0:heads] = bias_all + rate * flow_sl_all
    stat_ref[2:3, 0:heads] = skip_all


def full(shape):
    return pl.BlockSpec(shape, lambda *_: (0,) * len(shape))


def by_group(width):
    return pl.BlockSpec((GROUP, width), lambda g: (g, 0))


def call(kernel, out, name, flops, nbytes, **options):
    params = pltpu.CompilerParams(vmem_limit_bytes=options.pop("vmem", 56 * 1024 * 1024))
    cost = pl.CostEstimate(flops=flops, bytes_accessed=nbytes, transcendentals=0)
    return pl.pallas_call(kernel, out_shape=out, name=name, cost_estimate=cost, compiler_params=params, **options)


def on_device(layer_in, ssm_input, b_matrix, c_matrix, dt_raw, dt_bias, a_log, d_skip, grad_out):
    tokens, heads = dt_raw.shape
    width = heads * HEAD_DIM
    groups = tokens // GROUP
    devices = math.prod(lax.axis_size(axis) for axis in SEQ)
    rows = 2 * STATE // devices
    shifted = dt_raw + dt_bias[None, :]
    dt = jax.nn.softplus(shifted)
    slope = jax.nn.sigmoid(shifted)
    rate = -jnp.exp(a_log)
    log_step = dt * rate[None, :]
    sds = jax.ShapeDtypeStruct

    parts, ends = call(
        states_kernel,
        (sds((2 * groups - 2, STATE, width), F32), sds((2 * STATE, width + 128), F32)),
        "block_states", 10**9, 10**7,
        scratch_shapes=[VMEM((STATE, width), F32), VMEM((STATE, width), F32)],
    )(ssm_input, grad_out, b_matrix, c_matrix, dt, log_step)

    sent = ends.reshape(devices, rows, width + 128)
    got = lax.all_to_all(sent, SEQ, split_axis=0, concat_axis=0, tiled=True)
    position = lax.axis_index(SEQ)
    backward = (position >= devices // 2).astype(jnp.int32).reshape(1)
    scanned = call(
        scan_kernel, sds((devices, rows, width), F32), "carry_scan", 10**8, 3 * 10**6,
        in_specs=[pl.BlockSpec(memory_space=pltpu.SMEM), full((devices, rows, width + 128))],
        out_specs=full((devices, rows, width)),
        grid=(1,),
        scratch_shapes=[VMEM((devices, width), F32)],
    )(backward, got)
    carry = lax.all_to_all(scanned, SEQ, split_axis=0, concat_axis=0, tiled=True).reshape(2 * STATE, width)

    gi, dbc_local, flows = call(
        intra_kernel,
        (sds((tokens, width), BF16), sds((tokens, 2 * STATE), F32), sds((groups, 2 * heads, GROUP), F32)),
        "intra", 3 * 10**10, 8 * 10**6,
        grid=(groups,),
        in_specs=[by_group(width), by_group(width), by_group(STATE), by_group(STATE),
                  by_group(heads), by_group(heads), by_group(heads)],
        out_specs=(by_group(width), by_group(2 * STATE), pl.BlockSpec((1, 2 * heads, GROUP), lambda g: (g, 0, 0))),
        scratch_shapes=[VMEM((GROUP, GROUP), F32), VMEM((2, GROUP, GROUP), BF16)],
    )(ssm_input, grad_out, b_matrix, c_matrix, dt, slope, log_step)

    skip_wide = jnp.repeat(d_skip, HEAD_DIM)[None, :]
    dx, dbc, stats = call(
        final_kernel,
        (sds((tokens, width), BF16), sds((tokens, 2 * STATE), F32), sds((8, 128), F32)),
        "combine", 2 * 10**9, 2 * 10**7,
        scratch_shapes=[VMEM((groups, STATE, width), F32), VMEM((groups, STATE, width), F32)],
    )(ssm_input, grad_out, b_matrix, c_matrix, dt, slope, log_step, skip_wide, rate[None, :], gi, dbc_local,
      flows, parts, carry)

    grad_wx = lax.psum_scatter(
        lax.dot_general(layer_in, dx, (((0,), (0,)), ((), ())), preferred_element_type=F32),
        SEQ, scatter_dimension=0, tiled=True,
    )
    owned = lax.psum_scatter(dbc, "mp", scatter_dimension=1, tiled=True).astype(BF16)
    partial = lax.dot_general(layer_in, owned, (((0,), (0,)), ((), ())), preferred_element_type=F32)
    blocks = partial.reshape(devices, -1, owned.shape[1])
    extra = stats.reshape(-1, owned.shape[1])
    extra = jnp.broadcast_to(extra[None], (devices, *extra.shape))
    arrived = lax.all_to_all(
        jnp.concatenate([blocks, extra], axis=1), SEQ, split_axis=0, concat_axis=0, tiled=True
    ).sum(axis=0)
    grad_wbc = arrived[: blocks.shape[1]]
    totals = arrived[blocks.shape[1] :].reshape(8, 128)
    return (grad_wx, grad_wbc, totals[0, :heads], totals[1, :heads], totals[2, :heads])


def solution(mesh):
    n_seq, n_mp = mesh.shape["seq"], mesh.shape["mp"]
    split = Mesh(mesh.devices.reshape(n_seq // 8, 4, 2, n_mp), SEQ + ("mp",))
    in_specs = (
        P(SEQ, None),
        P(SEQ, "mp"),
        P(SEQ, None),
        P(SEQ, None),
        P(SEQ, "mp"),
        P("mp"),
        P("mp"),
        P("mp"),
        P(SEQ, "mp"),
    )
    out_specs = (P(SEQ, "mp"), P(SEQ, "mp"), P("mp"), P("mp"), P("mp"))
    return jax.shard_map(
        on_device, mesh=split, in_specs=in_specs, out_specs=out_specs, check_vma=False
    )
```

time: 425 us -> 241 us (0.57)
  blocking collectives: 102 us -> 23.5 us
  matrix products: 76.6 us -> 13.9 us
  other arithmetic: 56.7 us -> 3.5 us
  Pallas kernels: 0 us -> 49 us
  local copies, waits for them, and re-layouts: 68.5 us -> 24.2 us
  starting transfers between devices: 6.01 us -> 12.3 us
    all_gather x6 -> x0, waiting for transfers between devices: 81.6 us -> none  [carried_in(): pieces = jax.tree.map(lambda part: lax.all_gather(part, axis), subtotal)]
    psum x1 -> x0, blocking collectives: 72 us -> none  [together(): subtotal = lax.psum(flat, axis)]
    unnamed x9 -> x4, waiting for transfers between devices: 14.7 us -> 78 us
    dot_general x36 -> x2, matrix products: 76.6 us -> 13.9 us  [the longest x1 10.9 us: on_device(): lax.dot_general(layer_in, dx, (((0,), (0,)), ((), ())), preferred_element...]
    pallas_call x0 -> x4, Pallas kernels: none -> 49 us  [the longest x1 18.4 us: on_device(): call(intra_kernel, (sds((tokens, width), BF16), sds((tokens, 2 * STATE),...]
    all_gather x4 -> x0, blocking collectives: 29.9 us -> none  [carried_in(): pieces = jax.tree.map(lambda part: lax.all_gather(part, axis), subtotal)]
    all_to_all x0 -> x1, blocking collectives: none -> 23.5 us  [on_device(): lax.all_to_all(jnp.concatenate([blocks, extra], axis=1), SEQ, split_axis=...]
    all_to_all x1 -> x2, waiting for transfers between devices: 0.01 us -> 21.9 us  [the longest x1 21.4 us: on_device(): got = lax.all_to_all(sent, SEQ, split_axis=0, concat_axis=0, tiled=True)]
  transfers between devices with their start and end apart: 9 -> 4, of which waited for: 4 -> 3; matrix products, arithmetic and copies ran while one was open for 34% -> 13% of each run, Pallas kernels for 0% -> 8%
where the time goes in v1:
time: 241 us; the launch traced here: 240 us
  waiting for transfers between devices  99.9 us (41%)
  Pallas kernels  49 us (20%)
  local copies, waits for them, and re-layouts  24.2 us (10%)
  blocking collectives  23.5 us (10%)
  between operations  14.1 us (6%)
  matrix products  13.9 us (6%)
  starting transfers between devices  12.3 us (5%)
  other arithmetic  3.5 us (1%)
    unnamed x4, waiting for transfers between devices  78 us
    all_to_all x1, blocking collectives, on_device(): lax.all_to_all(jnp.concatenate([blocks, extra], axis=1), SEQ, split_axis=...  23.5 us
    all_to_all x1, waiting for transfers between devices, on_device(): got = lax.all_to_all(sent, SEQ, split_axis=0, concat_axis=0, tiled=True)  21.4 us
    unnamed x14, local copies, waits for them, and re-layouts  21.3 us
    pallas_call x1, Pallas kernels, on_device(): call(intra_kernel, (sds((tokens, width), BF16), sds((tokens, 2 * STATE),...  18.4 us
    pallas_call x1, Pallas kernels, on_device(): call(final_kernel, (sds((tokens, width), BF16), sds((tokens, 2 * STATE),...  16.6 us
    dot_general x1, matrix products, on_device(): lax.dot_general(layer_in, dx, (((0,), (0,)), ((), ())), preferred_element...  10.9 us
    pallas_call x1, Pallas kernels, on_device(): call(states_kernel, (sds((2 * groups - 2, STATE, width), F32), sds((2 * S...  10.9 us
  transfers between devices with their start and end apart: 4, of which 3 were waited for; matrix products, arithmetic and copies ran while one was open for 13% of the time, Pallas kernels for 8%

profile of v1, /device:TPU:0, one launch (start us, length us, event | category | flops | bytes accessed | tf_op | source)
XLA Modules:
  0.0 240.3 jit_solution(2869469665895430426)
XLA Ops:
  7.2 1.2 fusion.1
  8.3 1.1 copy.26
  9.4 1.9 broadcast_multiply_fusion
  11.3 10.9 %block_states.1 = (f32[4,128,1280]{2,1,0:T(8,128)}, f32[256,1408]{1,0:T(8,128)}) custom-call(bf16[768,1280]{1,0:T(8,128)(2,1)} %x_ref.5, bf16[768,1280]{1,0:T(8,128)(2,1)} %dy_ref.5, bf16[768,128]{1,0:T(8,128)(2,1)} %b_ref.5, bf16[768,128]{1,0:T(8,128)(2,1)} %c_ref.5, f32[768,20]{1,0:T(8,128)} %get-tuple-element.42.dt_ref, f32[768,20]{1,0:T(8,128)} %get-tuple-element.41.a_ref), custom_call_target="tpu_custom_call" | custom-call | flops 1000000000 | bytes 10000000 | tf_op jit(solution)/shard_map/block_states/pallas_call | solution.py:289
  22.2 8.3 %all-to-all-start = ((f32[32,8,1408]{2,1,0:T(8,128)}), f32[32,8,1408]{2,1,0:T(8,128)S(1)}, u32[]{:S(2)}, u32[]{:S(2)}) async-start(f32[32,8,1408]{2,1,0:T(8,128)} %bitcast.27), calls=%async_computation | async-start | bytes 2883584 | tf_op jit(solution)/shard_map/all_to_all | solution.py:297
  30.4 21.4 %all-to-all-done.in_ref = f32[32,8,1408]{2,1,0:T(8,128)S(1)} async-done(((f32[32,8,1408]{2,1,0:T(8,128)}), f32[32,8,1408]{2,1,0:T(8,128)S(1)}, u32[]{:S(2)}, u32[]{:S(2)}) %all-to-all-start) | async-done | bytes 1441824 | tf_op jit(solution)/shard_map/all_to_all | solution.py:297
  51.8 0.0 copy-start
  51.8 1.1 copy-done
  52.9 3.1 %carry_scan.1 = f32[32,8,1280]{2,1,0:T(8,128)} custom-call(s32[1]{0:T(128)} %bitcast.1.half_ref, f32[32,8,1408]{2,1,0:T(8,128)} %copy-done), custom_call_target="tpu_custom_call" | custom-call | flops 100000000 | bytes 3000000 | tf_op jit(solution)/shard_map/carry_scan/pallas_call | solution.py:300
  56.0 3.9 %all-to-all-start.1 = ((f32[32,8,1280]{2,1,0:T(8,128)}), f32[32,8,1280]{2,1,0:T(8,128)S(1)}, u32[]{:S(2)}, u32[]{:S(2)}) async-start(f32[32,8,1280]{2,1,0:T(8,128)} %carry_scan.1), calls=%async_computation.1 | async-start | bytes 2621440 | tf_op jit(solution)/shard_map/all_to_all | solution.py:307
  60.0 0.0 reduce-scatter.9.cloned.1.call-start
  60.0 0.0 copy-start.4
  60.0 18.4 %intra.1 = (bf16[768,1280]{1,0:T(8,128)(2,1)}, f32[768,256]{1,0:T(8,128)}, f32[3,40,256]{2,1,0:T(8,128)}) custom-call(bf16[768,1280]{1,0:T(8,128)(2,1)} %x_ref.5, bf16[768,1280]{1,0:T(8,128)(2,1)} %dy_ref.5, bf16[768,128]{1,0:T(8,128)(2,1)} %b_ref.5, bf16[768,128]{1,0:T(8,128)(2,1)} %c_ref.5, f32[768,20]{1,0:T(8,128)} %get-tuple-element.42.dt_ref, ...), custom_call_target="tpu_custom_call" | custom-call | flops 30000001024 | bytes 8000000 | tf_op jit(solution)/shard_map/intra/pallas_call | solution.py:309
  78.5 0.0 copy-done.4
  78.5 0.1 broadcast_in_dim.15
  78.5 0.7 broadcast_in_dim_reshape.4.skip_ref
  79.2 0.5 all-to-all-done.1
  79.7 0.0 copy-start.1
  79.7 1.1 copy-done.1
  80.8 16.6 %combine.1 = (bf16[768,1280]{1,0:T(8,128)(2,1)}, f32[768,256]{1,0:T(8,128)}, f32[8,128]{1,0:T(8,128)}) custom-call(bf16[768,1280]{1,0:T(8,128)(2,1)} %x_ref.5, bf16[768,1280]{1,0:T(8,128)(2,1)} %dy_ref.5, bf16[768,128]{1,0:T(8,128)(2,1)} %b_ref.5, bf16[768,128]{1,0:T(8,128)(2,1)} %c_ref.5, f32[768,20]{1,0:T(8,128)} %get-tuple-element.42.dt_ref, ...), custom_call_target="tpu_custom_call" | custom-call | flops 2000000000 | bytes 20000000 | tf_op jit(solution)/shard_map/combine/pallas_call | solution.py:321
  97.4 2.3 copy.34
  99.7 0.0 reduce-scatter.9.cloned.1.call-update
  99.7 0.0 reduce-scatter.7.cloned.1.call-start
  99.7 10.9 %convolution_bitcast_fusion = f32[2560,1280]{0,1:T(8,128)} fusion(bf16[768,1280]{1,0:T(8,128)(2,1)} %get-tuple-element.18, bf16[768,2560]{1,0:T(8,128)(2,1)} %param.9), kind=kOutput, calls=%fused_computation | convolution fusion | flops 5033164800 | bytes 19005440 | tf_op jit(solution)/shard_map/dot_general | solution.py:330
  110.7 14.0 %copy.32 = f32[2560,1280]{1,0:T(8,128)} copy(f32[2560,1280]{0,1:T(8,128)} %convolution_bitcast_fusion) | data formatting | bytes 26214400
  124.7 0.0 copy-start.3
  124.7 0.0 reduce-scatter.7.cloned.1.call-update
  124.7 0.7 copy-done.3
  125.4 0.1 broadcast_in_dim.17
  125.4 0.1 copy.28
  125.5 0.0 reduce-scatter.9.cloned.1.call-done
  125.5 1.1 copy.35
  126.6 2.9 %convolution_bitcast_fusion.1 = f32[2560,64]{0,1:T(8,128)S(1)} fusion(bf16[768,2560]{1,0:T(8,128)(2,1)} %param.9, bf16[768,64]{1,0:T(8,128)(2,1)S(1)} %copy.35), kind=kOutput, calls=%fused_computation.1 | convolution fusion | flops 251658240 | bytes 4685824 | tf_op jit(solution)/shard_map/dot_general | solution.py:334
  129.6 0.5 reshape.34
  130.1 0.6 copy.29
  130.7 0.1 broadcast_in_dim.18
  130.8 0.3 pad_maximum_fusion
  131.2 23.5 %all_to_all.15 = f32[32,96,64]{1,2,0:T(8,128)S(1)} all-to-all(f32[32,96,64]{1,2,0:T(8,128)S(1)} %pad_maximum_fusion), channel_id=1, replica_groups=mesh['seq_0'=4,'seq_1'=4,'seq_2'=2,'mp'=4] {'seq_0','seq_1','seq_2'}, dimensions={0} | all-to-all | bytes 1572864 | tf_op jit(solution)/shard_map/all_to_all | solution.py:338
  154.6 0.1 reduce_sum.9
  154.7 0.0 copy-start.2
  154.7 0.1 slice.21
  154.8 0.1 copy.30
  154.9 0.1 reshape.35
  155.0 0.5 slice_bitcast_fusion
  155.5 78.0 %reduce-scatter.7.cloned.1.call-done = f32[80,1280]{1,0:T(8,128)} async-done(((f32[2560,1280]{1,0:T(8,128)}), f32[80,1280]{1,0:T(8,128)}) %reduce-scatter.7.cloned.1.call-update) | async-done | bytes 409616
  233.5 0.0 copy-done.2
Async XLA Ops:
  22.2 29.6 %all-to-all-start = ((f32[32,8,1408]{2,1,0:T(8,128)}), f32[32,8,1408]{2,1,0:T(8,128)S(1)}, u32[]{:S(2)}, u32[]{:S(2)}) async-start(f32[32,8,1408]{2,1,0:T(8,128)} %bitcast.27), calls=%async_computation | async-start | bytes 2883584 | tf_op jit(solution)/shard_map/all_to_all | solution.py:297
  51.8 1.1 copy-start
  56.0 23.7 %all-to-all-start.1 = ((f32[32,8,1280]{2,1,0:T(8,128)}), f32[32,8,1280]{2,1,0:T(8,128)S(1)}, u32[]{:S(2)}, u32[]{:S(2)}) async-start(f32[32,8,1280]{2,1,0:T(8,128)} %carry_scan.1), calls=%async_computation.1 | async-start | bytes 2621440 | tf_op jit(solution)/shard_map/all_to_all | solution.py:307
  60.0 65.6 %reduce-scatter.9.cloned.1.call-start = ((), (), s32[]{:S(2)}) async-start(), calls=%async_computation.6 | async-start | bytes 983040
  60.0 18.4 %copy-start.4 = (f32[20]{0:T(128)S(1)}, f32[20]{0:T(128)}, u32[]{:S(2)}) copy-start(f32[20]{0:T(128)} %param.16) | copy-start | bytes 244
  79.7 1.1 copy-start.1
  99.7 133.8 %reduce-scatter.7.cloned.1.call-start = ((), (), s32[]{:S(2)}) async-start(), calls=%async_computation.5 | async-start | bytes 13516800
  124.7 0.7 copy-start.3
  154.7 78.8 %copy-start.2 = (f32[96,64]{0,1:T(8,128)}, f32[96,64]{0,1:T(8,128)S(1)}, u32[]{:S(2)}) copy-start(f32[96,64]{0,1:T(8,128)S(1)} %reduce_sum.9) | copy-start | bytes 73732
Sparse Core Ops, SparseCore 0:
  99.8 23.7 reduce-scatter.8
  128.0 105.4 reduce-scatter.6

commit v2 on v1

--- a/solution.py
+++ b/solution.py
@@ -235,8 +235,15 @@
         yw = (dy * rise_wide).astype(BF16)
         from_start = dot(c, sp_low)
         back = rise * dot((dy * from_start).astype(BF16), gather_m)
-        dbc_out[rows, 0:STATE] = dbc_ref[rows, 0:STATE] + dot_nt(xw, gp_low)
-        dbc_out[rows, STATE : 2 * STATE] = dbc_ref[rows, STATE : 2 * STATE] + dot_nt(yw, sp_low)
+        grads = (dbc_ref[rows, 0:STATE] + dot_nt(xw, gp_low), dbc_ref[rows, STATE : 2 * STATE] + dot_nt(yw, sp_low))
+        for piece in range(GROUP // 128):
+            at = g * (GROUP // 128) + piece
+            side, base = divmod(at * 128, dbc_out.shape[1])
+            for m in range(dbc_out.shape[0]):
+                source, left = divmod(m * 64, STATE)
+                dbc_out[m, base : base + 128, side * 64 : side * 64 + 64] = grads[source][
+                    piece * 128 : (piece + 1) * 128, left : left + 64
+                ]
         sum_dt = dot_exact(tri, dt)
         sum_sl = dot_exact(tri, slope)
         all_dt = sum_dt[GROUP - 1 : GROUP, :]
@@ -259,6 +266,254 @@
     stat_ref[2:3, 0:heads] = skip_all
 
 
+MESH = pl.DeviceIdType.MESH
+W_ROWS = 48
+
+
+def around(axis, shift):
+    return {axis: lax.rem(lax.axis_index(axis) + shift, 4)}
+
+
+def remote(source, target, send, recv, device):
+    return pltpu.make_async_remote_copy(
+        src_ref=source, dst_ref=target, send_sem=send, recv_sem=recv, device_id=device, device_id_type=MESH
+    )
+
+
+class RingSum:
+    def __init__(self, axis, part, relay, final, send, recv, base):
+        self.axis, self.part, self.relay, self.final = axis, part, relay, final
+        self.send, self.recv, self.base = send, recv, base
+        me = lax.axis_index(axis)
+        self.me = me
+        self.ahead, self.behind, self.across = (lax.rem(me + k, 4) for k in (1, 3, 2))
+        self.up, self.down = around(axis, 1), around(axis, 3)
+        self.copies = {}
+
+    def copy(self, n, source, target, device):
+        at = self.base + n
+        self.copies[n] = remote(source, target, self.send(at), self.recv(at), device)
+        self.copies[n].start()
+
+    def first(self):
+        self.copy(0, self.part(self.across, 0), self.relay(0), self.up)
+        self.copy(1, self.part(self.across, 1), self.relay(1), self.down)
+        self.copy(2, self.part(self.ahead, 1), self.final(0, 1), self.up)
+        self.copy(3, self.part(self.behind, 0), self.final(1, 0), self.down)
+
+    def second(self):
+        self.copies[0].wait_recv()
+        ahead = self.part(self.ahead, 0)
+        ahead[...] += self.relay(0)[...]
+        self.copy(4, ahead, self.final(0, 0), self.up)
+        self.copies[1].wait_recv()
+        behind = self.part(self.behind, 1)
+        behind[...] += self.relay(1)[...]
+        self.copy(5, behind, self.final(1, 1), self.down)
+
+    def result(self, half):
+        (self.copies[4] if half == 0 else self.copies[2]).wait_recv()
+        (self.copies[3] if half == 0 else self.copies[5]).wait_recv()
+        return self.part(self.me, half)[...] + self.final(0, half)[...] + self.final(1, half)[...]
+
+    def drain(self):
+        for copy in self.copies.values():
+            copy.wait_send()
+
+
+class PlaneSum:
+    def __init__(self, first_axis, second_axis, swap, own, relay, final, mid, relay2, final2, send, recv, store):
+        rows = mid.shape[1]
+        self.store, self.mid, self.rows = store, mid, rows
+
+        def part(d, half):
+            pair = pl.ds(2 * half, 2)
+            return own.at[pair, d] if swap else own.at[d, pair]
+
+        def part2(d, half):
+            return mid.at[d, pl.ds(half * (rows // 2), rows // 2)]
+
+        self.one = RingSum(first_axis, part, lambda h: relay.at[h], lambda w, h: final.at[w, pl.ds(2 * h, 2)],
+                           send, recv, 0)
+        self.two = RingSum(second_axis, part2, lambda h: relay2.at[h],
+                           lambda w, h: final2.at[w, pl.ds(h * (rows // 2), rows // 2)], send, recv, 6)
+
+    def run(self, stage):
+        if stage == 0:
+            self.one.first()
+        elif stage == 1:
+            self.one.second()
+        elif stage == 2:
+            for half in range(2):
+                self.mid[pl.ds(2 * half, 2)] = self.one.result(half)
+            self.two.first()
+        elif stage == 3:
+            self.two.second()
+        elif stage == 4:
+            for half in range(2):
+                self.store(half, self.two.result(half))
+
+    def drain(self):
+        self.one.drain()
+        self.two.drain()
+
+
+def project_kernel(lt_hbm, dx_hbm, dbc_ref, stats_ref, wx_ref, wbc_ref, total_ref,
+                   lt, dx, dbc_in, work, relay, final, mid, relay2, final2,
+                   w_work, w_relay, w_final, w_mid, w_relay2, w_final2,
+                   load_sem, mp_send, mp_recv, core_send, core_recv, send, recv):
+    block = wx_ref.shape[0]
+    chunks = work.shape[1]
+    core = lax.axis_index("seq_2")
+    mp = lax.axis_index("mp")
+    other = {"seq_2": 1 - core}
+
+    loads = [pltpu.make_async_copy(dx_hbm, dx, load_sem.at[32])]
+    loads[0].start()
+    for slot in range(2):
+        kind = 1 - core if slot == 0 else core
+        for k in range(16):
+            start = pl.multiple_of((2 * k + kind) * block, 16)
+            load = pltpu.make_async_copy(
+                lt_hbm.at[pl.ds(start, block)], lt.at[slot, pl.ds(k * block, block)], load_sem.at[slot * 16 + k]
+            )
+            load.start()
+            loads.append(load)
+
+    partners = [other] + [around(axis, k) for axis in ("seq_0", "seq_1") for k in (1, 3)]
+    partners += [around("mp", k) for k in (1, 2, 3)]
+    barrier = pltpu.get_barrier_semaphore()
+    for partner in partners:
+        pl.semaphore_signal(barrier, inc=1, device_id=partner, device_id_type=MESH)
+    pl.semaphore_wait(barrier, len(partners))
+
+    mp_copies = []
+    for k in (1, 2, 3):
+        target = around("mp", k)
+        copy = remote(dbc_ref.at[target["mp"]], dbc_in.at[k - 1], mp_send.at[k - 1], mp_recv.at[k - 1], target)
+        copy.start()
+        mp_copies.append(copy)
+
+    for load in loads:
+        load.wait()
+
+    send_own, got, own = (work.at[i] for i in range(3))
+    core_copies = {}
+
+    def give(j):
+        cols = dx[:, j * 256 : (j + 1) * 256]
+
+        def body(i, unused):
+            start = pl.multiple_of(i * 4 * block, 16)
+            res = dot(lt[0, pl.ds(start, 4 * block), :], cols)
+            for side in range(2):
+                send_own[j, side, i] = res[:, side * 128 : (side + 1) * 128].reshape(4, block, 128)
+            return unused
+
+        lax.fori_loop(0, 4, body, 0)
+        core_copies[j] = remote(send_own.at[j], got.at[j], core_send.at[j], core_recv.at[j], other)
+        core_copies[j].start()
+
+    def keep(j):
+        core_copies[j].wait_recv()
+        cols = dx[:, j * 256 : (j + 1) * 256]
+
+        def body(i, unused):
+            start = pl.multiple_of(i * 4 * block, 16)
+            res = dot(lt[1, pl.ds(start, 4 * block), :], cols)
+            for side in range(2):
+                own[j, side, i] = got[j, side, i] + res[:, side * 128 : (side + 1) * 128].reshape(4, block, 128)
+            return unused
+
+        lax.fori_loop(0, 4, body, 0)
+
+    def narrow(slot, i, cols):
+        start = pl.multiple_of(i * 4 * block, 16)
+        res = dot(lt[slot, pl.ds(start, 4 * block), :], cols).reshape(4, block, 64)
+        grads = jnp.concatenate([res[:, 0 : block // 2], res[:, block // 2 : block]], axis=2)
+        stats = jnp.broadcast_to(stats_ref[...][None], (4, 8, 128))
+        return jnp.concatenate([grads, stats], axis=1)
+
+    def owned_cols():
+        for copy in mp_copies:
+            copy.wait_recv()
+        owned = dbc_ref[mp] + dbc_in[0] + dbc_in[1] + dbc_in[2]
+        return jnp.concatenate([owned[:, 0:64], owned[:, 64:128]], axis=0).astype(BF16)
+
+    def give_narrow(cols):
+        def body(i, unused):
+            w_work[0, i] = narrow(0, i, cols)
+            return unused
+
+        lax.fori_loop(0, 4, body, 0)
+        core_copies[chunks] = remote(
+            w_work.at[0], w_work.at[1], core_send.at[chunks], core_recv.at[chunks], other
+        )
+        core_copies[chunks].start()
+
+    def keep_narrow(cols):
+        core_copies[chunks].wait_recv()
+
+        def body(i, unused):
+            w_work[2, i] = w_work[1, i] + narrow(1, i, cols)
+            return unused
+
+        lax.fori_loop(0, 4, body, 0)
+
+    def store_wide(j, side):
+        def store(half, value):
+            wx_ref[half * (block // 2) : (half + 1) * (block // 2), j * 256 + side * 128 : j * 256 + side * 128 + 128] = value
+
+        return store
+
+    def store_narrow(half, value):
+        w_work[0, 0, 0, half * (W_ROWS // 2) : (half + 1) * (W_ROWS // 2)] = value
+
+    def stream(j, side):
+        axes = ("seq_0", "seq_1") if side == 0 else ("seq_1", "seq_0")
+        n = 2 * j + side
+        return PlaneSum(*axes, side == 1, own.at[j, side], relay.at[:, j, side], final.at[:, j, side],
+                        mid.at[j, side], relay2.at[:, j, side], final2.at[:, j, side],
+                        lambda k: send.at[n, k], lambda k: recv.at[n, k], store_wide(j, side))
+
+    streams = [[stream(j, 0), stream(j, 1)] for j in range(chunks)]
+    last = 2 * chunks
+    streams.append([PlaneSum("seq_0", "seq_1", False, w_work.at[2], w_relay, w_final, w_mid, w_relay2, w_final2,
+                             lambda k: send.at[last, k], lambda k: recv.at[last, k], store_narrow)])
+
+    cols_low = []
+    give(0)
+    for t in range(chunks + 6):
+        if t + 1 < chunks:
+            give(t + 1)
+        elif t + 1 == chunks:
+            cols_low.append(owned_cols())
+            give_narrow(cols_low[0])
+        if t < chunks:
+            keep(t)
+        elif t == chunks:
+            keep_narrow(cols_low[0])
+        for stage in range(5):
+            j = t - stage
+            if 0 <= j <= chunks:
+                if stage == 4 and j == chunks:
+                    core_copies[chunks].wait_send()
+                for one in streams[j]:
+                    one.run(stage)
+
+    half = block // 2
+    wbc_ref[0:half, :] = w_work[0, 0, 0, 0:half, 0:64]
+    wbc_ref[half:block, :] = w_work[0, 0, 0, 0:half, 64:128]
+    total_ref[...] = w_work[0, 0, 0, half : half + 8, :]
+    for copy in mp_copies:
+        copy.wait_send()
+    for j in range(chunks):
+        core_copies[j].wait_send()
+    for group in streams:
+        for one in group:
+            one.drain()
+
+
 def full(shape):
     return pl.BlockSpec(shape, lambda *_: (0,) * len(shape))
 
@@ -320,26 +575,51 @@
     skip_wide = jnp.repeat(d_skip, HEAD_DIM)[None, :]
     dx, dbc, stats = call(
         final_kernel,
-        (sds((tokens, width), BF16), sds((tokens, 2 * STATE), F32), sds((8, 128), F32)),
+        (sds((tokens, width), BF16), sds((4, tokens // 2, 128), F32), sds((8, 128), F32)),
         "combine", 2 * 10**9, 2 * 10**7,
         scratch_shapes=[VMEM((groups, STATE, width), F32), VMEM((groups, STATE, width), F32)],
     )(ssm_input, grad_out, b_matrix, c_matrix, dt, slope, log_step, skip_wide, rate[None, :], gi, dbc_local,
       flows, parts, carry)
 
-    grad_wx = lax.psum_scatter(
-        lax.dot_general(layer_in, dx, (((0,), (0,)), ((), ())), preferred_element_type=F32),
-        SEQ, scatter_dimension=0, tiled=True,
-    )
-    owned = lax.psum_scatter(dbc, "mp", scatter_dimension=1, tiled=True).astype(BF16)
-    partial = lax.dot_general(layer_in, owned, (((0,), (0,)), ((), ())), preferred_element_type=F32)
-    blocks = partial.reshape(devices, -1, owned.shape[1])
-    extra = stats.reshape(-1, owned.shape[1])
-    extra = jnp.broadcast_to(extra[None], (devices, *extra.shape))
-    arrived = lax.all_to_all(
-        jnp.concatenate([blocks, extra], axis=1), SEQ, split_axis=0, concat_axis=0, tiled=True
-    ).sum(axis=0)
-    grad_wbc = arrived[: blocks.shape[1]]
-    totals = arrived[blocks.shape[1] :].reshape(8, 128)
+    flipped = layer_in.T
+    block = flipped.shape[0] // devices
+    chunks = width // 256
+    grad_wx, grad_wbc, totals = pl.pallas_call(
+        project_kernel,
+        out_shape=(sds((block, width), F32), sds((block, 64), F32), sds((8, 128), F32)),
+        in_specs=[pl.BlockSpec(memory_space=pl.ANY), pl.BlockSpec(memory_space=pl.ANY),
+                  pl.BlockSpec(memory_space=VMEM), pl.BlockSpec(memory_space=VMEM)],
+        out_specs=(pl.BlockSpec(memory_space=VMEM),) * 3,
+        scratch_shapes=[
+            VMEM((2, 16 * block, tokens), BF16),
+            VMEM((tokens, width), BF16),
+            VMEM((3, tokens // 2, 128), F32),
+            VMEM((3, chunks, 2, 4, 4, block, 128), F32),
+            VMEM((2, chunks, 2, 2, block, 128), F32),
+            VMEM((2, chunks, 2, 4, block, 128), F32),
+            VMEM((chunks, 2, 4, block, 128), F32),
+            VMEM((2, chunks, 2, block // 2, 128), F32),
+            VMEM((2, chunks, 2, block, 128), F32),
+            VMEM((3, 4, 4, W_ROWS, 128), F32),
+            VMEM((2, 2, W_ROWS, 128), F32),
+            VMEM((2, 4, W_ROWS, 128), F32),
+            VMEM((4, W_ROWS, 128), F32),
+            VMEM((2, W_ROWS // 2, 128), F32),
+            VMEM((2, W_ROWS, 128), F32),
+            pltpu.SemaphoreType.DMA((33,)),
+            pltpu.SemaphoreType.DMA((3,)),
+            pltpu.SemaphoreType.DMA((3,)),
+            pltpu.SemaphoreType.DMA((chunks + 1,)),
+            pltpu.SemaphoreType.DMA((chunks + 1,)),
+            pltpu.SemaphoreType.DMA((2 * chunks + 1, 12)),
+            pltpu.SemaphoreType.DMA((2 * chunks + 1, 12)),
+        ],
+        name="project",
+        cost_estimate=pl.CostEstimate(flops=5 * 10**9, bytes_accessed=10**7, transcendentals=0),
+        compiler_params=pltpu.CompilerParams(
+            collective_id=0, has_side_effects=True, vmem_limit_bytes=60 * 1024 * 1024
+        ),
+    )(flipped, dx, dbc, stats)
     return (grad_wx, grad_wbc, totals[0, :heads], totals[1, :heads], totals[2, :heads])
 
 

time: 241 us -> 161 us (0.67)
  waiting for transfers between devices: 99.9 us -> 21.4 us
  Pallas kernels: 49 us -> 108 us
  blocking collectives: 23.5 us -> 0 us
  matrix products: 13.9 us -> 0 us
  between operations: 14.1 us -> 0.69 us
  local copies, waits for them, and re-layouts: 24.2 us -> 14.8 us
    unnamed x4 -> x0, waiting for transfers between devices: 78 us -> none
    pallas_call x1 -> x2, Pallas kernels: 16.6 us -> 75.5 us  [the longest x1 58.9 us: on_device(): pl.pallas_call(project_kernel, out_shape=(sds((block, width), F32), sds((...]
    all_to_all x1 -> x0, blocking collectives: 23.5 us -> none  [on_device(): lax.all_to_all(jnp.concatenate([blocks, extra], axis=1), SEQ, split_axis=...]
    dot_general x2 -> x0, matrix products: 13.9 us -> none  [the longest x1 10.9 us: on_device(): lax.dot_general(layer_in, dx, (((0,), (0,)), ((), ())), preferred_element...]
    unnamed x14 -> x10, local copies, waits for them, and re-layouts: 21.3 us -> 12.8 us
  transfers between devices with their start and end apart: 4 -> 2, of which waited for: 3 -> 1; matrix products, arithmetic and copies ran while one was open for 13% -> 4% of each run, Pallas kernels for 8% -> 11%
where the time goes in v2:
time: 161 us; the launch traced here: 160 us
  Pallas kernels  108 us (67%)
  waiting for transfers between devices  21.4 us (13%)
  local copies, waits for them, and re-layouts  14.8 us (9%)
  starting transfers between devices  12.2 us (8%)
  other arithmetic  3.1 us (2%)
    pallas_call x1, Pallas kernels, on_device(): pl.pallas_call(project_kernel, out_shape=(sds((block, width), F32), sds((...  58.9 us
    all_to_all x1, waiting for transfers between devices, on_device(): got = lax.all_to_all(sent, SEQ, split_axis=0, concat_axis=0, tiled=True)  21.4 us
    pallas_call x1, Pallas kernels, on_device(): call(intra_kernel, (sds((tokens, width), BF16), sds((tokens, 2 * STATE),...  18.4 us
    pallas_call x1, Pallas kernels, on_device(): call(final_kernel, (sds((tokens, width), BF16), sds((4, tokens // 2, 128)...  16.6 us
    unnamed x10, local copies, waits for them, and re-layouts  12.8 us
    pallas_call x1, Pallas kernels, on_device(): call(states_kernel, (sds((2 * groups - 2, STATE, width), F32), sds((2 * S...  10.9 us
    all_to_all x1, starting transfers between devices, on_device(): got = lax.all_to_all(sent, SEQ, split_axis=0, concat_axis=0, tiled=True)  8.27 us
    all_to_all x1, starting transfers between devices, on_device(): lax.all_to_all(scanned, SEQ, split_axis=0, concat_axis=0, tiled=True)  3.95 us
  transfers between devices with their start and end apart: 2, of which 1 were waited for; matrix products, arithmetic and copies ran while one was open for 4% of the time, Pallas kernels for 11%

profile of v2, /device:TPU:0, one launch (start us, length us, event | category | flops | bytes accessed | tf_op | source)
XLA Modules:
  0.0 160.1 jit_solution(7165588524087859045)
XLA Ops:
  0.6 1.2 fusion
  1.8 1.1 copy.18
  2.9 1.9 %broadcast_multiply_fusion = (f32[768,20]{1,0:T(8,128)}, f32[768,20]{1,0:T(8,128)}, f32[768,20]{1,0:T(8,128)}) fusion(f32[20]{0:T(128)S(1)} %get-tuple-element.44, f32[768,20]{1,0:T(8,128)S(1)} %copy.18, f32[20]{0:T(128)} %param.14), kind=kLoop, calls=%fused_computation.2 | loop fusion | flops 168960 | bytes 245920 | tf_op jit(solution)/shard_map/mul | solution.py:541
  4.8 10.9 %block_states.1 = (f32[4,128,1280]{2,1,0:T(8,128)}, f32[256,1408]{1,0:T(8,128)}) custom-call(bf16[768,1280]{1,0:T(8,128)(2,1)} %x_ref.5, bf16[768,1280]{1,0:T(8,128)(2,1)} %dy_ref.5, bf16[768,128]{1,0:T(8,128)(2,1)} %b_ref.5, bf16[768,128]{1,0:T(8,128)(2,1)} %c_ref.5, f32[768,20]{1,0:T(8,128)} %get-tuple-element.38.dt_ref, f32[768,20]{1,0:T(8,128)} %get-tuple-element.37.a_ref), custom_call_target="tpu_custom_call" | custom-call | flops 1000000000 | bytes 10000000 | tf_op jit(solution)/shard_map/block_states/pallas_call | solution.py:544
  15.7 8.3 %all-to-all-start = ((f32[32,8,1408]{2,1,0:T(8,128)}), f32[32,8,1408]{2,1,0:T(8,128)S(1)}, u32[]{:S(2)}, u32[]{:S(2)}) async-start(f32[32,8,1408]{2,1,0:T(8,128)} %bitcast.14), calls=%async_computation | async-start | bytes 2883584 | tf_op jit(solution)/shard_map/all_to_all | solution.py:552
  24.0 21.4 %all-to-all-done.in_ref = f32[32,8,1408]{2,1,0:T(8,128)S(1)} async-done(((f32[32,8,1408]{2,1,0:T(8,128)}), f32[32,8,1408]{2,1,0:T(8,128)S(1)}, u32[]{:S(2)}, u32[]{:S(2)}) %all-to-all-start) | async-done | bytes 1441824 | tf_op jit(solution)/shard_map/all_to_all | solution.py:552
  45.3 0.0 copy-start
  45.3 1.1 copy-done
  46.4 3.1 %carry_scan.1 = f32[32,8,1280]{2,1,0:T(8,128)} custom-call(s32[1]{0:T(128)} %bitcast.2.half_ref, f32[32,8,1408]{2,1,0:T(8,128)} %copy-done), custom_call_target="tpu_custom_call" | custom-call | flops 100000000 | bytes 3000000 | tf_op jit(solution)/shard_map/carry_scan/pallas_call | solution.py:555
  49.5 3.9 %all-to-all-start.1 = ((f32[32,8,1280]{2,1,0:T(8,128)}), f32[32,8,1280]{2,1,0:T(8,128)S(1)}, u32[]{:S(2)}, u32[]{:S(2)}) async-start(f32[32,8,1280]{2,1,0:T(8,128)} %carry_scan.1), calls=%async_computation.1 | async-start | bytes 2621440 | tf_op jit(solution)/shard_map/all_to_all | solution.py:562
  53.5 0.0 copy-start.2
  53.5 18.4 %intra.1 = (bf16[768,1280]{1,0:T(8,128)(2,1)}, f32[768,256]{1,0:T(8,128)}, f32[3,40,256]{2,1,0:T(8,128)}) custom-call(bf16[768,1280]{1,0:T(8,128)(2,1)} %x_ref.5, bf16[768,1280]{1,0:T(8,128)(2,1)} %dy_ref.5, bf16[768,128]{1,0:T(8,128)(2,1)} %b_ref.5, bf16[768,128]{1,0:T(8,128)(2,1)} %c_ref.5, f32[768,20]{1,0:T(8,128)} %get-tuple-element.38.dt_ref, ...), custom_call_target="tpu_custom_call" | custom-call | flops 30000001024 | bytes 8000000 | tf_op jit(solution)/shard_map/intra/pallas_call | solution.py:564
  71.9 0.0 copy-done.2
  71.9 0.1 broadcast_in_dim.8
  72.0 0.7 broadcast_in_dim_reshape.3.skip_ref
  72.6 6.3 %copy.17 = bf16[768,2560]{0,1:T(8,128)(2,1)} copy(bf16[768,2560]{1,0:T(8,128)(2,1)} %param.9) | data formatting | bytes 7864320 | tf_op args[0]
  78.9 0.0 all-to-all-done.1
  78.9 0.0 copy-start.1
  78.9 1.1 copy-done.1
  80.0 16.6 %combine.1 = (bf16[768,1280]{1,0:T(8,128)(2,1)}, f32[4,384,128]{2,1,0:T(8,128)}, f32[8,128]{1,0:T(8,128)}) custom-call(bf16[768,1280]{1,0:T(8,128)(2,1)} %x_ref.5, bf16[768,1280]{1,0:T(8,128)(2,1)} %dy_ref.5, bf16[768,128]{1,0:T(8,128)(2,1)} %b_ref.5, bf16[768,128]{1,0:T(8,128)(2,1)} %c_ref.5, f32[768,20]{1,0:T(8,128)} %get-tuple-element.38.dt_ref, ...), custom_call_target="tpu_custom_call" | custom-call | flops 2000000000 | bytes 20000000 | tf_op jit(solution)/shard_map/combine/pallas_call | solution.py:576
  96.6 58.9 %project.1 = (f32[80,1280]{1,0:T(8,128)}, f32[80,64]{1,0:T(8,128)}, f32[8,128]{1,0:T(8,128)}) custom-call(bf16[2560,768]{1,0:T(8,128)(2,1)} %bitcast.13, bf16[768,1280]{1,0:T(8,128)(2,1)} %get-tuple-element.21.dx_hbm, f32[4,384,128]{2,1,0:T(8,128)} %get-tuple-element.22.dbc_ref, f32[8,128]{1,0:T(8,128)} %get-tuple-element.23.stats_ref), custom_call_target="tpu_custom_call" | custom-call | flops 5000000000 | bytes 10000000 | tf_op jit(solution)/shard_map/project/pallas_call | solution.py:587
  155.5 1.5 copy.20
  157.0 1.3 slice_bitcast_fusion
  158.3 1.8 %copy.22 = f32[80,1280]{1,0:T(8,128)} copy(f32[80,1280]{1,0:T(8,128)} %get-tuple-element.50) | data formatting | bytes 819200
Async XLA Ops:
  15.7 29.6 %all-to-all-start = ((f32[32,8,1408]{2,1,0:T(8,128)}), f32[32,8,1408]{2,1,0:T(8,128)S(1)}, u32[]{:S(2)}, u32[]{:S(2)}) async-start(f32[32,8,1408]{2,1,0:T(8,128)} %bitcast.14), calls=%async_computation | async-start | bytes 2883584 | tf_op jit(solution)/shard_map/all_to_all | solution.py:552
  45.3 1.1 copy-start
  49.5 29.4 %all-to-all-start.1 = ((f32[32,8,1280]{2,1,0:T(8,128)}), f32[32,8,1280]{2,1,0:T(8,128)S(1)}, u32[]{:S(2)}, u32[]{:S(2)}) async-start(f32[32,8,1280]{2,1,0:T(8,128)} %carry_scan.1), calls=%async_computation.1 | async-start | bytes 2621440 | tf_op jit(solution)/shard_map/all_to_all | solution.py:562
  53.5 18.4 %copy-start.2 = (f32[20]{0:T(128)S(1)}, f32[20]{0:T(128)}, u32[]{:S(2)}) copy-start(f32[20]{0:T(128)} %param.16) | copy-start | bytes 244
  78.9 1.1 copy-start.1

commit v3 on v2

v3 whole, which is shorter than its diff:
```python
import functools
import math

import jax
import jax.numpy as jnp
from jax import lax
from jax.experimental import pallas as pl
from jax.experimental.pallas import tpu as pltpu
from jax.sharding import Mesh
from jax.sharding import PartitionSpec as P

GROUP = 256
HEAD_DIM = 64
STATE = 128
LOG2E = 1.0 / math.log(2.0)
SEQ = ("seq_0", "seq_1", "seq_2")
F32 = jnp.float32
BF16 = jnp.bfloat16
VMEM = pltpu.VMEM


def dot(left, right):
    return jnp.dot(left, right, preferred_element_type=F32)


def dot_nt(left, right):
    return lax.dot_general(left, right, (((1,), (1,)), ((), ())), preferred_element_type=F32)


def dot_tn(left, right):
    return lax.dot_general(left, right, (((0,), (0,)), ((), ())), preferred_element_type=F32)


def dot_exact(left, right):
    return jnp.dot(left, right, preferred_element_type=F32, precision=lax.Precision.HIGHEST)


def lane_iota(shape, dim):
    return lax.broadcasted_iota(jnp.int32, shape, dim)


def spread_matrix(heads, dtype):
    rows = lane_iota((heads, heads * HEAD_DIM), 0)
    cols = lane_iota((heads, heads * HEAD_DIM), 1)
    inside = (cols >= rows * HEAD_DIM) & (cols < (rows + 1) * HEAD_DIM)
    return jnp.where(inside, 1.0, 0.0).astype(dtype)


def gather_matrix(heads, dtype):
    rows = lane_iota((heads * HEAD_DIM, heads), 0)
    cols = lane_iota((heads * HEAD_DIM, heads), 1)
    inside = (rows >= cols * HEAD_DIM) & (rows < (cols + 1) * HEAD_DIM)
    return jnp.where(inside, 1.0, 0.0).astype(dtype)


def lower_ones(size):
    return jnp.where(lane_iota((size, size), 0) >= lane_iota((size, size), 1), 1.0, 0.0)


def spread(values, matrix):
    high = values.astype(BF16)
    low = (values - high.astype(F32)).astype(BF16)
    return dot(high, matrix) + dot(low, matrix)


MESH = pl.DeviceIdType.MESH
W_ROWS = 48


def around(axis, shift):
    return {axis: lax.rem(lax.axis_index(axis) + shift, 4)}


def remote(source, target, send, recv, device):
    return pltpu.make_async_remote_copy(
        src_ref=source, dst_ref=target, send_sem=send, recv_sem=recv, device_id=device, device_id_type=MESH
    )


class RingSum:
    def __init__(self, axis, part, relay, final, send, recv, base):
        self.axis, self.part, self.relay, self.final = axis, part, relay, final
        self.send, self.recv, self.base = send, recv, base
        me = lax.axis_index(axis)
        self.me = me
        self.ahead, self.behind, self.across = (lax.rem(me + k, 4) for k in (1, 3, 2))
        self.up, self.down = around(axis, 1), around(axis, 3)
        self.copies = {}

    def copy(self, n, source, target, device):
        at = self.base + n
        self.copies[n] = remote(source, target, self.send(at), self.recv(at), device)
        self.copies[n].start()

    def first(self):
        self.copy(0, self.part(self.across, 0), self.relay(0), self.up)
        self.copy(1, self.part(self.across, 1), self.relay(1), self.down)
        self.copy(2, self.part(self.ahead, 1), self.final(0, 1), self.up)
        self.copy(3, self.part(self.behind, 0), self.final(1, 0), self.down)

    def second(self):
        self.copies[0].wait_recv()
        ahead = self.part(self.ahead, 0)
        ahead[...] += self.relay(0)[...]
        self.copy(4, ahead, self.final(0, 0), self.up)
        self.copies[1].wait_recv()
        behind = self.part(self.behind, 1)
        behind[...] += self.relay(1)[...]
        self.copy(5, behind, self.final(1, 1), self.down)

    def result(self, half):
        (self.copies[4] if half == 0 else self.copies[2]).wait_recv()
        (self.copies[3] if half == 0 else self.copies[5]).wait_recv()
        return self.part(self.me, half)[...] + self.final(0, half)[...] + self.final(1, half)[...]

    def drain(self):
        for copy in self.copies.values():
            copy.wait_send()


class PlaneSum:
    def __init__(self, first_axis, second_axis, swap, own, relay, final, mid, relay2, final2, send, recv, store):
        rows = mid.shape[1]
        self.store, self.mid, self.rows = store, mid, rows

        def part(d, half):
            pair = pl.ds(2 * half, 2)
            return own.at[pair, d] if swap else own.at[d, pair]

        def part2(d, half):
            return mid.at[d, pl.ds(half * (rows // 2), rows // 2)]

        self.one = RingSum(first_axis, part, lambda h: relay.at[h], lambda w, h: final.at[w, pl.ds(2 * h, 2)],
                           send, recv, 0)
        self.two = RingSum(second_axis, part2, lambda h: relay2.at[h],
                           lambda w, h: final2.at[w, pl.ds(h * (rows // 2), rows // 2)], send, recv, 6)

    def run(self, stage):
        if stage == 0:
            self.one.first()
        elif stage == 1:
            self.one.second()
        elif stage == 2:
            for half in range(2):
                self.mid[pl.ds(2 * half, 2)] = self.one.result(half)
            self.two.first()
        elif stage == 3:
            self.two.second()
        elif stage == 4:
            for half in range(2):
                self.store(half, self.two.result(half))

    def drain(self):
        self.one.drain()
        self.two.drain()


STRIP = 64


def scalars(raw_ref, bias_ref, log_ref, dt_ref, slope_ref, a_ref):
    shifted = raw_ref[...] + bias_ref[...]
    small = jnp.exp(-jnp.abs(shifted))
    one = 1.0 + small
    log_one = jnp.where(one == 1.0, small, jnp.log(one) * small / jnp.where(one == 1.0, 1.0, one - 1.0))
    dt = jnp.maximum(shifted, 0.0) + log_one
    dt_ref[...] = dt
    slope_ref[...] = jnp.where(shifted >= 0.0, 1.0, small) / one
    a_ref[...] = dt * -jnp.exp(log_ref[...])


def states(x, dy, b_ref, c_ref, dt_ref, slope_ref, a_ref, within_ref, last_ref, cols_ref, rows_ref, cross_ref,
           decay_ref, spread_ref, parts, ends):
    tokens, heads = dt_ref.shape
    groups = tokens // GROUP
    width = heads * HEAD_DIM
    tri = lower_ones(GROUP)
    spread_m = spread_matrix(heads, BF16)
    spread_ref[...] = spread_m
    spread_e = spread_matrix(heads, F32)
    block_end = jnp.zeros((1, heads), F32)
    for g in range(groups):
        rows = slice(g * GROUP, (g + 1) * GROUP)
        dt = dt_ref[rows, :]
        sums = dot_exact(tri, jnp.concatenate([a_ref[rows, :], dt, slope_ref[rows, :]], axis=1))
        within = sums[:, 0:heads]
        last = within[GROUP - 1 : GROUP, :]
        block_end = block_end + last
        within_ref[rows, :] = within
        last_ref[g : g + 1, :] = last
        decay = dot_exact(jnp.broadcast_to(jnp.exp(last), (8, heads)), spread_e)[0:1, :]
        decay_ref[g : g + 1, :] = decay
        fall = spread(dt * jnp.exp(last - within), spread_m)
        xw = (x[rows, :].astype(F32) * fall).astype(BF16)
        state = dot_tn(b_ref[rows, :], xw)
        rise = spread(jnp.exp(within), spread_m)
        yw = (dy[rows, :].astype(F32) * rise).astype(BF16)
        grad = dot_tn(c_ref[rows, :], yw)
        if g < groups - 1:
            parts[g] = state
        if g > 0:
            parts[groups - 2 + g] = grad
        if g == 0:
            ends[0:STATE, 0:width] = state
            ends[STATE : 2 * STATE, 0:width] = grad
            gain = decay
        else:
            ends[0:STATE, 0:width] = decay * ends[0:STATE, 0:width] + state
            ends[STATE : 2 * STATE, 0:width] = ends[STATE : 2 * STATE, 0:width] + gain * grad
            gain = gain * decay
        packed = jnp.concatenate([within * LOG2E - jnp.log2(dt), sums[:, heads : 3 * heads]], axis=1)
        cols_ref[rows, :] = packed
        rows_ref[g] = jnp.transpose(jnp.concatenate([within * LOG2E, sums[:, heads : 3 * heads]], axis=1))
        cross_ref[g] = dot_nt(b_ref[rows, :], c_ref[rows, :])
    pad = jnp.concatenate([jnp.exp(block_end), jnp.zeros((1, 128 - heads), F32)], axis=1)
    ends[:, width : width + 128] = jnp.broadcast_to(pad, (2 * STATE, 128))


class Carry:
    def __init__(self, ends, pair, out, got, scanned, back, mine, yours, carry, gains, core_sems, sems):
        self.ends, self.pair, self.out, self.got, self.scanned = ends, pair, out, got, scanned
        self.back, self.mine, self.yours, self.carry, self.gains = back, mine, yours, carry, gains
        self.core_sems, self.sems = core_sems, sems
        self.core = lax.axis_index("seq_2")
        self.other = {"seq_2": 1 - self.core}
        self.me = lax.axis_index("seq_0") * 4 + lax.axis_index("seq_1")
        self.width = carry.shape[1]
        self.heads = self.width // HEAD_DIM

    def own_rows(self, kind, core):
        return pl.ds(pl.multiple_of(kind * STATE + core * (STATE // 2), STATE // 2), STATE // 2)

    def chip(self, offset):
        index = lax.rem(self.me + offset, 16)
        return index, {"seq_0": index // 4, "seq_1": lax.rem(index, 4)}

    def give_pair(self):
        self.pair_copies = []
        for kind in range(2):
            copy = remote(self.ends.at[self.own_rows(kind, 1 - self.core)], self.pair.at[kind],
                          self.core_sems.at[0, kind], self.core_sems.at[1, kind], self.other)
            copy.start()
            self.pair_copies.append(copy)

    def both(self, kind):
        own = self.ends[self.own_rows(kind, self.core), 0 : self.width]
        other = self.pair[kind, :, 0 : self.width]
        first = self.core == 0
        return jnp.where(first, own, other), jnp.where(first, other, own)

    def gains_of(self, tile):
        return dot_exact(tile[:, 0 : self.heads], spread_matrix(self.heads, F32))

    def give_chips(self):
        width, heads = self.width, self.heads
        half = STATE // 2
        for copy in self.pair_copies:
            copy.wait_recv()
        mine, theirs = self.ends[0:8, width : width + 128], self.pair[0, 0:8, width : width + 128]
        first = self.core == 0
        tile0, tile1 = jnp.where(first, mine, theirs), jnp.where(first, theirs, mine)
        self.gains[0:8, :] = self.gains_of(tile0)
        self.gains[8:16, :] = self.gains_of(tile1)
        s0, s1 = self.both(0)
        chip_s = self.gains[8:9, :] * s0 + s1
        self.out[0:8, :, 0:width] = chip_s.reshape(8, 8, width)
        g0, g1 = self.both(1)
        chip_g = g0 + self.gains[0:1, :] * g1
        self.out[8:16, :, 0:width] = chip_g.reshape(8, 8, width)
        self.out[:, :, width : width + 128] = jnp.broadcast_to((tile0 * tile1)[None], (16, 8, 128))
        self.got[0] = self.out[self.me]
        self.copies = []
        for k in range(1, 16):
            index, device = self.chip(k)
            copy = remote(self.out.at[index], self.got.at[k], self.sems.at[0, k], self.sems.at[1, k], device)
            copy.start()
            self.copies.append(copy)

    def scan(self):
        width = self.width
        for copy in self.copies:
            copy.wait_recv()
        self.gains[16:32, :] = self.gains_of(self.got[:, 0, width : width + 128])
        backward = self.me >= 8

        def step(i, running):
            chip = jnp.where(backward, 15 - i, i)
            slot = lax.rem(self.me - chip + 16, 16)
            self.scanned[slot] = running
            return self.gains[pl.ds(16 + slot, 1), :] * running + self.got[slot, :, 0:width]

        lax.fori_loop(0, 16, step, jnp.zeros((8, width), F32))
        self.back[self.me] = self.scanned[0]
        self.back_copies = []
        for k in range(1, 16):
            index, device = self.chip(16 - k)
            copy = remote(self.scanned.at[k], self.back.at[self.me], self.sems.at[2, k], self.sems.at[3, k], device)
            copy.start()
            self.back_copies.append(copy)

    def give_back(self):
        width = self.width
        half = STATE // 2
        for copy in self.back_copies:
            copy.wait_recv()
        first = self.core == 0
        s_in = self.back[0:8].reshape(half, width)
        s0, _ = self.both(0)
        s_next = self.gains[0:1, :] * s_in + s0
        self.carry[self.own_rows(0, self.core), :] = jnp.where(first, s_in, s_next)
        self.mine[0] = jnp.where(first, s_next, s_in)
        g_in = self.back[8:16].reshape(half, width)
        _, g1 = self.both(1)
        g_before = g1 + self.gains[8:9, :] * g_in
        self.carry[self.own_rows(1, self.core), :] = jnp.where(first, g_before, g_in)
        self.mine[1] = jnp.where(first, g_in, g_before)
        self.last = remote(self.mine, self.yours, self.core_sems.at[0, 2], self.core_sems.at[1, 2], self.other)
        self.last.start()

    def finish(self):
        self.last.wait_recv()
        for kind in range(2):
            self.carry[self.own_rows(kind, 1 - self.core), :] = self.yours[kind]

    def drain(self):
        for copy in self.pair_copies + self.copies + self.back_copies + [self.last]:
            copy.wait_send()


def intra(j, x, dy, cols_ref, rows_ref, cross_ref, v_ref, mix_ref, gi, flow_ref, heads):
    half = GROUP // 2

    def group(g, unused):
        at = pl.multiple_of(g * GROUP, GROUP)
        for pair in range(2 * j, 2 * j + 2):
            zs, sides = [], []
            for sub in range(2):
                h = 2 * pair + sub
                lanes = slice(h * HEAD_DIM, (h + 1) * HEAD_DIM)
                x_h = x[pl.ds(at, GROUP), lanes]
                dy_h = dy[pl.ds(at, GROUP), lanes]
                top = dot_nt(x_h[0:half], dy_h)
                low = dot_nt(x_h[half:GROUP], dy_h[half:GROUP])
                acc = [jnp.zeros((8, GROUP), F32) for _ in range(3)]
                z_strips = []
                for k in range(GROUP // STRIP):
                    first = (k * STRIP // half) * half
                    wide = GROUP - first
                    rows = slice(k * STRIP, (k + 1) * STRIP)
                    here = pl.ds(at + k * STRIP, STRIP)
                    gap = rows_ref[g, h : h + 1, first:GROUP] - cols_ref[here, h : h + 1]
                    reach = lane_iota((STRIP, wide), 1) + first >= lane_iota((STRIP, wide), 0) + k * STRIP
                    decay = jnp.where(reach, jnp.exp2(gap), 0.0)
                    bc = cross_ref[g, rows, first:GROUP]
                    mix_ref[sub, rows, first:GROUP] = (decay * bc).astype(BF16)
                    z = decay * (top[rows, :] if first == 0 else low[k * STRIP - half : (k + 1) * STRIP - half, :])
                    z_strips.append(z)
                    box = z * bc
                    w_dt = cols_ref[here, heads + h : heads + h + 1]
                    w_sl = cols_ref[here, 2 * heads + h : 2 * heads + h + 1]
                    for n, term in enumerate((box, box * w_dt, box * w_sl)):
                        part = jnp.sum(term.reshape(STRIP // 8, 8, wide), axis=0)
                        if first > 0:
                            acc[n] = jnp.concatenate([acc[n][:, 0:first], acc[n][:, first:GROUP] + part], axis=1)
                        else:
                            acc[n] = acc[n] + part
                zs.append(z_strips)
                sides.append(dot(mix_ref[sub], dy_h))
                flow_dt = acc[0] * rows_ref[g, heads + h : heads + h + 1, :] - acc[1]
                flow_sl = acc[0] * rows_ref[g, 2 * heads + h : 2 * heads + h + 1, :] - acc[2]
                flow_ref[g, h : h + 1, :] = jnp.sum(flow_dt, axis=0, keepdims=True)
                flow_ref[g, heads + h : heads + h + 1, :] = jnp.sum(flow_sl, axis=0, keepdims=True)
            for k in range(GROUP // STRIP):
                first = (k * STRIP // half) * half
                rows = slice(k * STRIP, (k + 1) * STRIP)
                both = zs[0][k] + zs[1][k]
                if pair == 0:
                    v_ref[g, rows, first:GROUP] = both
                else:
                    v_ref[g, rows, first:GROUP] += both
            gi[pl.ds(at, GROUP), pair * 128 : (pair + 1) * 128] = jnp.concatenate(sides, axis=1).astype(BF16)
        return unused

    lax.fori_loop(0, x.shape[0] // GROUP, group, 0)


def combine(j, x, dy, b_ref, c_ref, dt_ref, within_ref, last_ref, decay_ref, spread_ref, skip_ref, parts, carry,
            sp_ref, gp_ref, dx, dbc, sums_ref, inner_ref):
    tokens, heads = dt_ref.shape
    groups = tokens // GROUP
    cols = slice(j * 256, (j + 1) * 256)
    sp_ref[0] = carry[0:STATE, cols]
    gp_ref[groups - 1] = carry[STATE : 2 * STATE, cols]
    for g in range(groups - 1):
        sp_ref[g + 1] = decay_ref[g : g + 1, cols] * sp_ref[g] + parts[g, :, cols]
    for g in range(groups - 1, 0, -1):
        gp_ref[g - 1] = parts[groups - 2 + g, :, cols] + decay_ref[g : g + 1, cols] * gp_ref[g]
    spread_m = spread_ref[:, cols]
    head = (lane_iota((256, 128), 0) + j * 256) // HEAD_DIM
    lane = lane_iota((256, 128), 1)

    def gather(k):
        return jnp.where(lane == head + k * heads, 1.0, 0.0).astype(BF16)

    for g in range(groups):
        rows = slice(g * GROUP, (g + 1) * GROUP)
        within = within_ref[rows, :]
        fall = spread(dt_ref[rows, :] * jnp.exp(last_ref[g : g + 1, :] - within), spread_m)
        rise = spread(jnp.exp(within), spread_m)
        xs = x[rows, cols].astype(F32)
        dys = dy[rows, cols].astype(F32)
        sp = sp_ref[g]
        gp = gp_ref[g]
        inner_ref[g : g + 1, cols] = jnp.sum(sp * gp, axis=0, keepdims=True)
        sp_low = sp.astype(BF16)
        gp_low = gp.astype(BF16)
        from_end = dot(b_ref[rows, :], gp_low)
        from_start = dot(c_ref[rows, :], sp_low)
        raw = dx[rows, cols].astype(F32) + fall * from_end
        total = dot((xs * raw).astype(BF16), gather(0))
        total += dot((xs * from_end).astype(BF16), gather(1))
        total += dot((xs * dys).astype(BF16), gather(2))
        total += dot((dys * from_start).astype(BF16), gather(3))
        dx[rows, cols] = (raw + skip_ref[:, cols] * dys).astype(BF16)
        d_b = dot_nt((xs * fall).astype(BF16), gp_low)
        d_c = dot_nt((dys * rise).astype(BF16), sp_low)
        if j == 0:
            sums_ref[rows, :] = total
            dbc[rows, 0:STATE] = d_b
            dbc[rows, STATE : 2 * STATE] = d_c
        else:
            sums_ref[rows, :] += total
            dbc[rows, 0:STATE] += d_b
            dbc[rows, STATE : 2 * STATE] += d_c


def mixed_grads(b_ref, c_ref, v_ref, dbc, packed):
    groups = v_ref.shape[0]
    for g in range(groups):
        rows = slice(g * GROUP, (g + 1) * GROUP)
        mixed = v_ref[g].astype(BF16)
        grads = (dbc[rows, 0:STATE] + dot(mixed, c_ref[rows, :]),
                 dbc[rows, STATE : 2 * STATE] + dot_tn(mixed, b_ref[rows, :]))
        for piece in range(GROUP // 128):
            at = g * (GROUP // 128) + piece
            side, base = divmod(at * 128, packed.shape[1])
            for m in range(packed.shape[0]):
                source, left = divmod(m * 64, STATE)
                packed[m, base : base + 128, side * 64 : side * 64 + 64] = grads[source][
                    piece * 128 : (piece + 1) * 128, left : left + 64
                ]


def statistics(dt_ref, slope_ref, log_ref, within_ref, last_ref, cols_ref, sums_ref, inner_ref, flow_ref, stat_ref):
    tokens, heads = dt_ref.shape
    groups = tokens // GROUP
    gather_e = gather_matrix(heads, F32)
    rate = -jnp.exp(log_ref[...])
    flow_dt = jnp.zeros((1, heads), F32)
    flow_sl = jnp.zeros((1, heads), F32)
    bias = jnp.zeros((1, heads), F32)
    skips = jnp.zeros((1, heads), F32)
    inner = dot_exact(inner_ref[...], gather_e)
    for g in range(groups):
        rows = slice(g * GROUP, (g + 1) * GROUP)
        dt = dt_ref[rows, :]
        within = within_ref[rows, :]
        last = last_ref[g : g + 1, :]
        back = jnp.exp(within) * sums_ref[rows, 3 * heads : 4 * heads]
        fore = dt * jnp.exp(last - within) * sums_ref[rows, heads : 2 * heads]
        meet = jnp.exp(last) * inner[g : g + 1, :]
        for which in range(2):
            sums = cols_ref[rows, (which + 1) * heads : (which + 2) * heads]
            whole = sums[GROUP - 1 : GROUP, :]
            flow = jnp.sum(back * sums + fore * (whole - sums), axis=0, keepdims=True) + meet * whole
            if which == 0:
                flow_dt += flow
            else:
                flow_sl += flow
        bias += jnp.sum(slope_ref[rows, :] / dt * sums_ref[rows, 0:heads], axis=0, keepdims=True)
        skips += jnp.sum(sums_ref[rows, 2 * heads : 3 * heads], axis=0, keepdims=True)
    flows = flow_ref[0]
    for g in range(1, groups):
        flows = flows + flow_ref[g]
    totals = jnp.transpose(jnp.sum(flows, axis=1, keepdims=True) + jnp.zeros((2 * heads, 128), F32))[0:1, :]
    stat_ref[...] = jnp.zeros_like(stat_ref)
    stat_ref[0:1, 0:heads] = rate * (flow_dt + totals[:, 0:heads])
    stat_ref[1:2, 0:heads] = bias + rate * (flow_sl + totals[:, heads : 2 * heads])
    stat_ref[2:3, 0:heads] = skips


def flip(li, lt, block):
    def group(g, unused):
        at = pl.multiple_of(g * GROUP, GROUP)
        wide = 8 * block
        for q in range(li.shape[1] // wide):
            turned = jnp.transpose(li[pl.ds(at, GROUP), q * wide : (q + 1) * wide])
            for k in range(8):
                n = q * 8 + k
                lt[n % 2, (n // 2) * block : (n // 2 + 1) * block, pl.ds(at, GROUP)] = turned[
                    k * block : (k + 1) * block, :
                ]
        return unused

    lax.fori_loop(0, li.shape[0] // GROUP, group, 0)


def whole_kernel(refs_in, refs_out, s):
    x_hbm, dy_hbm, li_hbm, b_ref, c_ref, raw_ref, bias_ref, log_ref, skip_ref = refs_in
    wx_ref, wbc_ref, total_ref = refs_out
    block = wx_ref.shape[0]
    heads = raw_ref.shape[1]
    x, dy, li, dx, lt = s["x"], s["dy"], s["li"], s["dx"], s["lt"]
    work, got_sems = s["work"], s["core_sems"]
    chunks = work.shape[1]
    core = lax.axis_index("seq_2")
    mp = lax.axis_index("mp")
    other = {"seq_2": 1 - core}

    loads = []
    for n, (source, target) in enumerate(((x_hbm, x), (dy_hbm, dy), (li_hbm, li))):
        load = pltpu.make_async_copy(source, target, s["load_sems"].at[n])
        load.start()
        loads.append(load)

    carry = Carry(s["ends"], s["pair"], s["out"], s["got"], s["scanned"], s["back"], s["mine"], s["yours"],
                  s["carry"], s["gains"], s["pair_sems"], s["chip_sems"])
    partners = [other] + [carry.chip(k)[1] for k in range(1, 16)] + [around("mp", k) for k in (1, 2, 3)]
    barrier = pltpu.get_barrier_semaphore()
    for partner in partners:
        pl.semaphore_signal(barrier, inc=1, device_id=partner, device_id_type=MESH)

    scalars(raw_ref, bias_ref, log_ref, s["dt"], s["slope"], s["a"])
    s["mix"][:, GROUP // 2 : GROUP, 0 : GROUP // 2] = jnp.zeros((2, GROUP // 2, GROUP // 2), BF16)
    s["v"][:, GROUP // 2 : GROUP, 0 : GROUP // 2] = jnp.zeros((s["v"].shape[0], GROUP // 2, GROUP // 2), F32)
    s["inner"][...] = jnp.zeros_like(s["inner"])
    loads[0].wait()
    loads[1].wait()
    states(x, dy, b_ref, c_ref, s["dt"], s["slope"], s["a"], s["within"], s["last"], s["cols"], s["rows"],
           s["cross"], s["decay"], s["spread"], s["parts"], s["ends"])
    pl.semaphore_wait(barrier, len(partners))
    carry.give_pair()

    def intra_part(j):
        intra(j, x, dy, s["cols"], s["rows"], s["cross"], s["v"], s["mix"], dx, s["flow"], heads)

    def combine_part(j):
        combine(j, x, dy, b_ref, c_ref, s["dt"], s["within"], s["last"], s["decay"], s["spread"], skip_ref,
                s["parts"], s["carry"], s["sp"], s["gp"], dx, s["dbc"], s["sums"], s["inner"])

    carry.give_chips()
    loads[2].wait()
    flip(li, lt, block)
    intra_part(0)
    carry.scan()
    for j in range(1, min(3, chunks)):
        intra_part(j)
    carry.give_back()
    carry.finish()

    send_own, got, own = (work.at[i] for i in range(3))
    core_copies = {}

    def give(j):
        cols = dx[:, j * 256 : (j + 1) * 256]

        def body(i, unused):
            start = pl.multiple_of(i * 4 * block, 16)
            res = dot(lt[1 - core, pl.ds(start, 4 * block), :], cols)
            for side in range(2):
                send_own[j, side, i] = res[:, side * 128 : (side + 1) * 128].reshape(4, block, 128)
            return unused

        lax.fori_loop(0, 4, body, 0)
        core_copies[j] = remote(send_own.at[j], got.at[j], got_sems.at[0, j], got_sems.at[1, j], other)
        core_copies[j].start()

    def keep(j):
        core_copies[j].wait_recv()
        cols = dx[:, j * 256 : (j + 1) * 256]

        def body(i, unused):
            start = pl.multiple_of(i * 4 * block, 16)
            res = dot(lt[core, pl.ds(start, 4 * block), :], cols)
            for side in range(2):
                own[j, side, i] = got[j, side, i] + res[:, side * 128 : (side + 1) * 128].reshape(4, block, 128)
            return unused

        lax.fori_loop(0, 4, body, 0)

    w_work = s["w_work"]
    dbc_in, packed = s["dbc_in"], s["packed"]

    def narrow(kind, i, cols):
        start = pl.multiple_of(i * 4 * block, 16)
        res = dot(lt[kind, pl.ds(start, 4 * block), :], cols).reshape(4, block, 64)
        grads = jnp.concatenate([res[:, 0 : block // 2], res[:, block // 2 : block]], axis=2)
        stats = jnp.broadcast_to(s["stats"][...][None], (4, 8, 128))
        return jnp.concatenate([grads, stats], axis=1)

    mp_copies = []

    def give_mp():
        mixed_grads(b_ref, c_ref, s["v"], s["dbc"], packed)
        for k in (1, 2, 3):
            target = around("mp", k)
            copy = remote(packed.at[target["mp"]], dbc_in.at[k - 1], s["mp_sems"].at[0, k - 1],
                          s["mp_sems"].at[1, k - 1], target)
            copy.start()
            mp_copies.append(copy)
        statistics(s["dt"], s["slope"], log_ref, s["within"], s["last"], s["cols"], s["sums"], s["inner"],
                   s["flow"], s["stats"])

    def owned_cols():
        for copy in mp_copies:
            copy.wait_recv()
        owned = packed[mp] + dbc_in[0] + dbc_in[1] + dbc_in[2]
        return jnp.concatenate([owned[:, 0:64], owned[:, 64:128]], axis=0).astype(BF16)

    def give_narrow(cols):
        def body(i, unused):
            w_work[0, i] = narrow(1 - core, i, cols)
            return unused

        lax.fori_loop(0, 4, body, 0)
        core_copies[chunks] = remote(
            w_work.at[0], w_work.at[1], got_sems.at[0, chunks], got_sems.at[1, chunks], other
        )
        core_copies[chunks].start()

    def keep_narrow(cols):
        core_copies[chunks].wait_recv()

        def body(i, unused):
            w_work[2, i] = w_work[1, i] + narrow(core, i, cols)
            return unused

        lax.fori_loop(0, 4, body, 0)

    def store_wide(j, side):
        left = j * 256 + side * 128

        def store(half, value):
            wx_ref[half * (block // 2) : (half + 1) * (block // 2), left : left + 128] = value

        return store

    def store_narrow(half, value):
        w_work[0, 0, 0, half * (W_ROWS // 2) : (half + 1) * (W_ROWS // 2)] = value

    send, recv = s["ring_send"], s["ring_recv"]

    def stream(j, side):
        axes = ("seq_0", "seq_1") if side == 0 else ("seq_1", "seq_0")
        n = 2 * j + side
        return PlaneSum(*axes, side == 1, own.at[j, side], s["relay"].at[:, j, side], s["final"].at[:, j, side],
                        s["mid"].at[j, side], s["relay2"].at[:, j, side], s["final2"].at[:, j, side],
                        lambda k: send.at[n, k], lambda k: recv.at[n, k], store_wide(j, side))

    streams = [[stream(j, 0), stream(j, 1)] for j in range(chunks)]
    end = 2 * chunks
    streams.append([PlaneSum("seq_0", "seq_1", False, w_work.at[2], s["w_relay"], s["w_final"], s["w_mid"],
                             s["w_relay2"], s["w_final2"],
                             lambda k: send.at[end, k], lambda k: recv.at[end, k], store_narrow)])

    combine_part(0)
    give(0)
    cols_low = []
    for t in range(chunks + 6):
        if t + 1 < chunks:
            if t + 1 >= 3:
                intra_part(t + 1)
            combine_part(t + 1)
            give(t + 1)
        elif t + 1 == chunks:
            give_mp()
        if t < chunks:
            keep(t)
        if t + 1 == chunks:
            cols_low.append(owned_cols())
            give_narrow(cols_low[0])
        elif t == chunks:
            keep_narrow(cols_low[0])
        for stage in range(5):
            j = t - stage
            if 0 <= j <= chunks:
                if stage == 4 and j == chunks:
                    core_copies[chunks].wait_send()
                for one in streams[j]:
                    one.run(stage)

    half = block // 2
    wbc_ref[0:half, :] = w_work[0, 0, 0, 0:half, 0:64]
    wbc_ref[half:block, :] = w_work[0, 0, 0, 0:half, 64:128]
    total_ref[...] = w_work[0, 0, 0, half : half + 8, :]
    carry.drain()
    for copy in mp_copies:
        copy.wait_send()
    for j in range(chunks):
        core_copies[j].wait_send()
    for group in streams:
        for one in group:
            one.drain()


def scratch(tokens, heads, block, wide):
    width = heads * HEAD_DIM
    chunks = width // 256
    groups = tokens // GROUP
    half = STATE // 2
    dma = pltpu.SemaphoreType.DMA
    return {
        "x": VMEM((tokens, width), BF16), "dy": VMEM((tokens, width), BF16), "li": VMEM((tokens, wide), BF16),
        "dx": VMEM((tokens, width), BF16), "lt": VMEM((2, wide // 2, tokens), BF16),
        "dt": VMEM((tokens, heads), F32), "slope": VMEM((tokens, heads), F32), "a": VMEM((tokens, heads), F32),
        "within": VMEM((tokens, heads), F32), "last": VMEM((8, heads), F32), "cols": VMEM((tokens, 3 * heads), F32),
        "rows": VMEM((groups, 3 * heads, GROUP), F32), "cross": VMEM((groups, GROUP, GROUP), F32),
        "decay": VMEM((8, width), F32), "spread": VMEM((heads, width), BF16),
        "parts": VMEM((2 * groups - 2, STATE, width), F32), "ends": VMEM((2 * STATE, width + 128), F32),
        "pair": VMEM((2, half, width + 128), F32), "out": VMEM((16, 8, width + 128), F32),
        "got": VMEM((16, 8, width + 128), F32), "scanned": VMEM((16, 8, width), F32),
        "back": VMEM((16, 8, width), F32), "mine": VMEM((2, half, width), F32), "yours": VMEM((2, half, width), F32),
        "carry": VMEM((2 * STATE, width), F32), "gains": VMEM((32, width), F32),
        "v": VMEM((groups, GROUP, GROUP), F32), "mix": VMEM((2, GROUP, GROUP), BF16),
        "flow": VMEM((groups, 2 * heads, GROUP), F32), "sp": VMEM((groups, STATE, 256), F32),
        "gp": VMEM((groups, STATE, 256), F32), "dbc": VMEM((tokens, 2 * STATE), F32),
        "sums": VMEM((tokens, 128), F32), "inner": VMEM((8, width), F32), "stats": VMEM((8, 128), F32),
        "packed": VMEM((4, tokens // 2, 128), F32), "dbc_in": VMEM((3, tokens // 2, 128), F32),
        "work": VMEM((3, chunks, 2, 4, 4, block, 128), F32), "relay": VMEM((2, chunks, 2, 2, block, 128), F32),
        "final": VMEM((2, chunks, 2, 4, block, 128), F32), "mid": VMEM((chunks, 2, 4, block, 128), F32),
        "relay2": VMEM((2, chunks, 2, block // 2, 128), F32), "final2": VMEM((2, chunks, 2, block, 128), F32),
        "w_work": VMEM((3, 4, 4, W_ROWS, 128), F32), "w_relay": VMEM((2, 2, W_ROWS, 128), F32),
        "w_final": VMEM((2, 4, W_ROWS, 128), F32), "w_mid": VMEM((4, W_ROWS, 128), F32),
        "w_relay2": VMEM((2, W_ROWS // 2, 128), F32), "w_final2": VMEM((2, W_ROWS, 128), F32),
        "load_sems": dma((3,)), "pair_sems": dma((2, 3)), "chip_sems": dma((4, 16)),
        "core_sems": dma((2, chunks + 1)), "mp_sems": dma((2, 3)),
        "ring_send": dma((2 * chunks + 1, 12)), "ring_recv": dma((2 * chunks + 1, 12)),
    }


def on_device(layer_in, ssm_input, b_matrix, c_matrix, dt_raw, dt_bias, a_log, d_skip, grad_out):
    tokens, heads = dt_raw.shape
    wide = layer_in.shape[1]
    width = heads * HEAD_DIM
    block = wide // math.prod(lax.axis_size(axis) for axis in SEQ)
    sds = jax.ShapeDtypeStruct
    shapes = scratch(tokens, heads, block, wide)

    def kernel(*refs):
        whole_kernel(refs[:9], refs[9:12], dict(zip(shapes, refs[12:])))

    anywhere, local = pl.BlockSpec(memory_space=pl.ANY), pl.BlockSpec(memory_space=VMEM)
    grad_wx, grad_wbc, totals = pl.pallas_call(
        kernel,
        out_shape=(sds((block, width), F32), sds((block, 64), F32), sds((8, 128), F32)),
        in_specs=[anywhere] * 3 + [local] * 6,
        out_specs=(local,) * 3,
        scratch_shapes=list(shapes.values()),
        name="whole",
        cost_estimate=pl.CostEstimate(flops=4 * 10**10, bytes_accessed=10**7, transcendentals=0),
        compiler_params=pltpu.CompilerParams(
            collective_id=0, has_side_effects=True, vmem_limit_bytes=67043328
        ),
    )(ssm_input, grad_out, layer_in, b_matrix, c_matrix, dt_raw, dt_bias[None, :], a_log[None, :],
      jnp.repeat(d_skip, HEAD_DIM)[None, :])
    return (grad_wx, grad_wbc, totals[0, :heads], totals[1, :heads], totals[2, :heads])


def solution(mesh):
    n_seq, n_mp = mesh.shape["seq"], mesh.shape["mp"]
    split = Mesh(mesh.devices.reshape(n_seq // 8, 4, 2, n_mp), SEQ + ("mp",))
    in_specs = (
        P(SEQ, None),
        P(SEQ, "mp"),
        P(SEQ, None),
        P(SEQ, None),
        P(SEQ, "mp"),
        P("mp"),
        P("mp"),
        P("mp"),
        P(SEQ, "mp"),
    )
    out_specs = (P(SEQ, "mp"), P(SEQ, "mp"), P("mp"), P("mp"), P("mp"))
    return jax.shard_map(
        on_device, mesh=split, in_specs=in_specs, out_specs=out_specs, check_vma=False
    )
```

time: 161 us -> 119 us (0.74)
  waiting for transfers between devices: 21.4 us -> 0 us
  starting transfers between devices: 12.2 us -> 0 us
  local copies, waits for them, and re-layouts: 14.8 us -> 7.77 us
  other arithmetic: 3.1 us -> 0 us
  Pallas kernels: 108 us -> 110 us
    all_to_all x2 -> x0, waiting for transfers between devices: 21.4 us -> none  [the longest x1 21.4 us: on_device(): got = lax.all_to_all(sent, SEQ, split_axis=0, concat_axis=0, tiled=True)]
    all_to_all x2 -> x0, starting transfers between devices: 12.2 us -> none  [the longest x1 8.27 us: on_device(): got = lax.all_to_all(sent, SEQ, split_axis=0, concat_axis=0, tiled=True)]
    unnamed x10 -> x3, local copies, waits for them, and re-layouts: 12.8 us -> 5.06 us
    pallas_call x5 -> x1, Pallas kernels: 108 us -> 110 us  [on_device(): pl.pallas_call(kernel, out_shape=(sds((block, width), F32), sds((block, 6...]
    mul x1 -> x0, other arithmetic: 1.92 us -> none  [on_device(): log_step = dt * rate[None, :]]
  transfers between devices with their start and end apart: 2 -> 0, of which waited for: 1 -> 0; matrix products, arithmetic and copies ran while one was open for 4% -> 0% of each run, Pallas kernels for 11% -> 0%
where the time goes in v3:
time: 119 us
  Pallas kernels  110 us (92%)
  local copies, waits for them, and re-layouts  7.77 us (7%)
    pallas_call x1, Pallas kernels, on_device(): pl.pallas_call(kernel, out_shape=(sds((block, width), F32), sds((block, 6...  110 us
    unnamed x3, local copies, waits for them, and re-layouts  5.06 us

profile of v3, /device:TPU:0, one launch (start us, length us, event | category | flops | bytes accessed | tf_op | source)
XLA Modules:
  0.0 118.9 jit_solution(14222343840404745246)
XLA Ops:
  0.6 1.8 %copy.14.refs_5_ = f32[768,20]{1,0:T(8,128)} copy(f32[768,20]{0,1:T(8,128)} %param.13) | data formatting | bytes 122880 | tf_op args[4]
  2.4 0.7 broadcast_in_dim.11
  3.2 0.7 broadcast_in_dim_reshape.3.refs_8_
  3.8 110.5 %whole.1 = (f32[80,1280]{1,0:T(8,128)}, f32[80,64]{1,0:T(8,128)}, f32[8,128]{1,0:T(8,128)}) custom-call(bf16[768,1280]{1,0:T(8,128)(2,1)} %refs_0_.1, bf16[768,1280]{1,0:T(8,128)(2,1)} %refs_1_.1, bf16[768,2560]{1,0:T(8,128)(2,1)} %refs_2_.1, bf16[768,128]{1,0:T(8,128)(2,1)} %refs_3_.1, bf16[768,128]{1,0:T(8,128)(2,1)} %refs_4_.1, f32[768,20]{1,0:T(8,128)} %copy.14.refs_5_, ...), custom_call_target="tpu_custom_call" | custom-call | flops 40000000000 | bytes 10000000 | tf_op jit(solution)/shard_map/whole/pallas_call | solution.py:753
  114.3 1.3 %slice_bitcast_fusion = (f32[20]{0:T(128)}, f32[20]{0:T(128)}, f32[20]{0:T(128)}) fusion(f32[8,128]{1,0:T(8,128)} %get-tuple-element.10), kind=kLoop, calls=%fused_computation | loop fusion | bytes 480 | tf_op jit(solution)/shard_map/squeeze | solution.py:766
  115.7 1.5 %copy.15 = f32[80,64]{0,1:T(8,128)} copy(f32[80,64]{1,0:T(8,128)} %get-tuple-element.12) | data formatting | bytes 40960
  117.1 1.8 %copy.17 = f32[80,1280]{1,0:T(8,128)} copy(f32[80,1280]{1,0:T(8,128)} %get-tuple-element.24) | data formatting | bytes 819200

commit v4 on v3

--- a/solution.py
+++ b/solution.py
@@ -159,7 +159,7 @@
 
 
 def scalars(raw_ref, bias_ref, log_ref, dt_ref, slope_ref, a_ref):
-    shifted = raw_ref[...] + bias_ref[...]
+    shifted = jnp.transpose(raw_ref[...]) + bias_ref[...]
     small = jnp.exp(-jnp.abs(shifted))
     one = 1.0 + small
     log_one = jnp.where(one == 1.0, small, jnp.log(one) * small / jnp.where(one == 1.0, 1.0, one - 1.0))
@@ -170,7 +170,7 @@
 
 
 def states(x, dy, b_ref, c_ref, dt_ref, slope_ref, a_ref, within_ref, last_ref, cols_ref, rows_ref, cross_ref,
-           decay_ref, spread_ref, parts, ends):
+           decay_ref, spread_ref, parts, ends, tile, skip_ref, skip_wide):
     tokens, heads = dt_ref.shape
     groups = tokens // GROUP
     width = heads * HEAD_DIM
@@ -178,6 +178,7 @@
     spread_m = spread_matrix(heads, BF16)
     spread_ref[...] = spread_m
     spread_e = spread_matrix(heads, F32)
+    skip_wide[...] = dot_exact(jnp.broadcast_to(skip_ref[...], (8, heads)), spread_e)
     block_end = jnp.zeros((1, heads), F32)
     for g in range(groups):
         rows = slice(g * GROUP, (g + 1) * GROUP)
@@ -213,61 +214,84 @@
         rows_ref[g] = jnp.transpose(jnp.concatenate([within * LOG2E, sums[:, heads : 3 * heads]], axis=1))
         cross_ref[g] = dot_nt(b_ref[rows, :], c_ref[rows, :])
     pad = jnp.concatenate([jnp.exp(block_end), jnp.zeros((1, 128 - heads), F32)], axis=1)
-    ends[:, width : width + 128] = jnp.broadcast_to(pad, (2 * STATE, 128))
-
-
-class Carry:
-    def __init__(self, ends, pair, out, got, scanned, back, mine, yours, carry, gains, core_sems, sems):
-        self.ends, self.pair, self.out, self.got, self.scanned = ends, pair, out, got, scanned
-        self.back, self.mine, self.yours, self.carry, self.gains = back, mine, yours, carry, gains
-        self.core_sems, self.sems = core_sems, sems
+    tile[...] = jnp.broadcast_to(pad, (8, 128))
+
+
+class Decays:
+    def __init__(self, tile, pair, chip_tile, got, gains, heads, sems):
+        self.tile, self.pair, self.chip_tile, self.got, self.gains = tile, pair, chip_tile, got, gains
+        self.heads, self.sems = heads, sems
         self.core = lax.axis_index("seq_2")
-        self.other = {"seq_2": 1 - self.core}
         self.me = lax.axis_index("seq_0") * 4 + lax.axis_index("seq_1")
-        self.width = carry.shape[1]
-        self.heads = self.width // HEAD_DIM
-
-    def own_rows(self, kind, core):
-        return pl.ds(pl.multiple_of(kind * STATE + core * (STATE // 2), STATE // 2), STATE // 2)
 
     def chip(self, offset):
         index = lax.rem(self.me + offset, 16)
         return index, {"seq_0": index // 4, "seq_1": lax.rem(index, 4)}
 
+    def spread_rows(self, tile):
+        return dot_exact(tile[:, 0 : self.heads], spread_matrix(self.heads, F32))
+
+    def give_pair(self):
+        self.copies = [remote(self.tile, self.pair, self.sems.at[0, 0], self.sems.at[1, 0], {"seq_2": 1 - self.core})]
+        self.copies[0].start()
+
+    def give_chips(self):
+        self.copies[0].wait_recv()
+        first = self.core == 0
+        mine, theirs = self.tile[...], self.pair[...]
+        tile0, tile1 = jnp.where(first, mine, theirs), jnp.where(first, theirs, mine)
+        self.chip_tile[...] = tile0 * tile1
+        self.got[0] = tile0 * tile1
+        for k in range(1, 16):
+            copy = remote(self.chip_tile, self.got.at[k], self.sems.at[0, k], self.sems.at[1, k], self.chip(k)[1])
+            copy.start()
+            self.copies.append(copy)
+        self.gains[0:8, :] = self.spread_rows(tile0)
+        self.gains[8:16, :] = self.spread_rows(tile1)
+
+    def take(self):
+        for copy in self.copies[1:]:
+            copy.wait_recv()
+        self.gains[16:32, :] = self.spread_rows(self.got[:, 0, :])
+
+
+class Carry:
+    def __init__(self, decays, left, ends, carry, pair, out, got, scanned, back, mine, yours, core_sems, sems):
+        self.ends, self.pair, self.out, self.got, self.scanned = ends, pair, out, got, scanned
+        self.back, self.mine, self.yours, self.carry, self.gains = back, mine, yours, carry, decays.gains
+        self.core_sems, self.sems, self.decays = core_sems, sems, decays
+        self.core, self.me, self.chip = decays.core, decays.me, decays.chip
+        self.other = {"seq_2": 1 - self.core}
+        self.width = out.shape[2]
+        self.cols = pl.ds(left, self.width)
+
+    def own_rows(self, kind, core):
+        return pl.ds(pl.multiple_of(kind * STATE + core * (STATE // 2), STATE // 2), STATE // 2)
+
+    def gain(self, row):
+        return self.gains[pl.ds(row, 1), self.cols]
+
     def give_pair(self):
         self.pair_copies = []
         for kind in range(2):
-            copy = remote(self.ends.at[self.own_rows(kind, 1 - self.core)], self.pair.at[kind],
+            copy = remote(self.ends.at[self.own_rows(kind, 1 - self.core), self.cols], self.pair.at[kind],
                           self.core_sems.at[0, kind], self.core_sems.at[1, kind], self.other)
             copy.start()
             self.pair_copies.append(copy)
 
     def both(self, kind):
-        own = self.ends[self.own_rows(kind, self.core), 0 : self.width]
-        other = self.pair[kind, :, 0 : self.width]
+        own = self.ends[self.own_rows(kind, self.core), self.cols]
+        other = self.pair[kind]
         first = self.core == 0
         return jnp.where(first, own, other), jnp.where(first, other, own)
 
-    def gains_of(self, tile):
-        return dot_exact(tile[:, 0 : self.heads], spread_matrix(self.heads, F32))
-
     def give_chips(self):
-        width, heads = self.width, self.heads
-        half = STATE // 2
         for copy in self.pair_copies:
             copy.wait_recv()
-        mine, theirs = self.ends[0:8, width : width + 128], self.pair[0, 0:8, width : width + 128]
-        first = self.core == 0
-        tile0, tile1 = jnp.where(first, mine, theirs), jnp.where(first, theirs, mine)
-        self.gains[0:8, :] = self.gains_of(tile0)
-        self.gains[8:16, :] = self.gains_of(tile1)
         s0, s1 = self.both(0)
-        chip_s = self.gains[8:9, :] * s0 + s1
-        self.out[0:8, :, 0:width] = chip_s.reshape(8, 8, width)
+        self.out[0:8] = (self.gain(8) * s0 + s1).reshape(8, 8, self.width)
         g0, g1 = self.both(1)
-        chip_g = g0 + self.gains[0:1, :] * g1
-        self.out[8:16, :, 0:width] = chip_g.reshape(8, 8, width)
-        self.out[:, :, width : width + 128] = jnp.broadcast_to((tile0 * tile1)[None], (16, 8, 128))
+        self.out[8:16] = (g0 + self.gain(0) * g1).reshape(8, 8, self.width)
         self.got[0] = self.out[self.me]
         self.copies = []
         for k in range(1, 16):
@@ -277,19 +301,17 @@
             self.copies.append(copy)
 
     def scan(self):
-        width = self.width
         for copy in self.copies:
             copy.wait_recv()
-        self.gains[16:32, :] = self.gains_of(self.got[:, 0, width : width + 128])
         backward = self.me >= 8
 
         def step(i, running):
             chip = jnp.where(backward, 15 - i, i)
             slot = lax.rem(self.me - chip + 16, 16)
             self.scanned[slot] = running
-            return self.gains[pl.ds(16 + slot, 1), :] * running + self.got[slot, :, 0:width]
-
-        lax.fori_loop(0, 16, step, jnp.zeros((8, width), F32))
+            return self.gain(16 + slot) * running + self.got[slot]
+
+        lax.fori_loop(0, 16, step, jnp.zeros((8, self.width), F32))
         self.back[self.me] = self.scanned[0]
         self.back_copies = []
         for k in range(1, 16):
@@ -299,28 +321,27 @@
             self.back_copies.append(copy)
 
     def give_back(self):
-        width = self.width
         half = STATE // 2
         for copy in self.back_copies:
             copy.wait_recv()
         first = self.core == 0
-        s_in = self.back[0:8].reshape(half, width)
+        s_in = self.back[0:8].reshape(half, self.width)
         s0, _ = self.both(0)
-        s_next = self.gains[0:1, :] * s_in + s0
-        self.carry[self.own_rows(0, self.core), :] = jnp.where(first, s_in, s_next)
+        s_next = self.gain(0) * s_in + s0
         self.mine[0] = jnp.where(first, s_next, s_in)
-        g_in = self.back[8:16].reshape(half, width)
+        g_in = self.back[8:16].reshape(half, self.width)
         _, g1 = self.both(1)
-        g_before = g1 + self.gains[8:9, :] * g_in
-        self.carry[self.own_rows(1, self.core), :] = jnp.where(first, g_before, g_in)
+        g_before = g1 + self.gain(8) * g_in
         self.mine[1] = jnp.where(first, g_in, g_before)
         self.last = remote(self.mine, self.yours, self.core_sems.at[0, 2], self.core_sems.at[1, 2], self.other)
         self.last.start()
+        self.carry[self.own_rows(0, self.core), self.cols] = jnp.where(first, s_in, s_next)
+        self.carry[self.own_rows(1, self.core), self.cols] = jnp.where(first, g_before, g_in)
 
     def finish(self):
         self.last.wait_recv()
         for kind in range(2):
-            self.carry[self.own_rows(kind, 1 - self.core), :] = self.yours[kind]
+            self.carry[self.own_rows(kind, 1 - self.core), self.cols] = self.yours[kind]
 
     def drain(self):
         for copy in self.pair_copies + self.copies + self.back_copies + [self.last]:
@@ -421,7 +442,7 @@
         total += dot((xs * from_end).astype(BF16), gather(1))
         total += dot((xs * dys).astype(BF16), gather(2))
         total += dot((dys * from_start).astype(BF16), gather(3))
-        dx[rows, cols] = (raw + skip_ref[:, cols] * dys).astype(BF16)
+        dx[rows, cols] = (raw + skip_ref[0:1, cols] * dys).astype(BF16)
         d_b = dot_nt((xs * fall).astype(BF16), gp_low)
         d_c = dot_nt((dys * rise).astype(BF16), sp_low)
         if j == 0:
@@ -509,7 +530,7 @@
     x_hbm, dy_hbm, li_hbm, b_ref, c_ref, raw_ref, bias_ref, log_ref, skip_ref = refs_in
     wx_ref, wbc_ref, total_ref = refs_out
     block = wx_ref.shape[0]
-    heads = raw_ref.shape[1]
+    heads = raw_ref.shape[0]
     x, dy, li, dx, lt = s["x"], s["dy"], s["li"], s["dx"], s["lt"]
     work, got_sems = s["work"], s["core_sems"]
     chunks = work.shape[1]
@@ -523,9 +544,12 @@
         load.start()
         loads.append(load)
 
-    carry = Carry(s["ends"], s["pair"], s["out"], s["got"], s["scanned"], s["back"], s["mine"], s["yours"],
-                  s["carry"], s["gains"], s["pair_sems"], s["chip_sems"])
-    partners = [other] + [carry.chip(k)[1] for k in range(1, 16)] + [around("mp", k) for k in (1, 2, 3)]
+    decays = Decays(s["tile"], s["tile_pair"], s["tile_chip"], s["tile_got"], s["gains"], heads, s["tile_sems"])
+    carries = []
+    for n, (left, right) in enumerate(parts_of(heads * HEAD_DIM)):
+        buffers = [s[f"{name}{n}"] for name in ("pair", "out", "got", "scanned", "back", "mine", "yours")]
+        carries.append(Carry(decays, left, s["ends"], s["carry"], *buffers, s["pair_sems"].at[n], s["chip_sems"].at[n]))
+    partners = [other] + [decays.chip(k)[1] for k in range(1, 16)] + [around("mp", k) for k in (1, 2, 3)]
     barrier = pltpu.get_barrier_semaphore()
     for partner in partners:
         pl.semaphore_signal(barrier, inc=1, device_id=partner, device_id_type=MESH)
@@ -537,26 +561,30 @@
     loads[0].wait()
     loads[1].wait()
     states(x, dy, b_ref, c_ref, s["dt"], s["slope"], s["a"], s["within"], s["last"], s["cols"], s["rows"],
-           s["cross"], s["decay"], s["spread"], s["parts"], s["ends"])
+           s["cross"], s["decay"], s["spread"], s["parts"], s["ends"], s["tile"], skip_ref, s["skip"])
     pl.semaphore_wait(barrier, len(partners))
-    carry.give_pair()
+    decays.give_pair()
+    for one in carries:
+        one.give_pair()
 
     def intra_part(j):
         intra(j, x, dy, s["cols"], s["rows"], s["cross"], s["v"], s["mix"], dx, s["flow"], heads)
 
     def combine_part(j):
-        combine(j, x, dy, b_ref, c_ref, s["dt"], s["within"], s["last"], s["decay"], s["spread"], skip_ref,
+        combine(j, x, dy, b_ref, c_ref, s["dt"], s["within"], s["last"], s["decay"], s["spread"], s["skip"],
                 s["parts"], s["carry"], s["sp"], s["gp"], dx, s["dbc"], s["sums"], s["inner"])
 
-    carry.give_chips()
+    decays.give_chips()
+    for one in carries:
+        one.give_chips()
     loads[2].wait()
     flip(li, lt, block)
+    decays.take()
+    carries[0].scan()
     intra_part(0)
-    carry.scan()
-    for j in range(1, min(3, chunks)):
-        intra_part(j)
-    carry.give_back()
-    carry.finish()
+    carries[1].scan()
+    intra_part(1)
+    carries[0].give_back()
 
     send_own, got, own = (work.at[i] for i in range(3))
     core_copies = {}
@@ -608,8 +636,6 @@
                           s["mp_sems"].at[1, k - 1], target)
             copy.start()
             mp_copies.append(copy)
-        statistics(s["dt"], s["slope"], log_ref, s["within"], s["last"], s["cols"], s["sums"], s["inner"],
-                   s["flow"], s["stats"])
 
     def owned_cols():
         for copy in mp_copies:
@@ -663,23 +689,23 @@
                              s["w_relay2"], s["w_final2"],
                              lambda k: send.at[end, k], lambda k: recv.at[end, k], store_narrow)])
 
+    second = parts_of(heads * HEAD_DIM)[1][0] // 256
+    carries[0].finish()
     combine_part(0)
     give(0)
+    carries[1].give_back()
     cols_low = []
-    for t in range(chunks + 6):
+    for t in range(chunks + 5):
         if t + 1 < chunks:
-            if t + 1 >= 3:
+            if t + 1 >= 2:
                 intra_part(t + 1)
+            if t + 1 == second:
+                carries[1].finish()
             combine_part(t + 1)
             give(t + 1)
-        elif t + 1 == chunks:
-            give_mp()
         if t < chunks:
             keep(t)
-        if t + 1 == chunks:
-            cols_low.append(owned_cols())
-            give_narrow(cols_low[0])
-        elif t == chunks:
+        if t == chunks:
             keep_narrow(cols_low[0])
         for stage in range(5):
             j = t - stage
@@ -688,19 +714,50 @@
                     core_copies[chunks].wait_send()
                 for one in streams[j]:
                     one.run(stage)
+        if t == chunks - 2:
+            give_mp()
+        if t == chunks - 1:
+            statistics(s["dt"], s["slope"], log_ref, s["within"], s["last"], s["cols"], s["sums"], s["inner"],
+                       s["flow"], s["stats"])
+            cols_low.append(owned_cols())
+            give_narrow(cols_low[0])
 
     half = block // 2
-    wbc_ref[0:half, :] = w_work[0, 0, 0, 0:half, 0:64]
-    wbc_ref[half:block, :] = w_work[0, 0, 0, 0:half, 64:128]
+    turned = jnp.transpose(w_work[0, 0, 0, 0:half, :])
+    wbc_ref[...] = jnp.concatenate([turned[0:64], turned[64:128]], axis=1)
     total_ref[...] = w_work[0, 0, 0, half : half + 8, :]
-    carry.drain()
-    for copy in mp_copies:
+    for one in carries:
+        one.drain()
+    for copy in decays.copies + mp_copies:
         copy.wait_send()
     for j in range(chunks):
         core_copies[j].wait_send()
     for group in streams:
         for one in group:
             one.drain()
+
+
+def parts_of(width):
+    cut = 2 * 256
+    return ((0, cut), (cut, width))
+
+
+def carry_buffers(width):
+    found = {}
+    for n, (left, right) in enumerate(parts_of(width)):
+        wide = right - left
+        for name in ("out", "got", "scanned", "back"):
+            found[f"{name}{n}"] = VMEM((16, 8, wide), F32)
+        for name in ("pair", "mine", "yours"):
+            found[f"{name}{n}"] = VMEM((2, STATE // 2, wide), F32)
+    return found
+
+
+def finish_kernel(wx_in, wbc_in, totals, wx_ref, wbc_ref, log_ref, bias_ref, skip_ref):
+    wx_ref[...] = wx_in[...]
+    wbc_ref[...] = wbc_in[...]
+    for n, ref in enumerate((log_ref, bias_ref, skip_ref)):
+        ref[...] = totals[n : n + 1, 0 : ref.shape[1]]
 
 
 def scratch(tokens, heads, block, wide):
@@ -716,10 +773,10 @@
         "within": VMEM((tokens, heads), F32), "last": VMEM((8, heads), F32), "cols": VMEM((tokens, 3 * heads), F32),
         "rows": VMEM((groups, 3 * heads, GROUP), F32), "cross": VMEM((groups, GROUP, GROUP), F32),
         "decay": VMEM((8, width), F32), "spread": VMEM((heads, width), BF16),
-        "parts": VMEM((2 * groups - 2, STATE, width), F32), "ends": VMEM((2 * STATE, width + 128), F32),
-        "pair": VMEM((2, half, width + 128), F32), "out": VMEM((16, 8, width + 128), F32),
-        "got": VMEM((16, 8, width + 128), F32), "scanned": VMEM((16, 8, width), F32),
-        "back": VMEM((16, 8, width), F32), "mine": VMEM((2, half, width), F32), "yours": VMEM((2, half, width), F32),
+        "parts": VMEM((2 * groups - 2, STATE, width), F32), "ends": VMEM((2 * STATE, width), F32),
+        **carry_buffers(width), "tile": VMEM((8, 128), F32), "tile_pair": VMEM((8, 128), F32),
+        "tile_chip": VMEM((8, 128), F32), "tile_got": VMEM((16, 8, 128), F32), "skip": VMEM((8, width), F32),
+        "tile_sems": dma((2, 16)),
         "carry": VMEM((2 * STATE, width), F32), "gains": VMEM((32, width), F32),
         "v": VMEM((groups, GROUP, GROUP), F32), "mix": VMEM((2, GROUP, GROUP), BF16),
         "flow": VMEM((groups, 2 * heads, GROUP), F32), "sp": VMEM((groups, STATE, 256), F32),
@@ -732,7 +789,7 @@
         "w_work": VMEM((3, 4, 4, W_ROWS, 128), F32), "w_relay": VMEM((2, 2, W_ROWS, 128), F32),
         "w_final": VMEM((2, 4, W_ROWS, 128), F32), "w_mid": VMEM((4, W_ROWS, 128), F32),
         "w_relay2": VMEM((2, W_ROWS // 2, 128), F32), "w_final2": VMEM((2, W_ROWS, 128), F32),
-        "load_sems": dma((3,)), "pair_sems": dma((2, 3)), "chip_sems": dma((4, 16)),
+        "load_sems": dma((3,)), "pair_sems": dma((2, 2, 3)), "chip_sems": dma((2, 4, 16)),
         "core_sems": dma((2, chunks + 1)), "mp_sems": dma((2, 3)),
         "ring_send": dma((2 * chunks + 1, 12)), "ring_recv": dma((2 * chunks + 1, 12)),
     }
@@ -752,7 +809,7 @@
     anywhere, local = pl.BlockSpec(memory_space=pl.ANY), pl.BlockSpec(memory_space=VMEM)
     grad_wx, grad_wbc, totals = pl.pallas_call(
         kernel,
-        out_shape=(sds((block, width), F32), sds((block, 64), F32), sds((8, 128), F32)),
+        out_shape=(sds((block, width), F32), sds((64, block), F32), sds((8, 128), F32)),
         in_specs=[anywhere] * 3 + [local] * 6,
         out_specs=(local,) * 3,
         scratch_shapes=list(shapes.values()),
@@ -761,9 +818,15 @@
         compiler_params=pltpu.CompilerParams(
             collective_id=0, has_side_effects=True, vmem_limit_bytes=67043328
         ),
-    )(ssm_input, grad_out, layer_in, b_matrix, c_matrix, dt_raw, dt_bias[None, :], a_log[None, :],
-      jnp.repeat(d_skip, HEAD_DIM)[None, :])
-    return (grad_wx, grad_wbc, totals[0, :heads], totals[1, :heads], totals[2, :heads])
+    )(ssm_input, grad_out, layer_in, b_matrix, c_matrix, dt_raw.T, dt_bias[None, :], a_log[None, :],
+      d_skip[None, :])
+    grad_wx, grad_wbc, *rows = pl.pallas_call(
+        finish_kernel,
+        out_shape=(sds((block, width), F32), sds((64, block), F32)) + (sds((1, heads), F32),) * 3,
+        name="finish",
+        cost_estimate=pl.CostEstimate(flops=10**6, bytes_accessed=10**6, transcendentals=0),
+    )(grad_wx, grad_wbc, totals)
+    return (grad_wx, grad_wbc.T, *(row.reshape(heads) for row in rows))
 
 
 def solution(mesh):

time: 119 us -> 102 us (0.86)
  Pallas kernels: 110 us -> 101 us
  local copies, waits for them, and re-layouts: 7.77 us -> 0 us
    pallas_call x1 -> x2, Pallas kernels: 110 us -> 101 us  [the longest x1 99 us: on_device(): pl.pallas_call(kernel, out_shape=(sds((block, width), F32), sds((64, bloc...]
    unnamed x3 -> x0, local copies, waits for them, and re-layouts: 5.06 us -> none
    squeeze x1 -> x0, local copies, waits for them, and re-layouts: 1.31 us -> none  [on_device(): totals[2, :heads]]
where the time goes in v4:
time: 102 us; the launch traced here: 101 us
  Pallas kernels  101 us (99%)
    pallas_call x1, Pallas kernels, on_device(): pl.pallas_call(kernel, out_shape=(sds((block, width), F32), sds((64, bloc...  99 us

profile of v4, /device:TPU:0, one launch (start us, length us, event | category | flops | bytes accessed | tf_op | source)
XLA Modules:
  0.0 101.5 jit_solution(10878624827603139909)
XLA Ops:
  0.6 99.0 %whole.1 = (f32[80,1280]{1,0:T(8,128)}, f32[64,80]{1,0:T(8,128)}, f32[8,128]{1,0:T(8,128)}) custom-call(bf16[768,1280]{1,0:T(8,128)(2,1)} %refs_0_.1, bf16[768,1280]{1,0:T(8,128)(2,1)} %refs_1_.1, bf16[768,2560]{1,0:T(8,128)(2,1)} %refs_2_.1, bf16[768,128]{1,0:T(8,128)(2,1)} %refs_3_.1, bf16[768,128]{1,0:T(8,128)(2,1)} %refs_4_.1, f32[20,768]{1,0:T(8,128)} %bitcast.8, ...), custom_call_target="tpu_custom_call" | custom-call | flops 40000000000 | bytes 10000000 | tf_op jit(solution)/shard_map/whole/pallas_call | solution.py:810
  99.6 1.8 %finish.1 = (f32[80,1280]{1,0:T(8,128)}, f32[64,80]{1,0:T(8,128)}, f32[1,20]{1,0:T(1,128)}, f32[1,20]{1,0:T(1,128)}, f32[1,20]{1,0:T(1,128)}) custom-call(f32[80,1280]{1,0:T(8,128)} %get-tuple-element.13.wx_in, f32[64,80]{1,0:T(8,128)} %get-tuple-element.14.wbc_in, f32[8,128]{1,0:T(8,128)} %get-tuple-element.15.totals), custom_call_target="tpu_custom_call" | custom-call | flops 1000000 | bytes 1000000 | tf_op jit(solution)/shard_map/finish/pallas_call | solution.py:823

commit v5 on v4

--- a/solution.py
+++ b/solution.py
@@ -57,13 +57,25 @@
     return jnp.where(lane_iota((size, size), 0) >= lane_iota((size, size), 1), 1.0, 0.0)
 
 
-def spread(values, matrix):
+def halves(values):
     high = values.astype(BF16)
     low = (values - high.astype(F32)).astype(BF16)
-    return dot(high, matrix) + dot(low, matrix)
+    return jnp.concatenate([high, low], axis=1)
+
+
+def spread(first, second, matrix):
+    rows = first.shape[0]
+    wide = dot(jnp.concatenate([halves(first), halves(second)], axis=0), matrix)
+    return wide[0:rows], wide[rows : 2 * rows]
 
 
 MESH = pl.DeviceIdType.MESH
+ORDER = (
+    "F", "S0", "I0", "S1", "I1", "B0", "I2", "E0", "C0", "G0", "C1", "G1", "K0", "r00", "B1", "K1", "r10",
+    "E1", "C2", "r01", "G2", "I3", "K2", "r20", "r11", "r02", "C3", "G3", "I4", "K3", "r30", "r21", "r12",
+    "r03", "C4", "G4", "M", "P0", "T", "K4", "r40", "r31", "P1", "r22", "r13", "O", "g", "r41", "k", "r50",
+    "r04", "r32", "r23", "r51", "r14", "r42", "r33", "r52", "r24", "r43", "r34", "r53", "r44", "r54",
+)
 W_ROWS = 48
 
 
@@ -169,32 +181,29 @@
     a_ref[...] = dt * -jnp.exp(log_ref[...])
 
 
-def states(x, dy, b_ref, c_ref, dt_ref, slope_ref, a_ref, within_ref, last_ref, cols_ref, rows_ref, cross_ref,
-           decay_ref, spread_ref, parts, ends, tile, skip_ref, skip_wide):
+def states(x, dy, b_ref, c_ref, dt_ref, a_ref, within_ref, last_ref, decay_ref, spread_ref, parts, ends, tile):
     tokens, heads = dt_ref.shape
     groups = tokens // GROUP
     width = heads * HEAD_DIM
     tri = lower_ones(GROUP)
-    spread_m = spread_matrix(heads, BF16)
+    once = spread_matrix(heads, F32)
+    spread_m = jnp.concatenate([once, once], axis=0).astype(BF16)
     spread_ref[...] = spread_m
     spread_e = spread_matrix(heads, F32)
-    skip_wide[...] = dot_exact(jnp.broadcast_to(skip_ref[...], (8, heads)), spread_e)
     block_end = jnp.zeros((1, heads), F32)
     for g in range(groups):
         rows = slice(g * GROUP, (g + 1) * GROUP)
         dt = dt_ref[rows, :]
-        sums = dot_exact(tri, jnp.concatenate([a_ref[rows, :], dt, slope_ref[rows, :]], axis=1))
-        within = sums[:, 0:heads]
+        within = dot_exact(tri, a_ref[rows, :])
         last = within[GROUP - 1 : GROUP, :]
         block_end = block_end + last
         within_ref[rows, :] = within
         last_ref[g : g + 1, :] = last
         decay = dot_exact(jnp.broadcast_to(jnp.exp(last), (8, heads)), spread_e)[0:1, :]
         decay_ref[g : g + 1, :] = decay
-        fall = spread(dt * jnp.exp(last - within), spread_m)
+        fall, rise = spread(dt * jnp.exp(last - within), jnp.exp(within), spread_m)
         xw = (x[rows, :].astype(F32) * fall).astype(BF16)
         state = dot_tn(b_ref[rows, :], xw)
-        rise = spread(jnp.exp(within), spread_m)
         yw = (dy[rows, :].astype(F32) * rise).astype(BF16)
         grad = dot_tn(c_ref[rows, :], yw)
         if g < groups - 1:
@@ -209,12 +218,22 @@
             ends[0:STATE, 0:width] = decay * ends[0:STATE, 0:width] + state
             ends[STATE : 2 * STATE, 0:width] = ends[STATE : 2 * STATE, 0:width] + gain * grad
             gain = gain * decay
-        packed = jnp.concatenate([within * LOG2E - jnp.log2(dt), sums[:, heads : 3 * heads]], axis=1)
-        cols_ref[rows, :] = packed
-        rows_ref[g] = jnp.transpose(jnp.concatenate([within * LOG2E, sums[:, heads : 3 * heads]], axis=1))
-        cross_ref[g] = dot_nt(b_ref[rows, :], c_ref[rows, :])
     pad = jnp.concatenate([jnp.exp(block_end), jnp.zeros((1, 128 - heads), F32)], axis=1)
     tile[...] = jnp.broadcast_to(pad, (8, 128))
+
+
+def tables(b_ref, c_ref, dt_ref, slope_ref, within_ref, cols_ref, rows_ref, cross_ref, skip_ref, skip_wide):
+    tokens, heads = dt_ref.shape
+    tri = lower_ones(GROUP)
+    skip_wide[...] = dot_exact(jnp.broadcast_to(skip_ref[...], (8, heads)), spread_matrix(heads, F32))
+    for g in range(tokens // GROUP):
+        rows = slice(g * GROUP, (g + 1) * GROUP)
+        dt = dt_ref[rows, :]
+        rise2 = within_ref[rows, :] * LOG2E
+        sums = dot_exact(tri, jnp.concatenate([dt, slope_ref[rows, :]], axis=1))
+        cols_ref[rows, :] = jnp.concatenate([rise2 - jnp.log2(dt), sums], axis=1)
+        rows_ref[g] = jnp.transpose(jnp.concatenate([rise2, sums], axis=1))
+        cross_ref[g] = dot_nt(b_ref[rows, :], c_ref[rows, :])
 
 
 class Decays:
@@ -426,8 +445,7 @@
     for g in range(groups):
         rows = slice(g * GROUP, (g + 1) * GROUP)
         within = within_ref[rows, :]
-        fall = spread(dt_ref[rows, :] * jnp.exp(last_ref[g : g + 1, :] - within), spread_m)
-        rise = spread(jnp.exp(within), spread_m)
+        fall, rise = spread(dt_ref[rows, :] * jnp.exp(last_ref[g : g + 1, :] - within), jnp.exp(within), spread_m)
         xs = x[rows, cols].astype(F32)
         dys = dy[rows, cols].astype(F32)
         sp = sp_ref[g]
@@ -555,13 +573,10 @@
         pl.semaphore_signal(barrier, inc=1, device_id=partner, device_id_type=MESH)
 
     scalars(raw_ref, bias_ref, log_ref, s["dt"], s["slope"], s["a"])
-    s["mix"][:, GROUP // 2 : GROUP, 0 : GROUP // 2] = jnp.zeros((2, GROUP // 2, GROUP // 2), BF16)
-    s["v"][:, GROUP // 2 : GROUP, 0 : GROUP // 2] = jnp.zeros((s["v"].shape[0], GROUP // 2, GROUP // 2), F32)
-    s["inner"][...] = jnp.zeros_like(s["inner"])
     loads[0].wait()
     loads[1].wait()
-    states(x, dy, b_ref, c_ref, s["dt"], s["slope"], s["a"], s["within"], s["last"], s["cols"], s["rows"],
-           s["cross"], s["decay"], s["spread"], s["parts"], s["ends"], s["tile"], skip_ref, s["skip"])
+    states(x, dy, b_ref, c_ref, s["dt"], s["a"], s["within"], s["last"], s["decay"], s["spread"], s["parts"],
+           s["ends"], s["tile"])
     pl.semaphore_wait(barrier, len(partners))
     decays.give_pair()
     for one in carries:
@@ -578,14 +593,6 @@
     for one in carries:
         one.give_chips()
     loads[2].wait()
-    flip(li, lt, block)
-    decays.take()
-    carries[0].scan()
-    intra_part(0)
-    carries[1].scan()
-    intra_part(1)
-    carries[0].give_back()
-
     send_own, got, own = (work.at[i] for i in range(3))
     core_copies = {}
 
@@ -593,13 +600,13 @@
         cols = dx[:, j * 256 : (j + 1) * 256]
 
         def body(i, unused):
-            start = pl.multiple_of(i * 4 * block, 16)
-            res = dot(lt[1 - core, pl.ds(start, 4 * block), :], cols)
+            start = pl.multiple_of(i * 8 * block, 16)
+            res = dot(lt[1 - core, pl.ds(start, 8 * block), :], cols)
             for side in range(2):
-                send_own[j, side, i] = res[:, side * 128 : (side + 1) * 128].reshape(4, block, 128)
+                send_own[j, side, pl.ds(2 * i, 2)] = res[:, side * 128 : (side + 1) * 128].reshape(2, 4, block, 128)
             return unused
 
-        lax.fori_loop(0, 4, body, 0)
+        lax.fori_loop(0, 2, body, 0)
         core_copies[j] = remote(send_own.at[j], got.at[j], got_sems.at[0, j], got_sems.at[1, j], other)
         core_copies[j].start()
 
@@ -608,13 +615,14 @@
         cols = dx[:, j * 256 : (j + 1) * 256]
 
         def body(i, unused):
-            start = pl.multiple_of(i * 4 * block, 16)
-            res = dot(lt[core, pl.ds(start, 4 * block), :], cols)
+            start = pl.multiple_of(i * 8 * block, 16)
+            res = dot(lt[core, pl.ds(start, 8 * block), :], cols)
             for side in range(2):
-                own[j, side, i] = got[j, side, i] + res[:, side * 128 : (side + 1) * 128].reshape(4, block, 128)
+                part = res[:, side * 128 : (side + 1) * 128].reshape(2, 4, block, 128)
+                own[j, side, pl.ds(2 * i, 2)] = got[j, side, pl.ds(2 * i, 2)] + part
             return unused
 
-        lax.fori_loop(0, 4, body, 0)
+        lax.fori_loop(0, 2, body, 0)
 
     w_work = s["w_work"]
     dbc_in, packed = s["dbc_in"], s["packed"]
@@ -626,21 +634,13 @@
         stats = jnp.broadcast_to(s["stats"][...][None], (4, 8, 128))
         return jnp.concatenate([grads, stats], axis=1)
 
-    mp_copies = []
-
-    def give_mp():
-        mixed_grads(b_ref, c_ref, s["v"], s["dbc"], packed)
-        for k in (1, 2, 3):
-            target = around("mp", k)
-            copy = remote(packed.at[target["mp"]], dbc_in.at[k - 1], s["mp_sems"].at[0, k - 1],
-                          s["mp_sems"].at[1, k - 1], target)
-            copy.start()
-            mp_copies.append(copy)
+    quarter = packed.shape[1] // 2
+    mp_ring = RingSum("mp", lambda d, h: packed.at[d, pl.ds(h * quarter, quarter)], lambda h: s["mp_relay"].at[h],
+                      lambda w, h: dbc_in.at[w, pl.ds(h * quarter, quarter)],
+                      lambda k: s["mp_sems"].at[0, k], lambda k: s["mp_sems"].at[1, k], 0)
 
     def owned_cols():
-        for copy in mp_copies:
-            copy.wait_recv()
-        owned = packed[mp] + dbc_in[0] + dbc_in[1] + dbc_in[2]
+        owned = jnp.concatenate([mp_ring.result(0), mp_ring.result(1)], axis=0)
         return jnp.concatenate([owned[:, 0:64], owned[:, 64:128]], axis=0).astype(BF16)
 
     def give_narrow(cols):
@@ -689,38 +689,47 @@
                              s["w_relay2"], s["w_final2"],
                              lambda k: send.at[end, k], lambda k: recv.at[end, k], store_narrow)])
 
-    second = parts_of(heads * HEAD_DIM)[1][0] // 256
-    carries[0].finish()
-    combine_part(0)
-    give(0)
-    carries[1].give_back()
     cols_low = []
-    for t in range(chunks + 5):
-        if t + 1 < chunks:
-            if t + 1 >= 2:
-                intra_part(t + 1)
-            if t + 1 == second:
-                carries[1].finish()
-            combine_part(t + 1)
-            give(t + 1)
-        if t < chunks:
-            keep(t)
-        if t == chunks:
-            keep_narrow(cols_low[0])
-        for stage in range(5):
-            j = t - stage
-            if 0 <= j <= chunks:
-                if stage == 4 and j == chunks:
-                    core_copies[chunks].wait_send()
-                for one in streams[j]:
-                    one.run(stage)
-        if t == chunks - 2:
-            give_mp()
-        if t == chunks - 1:
-            statistics(s["dt"], s["slope"], log_ref, s["within"], s["last"], s["cols"], s["sums"], s["inner"],
-                       s["flow"], s["stats"])
-            cols_low.append(owned_cols())
-            give_narrow(cols_low[0])
+
+    def ring(j, stage):
+        if stage == 4 and j == chunks:
+            core_copies[chunks].wait_send()
+        for one in streams[j]:
+            one.run(stage)
+
+    def stats_part(n):
+        statistics(s["dt"], s["slope"], log_ref, s["within"], s["last"], s["cols"], s["sums"], s["inner"],
+                   s["flow"], s["stats"])
+
+    def flip_part(n):
+        s["mix"][:, GROUP // 2 : GROUP, 0 : GROUP // 2] = jnp.zeros((2, GROUP // 2, GROUP // 2), BF16)
+        s["v"][:, GROUP // 2 : GROUP, 0 : GROUP // 2] = jnp.zeros((s["v"].shape[0], GROUP // 2, GROUP // 2), F32)
+        s["inner"][...] = jnp.zeros_like(s["inner"])
+        flip(li, lt, block)
+        tables(b_ref, c_ref, s["dt"], s["slope"], s["within"], s["cols"], s["rows"], s["cross"], skip_ref, s["skip"])
+        decays.take()
+
+    steps = {
+        "F": flip_part,
+        "S": lambda n: carries[n].scan(),
+        "B": lambda n: carries[n].give_back(),
+        "E": lambda n: carries[n].finish(),
+        "I": intra_part,
+        "C": combine_part,
+        "G": give,
+        "K": keep,
+        "M": lambda n: mixed_grads(b_ref, c_ref, s["v"], s["dbc"], packed),
+        "P": lambda n: mp_ring.first() if n == 0 else mp_ring.second(),
+        "T": stats_part,
+        "O": lambda n: cols_low.append(owned_cols()),
+        "g": lambda n: give_narrow(cols_low[0]),
+        "k": lambda n: keep_narrow(cols_low[0]),
+    }
+    for step in ORDER:
+        if step[0] == "r":
+            ring(int(step[1]), int(step[2]))
+        else:
+            steps[step[0]](int(step[1:] or 0))
 
     half = block // 2
     turned = jnp.transpose(w_work[0, 0, 0, 0:half, :])
@@ -728,7 +737,8 @@
     total_ref[...] = w_work[0, 0, 0, half : half + 8, :]
     for one in carries:
         one.drain()
-    for copy in decays.copies + mp_copies:
+    mp_ring.drain()
+    for copy in decays.copies:
         copy.wait_send()
     for j in range(chunks):
         core_copies[j].wait_send()
@@ -772,7 +782,7 @@
         "dt": VMEM((tokens, heads), F32), "slope": VMEM((tokens, heads), F32), "a": VMEM((tokens, heads), F32),
         "within": VMEM((tokens, heads), F32), "last": VMEM((8, heads), F32), "cols": VMEM((tokens, 3 * heads), F32),
         "rows": VMEM((groups, 3 * heads, GROUP), F32), "cross": VMEM((groups, GROUP, GROUP), F32),
-        "decay": VMEM((8, width), F32), "spread": VMEM((heads, width), BF16),
+        "decay": VMEM((8, width), F32), "spread": VMEM((2 * heads, width), BF16),
         "parts": VMEM((2 * groups - 2, STATE, width), F32), "ends": VMEM((2 * STATE, width), F32),
         **carry_buffers(width), "tile": VMEM((8, 128), F32), "tile_pair": VMEM((8, 128), F32),
         "tile_chip": VMEM((8, 128), F32), "tile_got": VMEM((16, 8, 128), F32), "skip": VMEM((8, width), F32),
@@ -782,7 +792,7 @@
         "flow": VMEM((groups, 2 * heads, GROUP), F32), "sp": VMEM((groups, STATE, 256), F32),
         "gp": VMEM((groups, STATE, 256), F32), "dbc": VMEM((tokens, 2 * STATE), F32),
         "sums": VMEM((tokens, 128), F32), "inner": VMEM((8, width), F32), "stats": VMEM((8, 128), F32),
-        "packed": VMEM((4, tokens // 2, 128), F32), "dbc_in": VMEM((3, tokens // 2, 128), F32),
+        "packed": VMEM((4, tokens // 2, 128), F32), "dbc_in": VMEM((2, tokens // 2, 128), F32),
         "work": VMEM((3, chunks, 2, 4, 4, block, 128), F32), "relay": VMEM((2, chunks, 2, 2, block, 128), F32),
         "final": VMEM((2, chunks, 2, 4, block, 128), F32), "mid": VMEM((chunks, 2, 4, block, 128), F32),
         "relay2": VMEM((2, chunks, 2, block // 2, 128), F32), "final2": VMEM((2, chunks, 2, block, 128), F32),
@@ -790,7 +800,7 @@
         "w_final": VMEM((2, 4, W_ROWS, 128), F32), "w_mid": VMEM((4, W_ROWS, 128), F32),
         "w_relay2": VMEM((2, W_ROWS // 2, 128), F32), "w_final2": VMEM((2, W_ROWS, 128), F32),
         "load_sems": dma((3,)), "pair_sems": dma((2, 2, 3)), "chip_sems": dma((2, 4, 16)),
-        "core_sems": dma((2, chunks + 1)), "mp_sems": dma((2, 3)),
+        "core_sems": dma((2, chunks + 1)), "mp_sems": dma((2, 6)), "mp_relay": VMEM((2, tokens // 4, 128), F32),
         "ring_send": dma((2 * chunks + 1, 12)), "ring_recv": dma((2 * chunks + 1, 12)),
     }
 

time: 102 us -> 93.4 us (0.916)
  Pallas kernels: 101 us -> 92.6 us
    pallas_call x1, Pallas kernels: 99 us -> 90.8 us  [on_device(): pl.pallas_call(kernel, out_shape=(sds((block, width), F32), sds((64, bloc...]
where the time goes in v5:
time: 93.4 us; the launch traced here: 93.3 us
  Pallas kernels  92.6 us (99%)
    pallas_call x1, Pallas kernels, on_device(): pl.pallas_call(kernel, out_shape=(sds((block, width), F32), sds((64, bloc...  90.8 us

profile of v5, /device:TPU:0, one launch (start us, length us, event | category | flops | bytes accessed | tf_op | source)
XLA Modules:
  0.0 93.3 jit_solution(6773362315580905596)
XLA Ops:
  0.6 90.8 %whole.1 = (f32[80,1280]{1,0:T(8,128)}, f32[64,80]{1,0:T(8,128)}, f32[8,128]{1,0:T(8,128)}) custom-call(bf16[768,1280]{1,0:T(8,128)(2,1)} %refs_0_.1, bf16[768,1280]{1,0:T(8,128)(2,1)} %refs_1_.1, bf16[768,2560]{1,0:T(8,128)(2,1)} %refs_2_.1, bf16[768,128]{1,0:T(8,128)(2,1)} %refs_3_.1, bf16[768,128]{1,0:T(8,128)(2,1)} %refs_4_.1, f32[20,768]{1,0:T(8,128)} %bitcast.8, ...), custom_call_target="tpu_custom_call" | custom-call | flops 40000000000 | bytes 10000000 | tf_op jit(solution)/shard_map/whole/pallas_call | solution.py:820
  91.4 1.8 %finish.1 = (f32[80,1280]{1,0:T(8,128)}, f32[64,80]{1,0:T(8,128)}, f32[1,20]{1,0:T(1,128)}, f32[1,20]{1,0:T(1,128)}, f32[1,20]{1,0:T(1,128)}) custom-call(f32[80,1280]{1,0:T(8,128)} %get-tuple-element.13.wx_in, f32[64,80]{1,0:T(8,128)} %get-tuple-element.14.wbc_in, f32[8,128]{1,0:T(8,128)} %get-tuple-element.15.totals), custom_call_target="tpu_custom_call" | custom-call | flops 1000000 | bytes 1000000 | tf_op jit(solution)/shard_map/finish/pallas_call | solution.py:833

commit v6 on v5

--- a/solution.py
+++ b/solution.py
@@ -1,5 +1,5 @@
-import functools
 import math
+from types import SimpleNamespace
 
 import jax
 import jax.numpy as jnp
@@ -70,12 +70,6 @@
 
 
 MESH = pl.DeviceIdType.MESH
-ORDER = (
-    "F", "S0", "I0", "S1", "I1", "B0", "I2", "E0", "C0", "G0", "C1", "G1", "K0", "r00", "B1", "K1", "r10",
-    "E1", "C2", "r01", "G2", "I3", "K2", "r20", "r11", "r02", "C3", "G3", "I4", "K3", "r30", "r21", "r12",
-    "r03", "C4", "G4", "M", "P0", "T", "K4", "r40", "r31", "P1", "r22", "r13", "O", "g", "r41", "k", "r50",
-    "r04", "r32", "r23", "r51", "r14", "r42", "r33", "r52", "r24", "r43", "r34", "r53", "r44", "r54",
-)
 W_ROWS = 48
 
 
@@ -181,24 +175,34 @@
     a_ref[...] = dt * -jnp.exp(log_ref[...])
 
 
-def states(x, dy, b_ref, c_ref, dt_ref, a_ref, within_ref, last_ref, decay_ref, spread_ref, parts, ends, tile):
-    tokens, heads = dt_ref.shape
-    groups = tokens // GROUP
-    width = heads * HEAD_DIM
+def block_decay(a_ref, within_ref, last_ref, tile):
+    tokens, heads = a_ref.shape
     tri = lower_ones(GROUP)
-    once = spread_matrix(heads, F32)
-    spread_m = jnp.concatenate([once, once], axis=0).astype(BF16)
-    spread_ref[...] = spread_m
-    spread_e = spread_matrix(heads, F32)
     block_end = jnp.zeros((1, heads), F32)
-    for g in range(groups):
+    for g in range(tokens // GROUP):
         rows = slice(g * GROUP, (g + 1) * GROUP)
-        dt = dt_ref[rows, :]
         within = dot_exact(tri, a_ref[rows, :])
         last = within[GROUP - 1 : GROUP, :]
         block_end = block_end + last
         within_ref[rows, :] = within
         last_ref[g : g + 1, :] = last
+    pad = jnp.concatenate([jnp.exp(block_end), jnp.zeros((1, 128 - heads), F32)], axis=1)
+    tile[...] = jnp.broadcast_to(pad, (8, 128))
+
+
+def states(x, dy, b_ref, c_ref, dt_ref, within_ref, last_ref, decay_ref, spread_ref, parts, ends):
+    tokens, heads = dt_ref.shape
+    groups = tokens // GROUP
+    width = heads * HEAD_DIM
+    once = spread_matrix(heads, F32)
+    spread_m = jnp.concatenate([once, once], axis=0).astype(BF16)
+    spread_ref[...] = spread_m
+    spread_e = spread_matrix(heads, F32)
+    for g in range(groups):
+        rows = slice(g * GROUP, (g + 1) * GROUP)
+        dt = dt_ref[rows, :]
+        within = within_ref[rows, :]
+        last = last_ref[g : g + 1, :]
         decay = dot_exact(jnp.broadcast_to(jnp.exp(last), (8, heads)), spread_e)[0:1, :]
         decay_ref[g : g + 1, :] = decay
         fall, rise = spread(dt * jnp.exp(last - within), jnp.exp(within), spread_m)
@@ -218,8 +222,6 @@
             ends[0:STATE, 0:width] = decay * ends[0:STATE, 0:width] + state
             ends[STATE : 2 * STATE, 0:width] = ends[STATE : 2 * STATE, 0:width] + gain * grad
             gain = gain * decay
-    pad = jnp.concatenate([jnp.exp(block_end), jnp.zeros((1, 128 - heads), F32)], axis=1)
-    tile[...] = jnp.broadcast_to(pad, (8, 128))
 
 
 def tables(b_ref, c_ref, dt_ref, slope_ref, within_ref, cols_ref, rows_ref, cross_ref, skip_ref, skip_wide):
@@ -240,18 +242,18 @@
     def __init__(self, tile, pair, chip_tile, got, gains, heads, sems):
         self.tile, self.pair, self.chip_tile, self.got, self.gains = tile, pair, chip_tile, got, gains
         self.heads, self.sems = heads, sems
-        self.core = lax.axis_index("seq_2")
-        self.me = lax.axis_index("seq_0") * 4 + lax.axis_index("seq_1")
+        self.core = lax.axis_index(SEQ[2])
+        self.me = lax.axis_index(SEQ[0]) * 4 + lax.axis_index(SEQ[1])
 
     def chip(self, offset):
         index = lax.rem(self.me + offset, 16)
-        return index, {"seq_0": index // 4, "seq_1": lax.rem(index, 4)}
+        return index, {SEQ[0]: index // 4, SEQ[1]: lax.rem(index, 4)}
 
     def spread_rows(self, tile):
         return dot_exact(tile[:, 0 : self.heads], spread_matrix(self.heads, F32))
 
     def give_pair(self):
-        self.copies = [remote(self.tile, self.pair, self.sems.at[0, 0], self.sems.at[1, 0], {"seq_2": 1 - self.core})]
+        self.copies = [remote(self.tile, self.pair, self.sems.at[0, 0], self.sems.at[1, 0], {SEQ[2]: 1 - self.core})]
         self.copies[0].start()
 
     def give_chips(self):
@@ -280,7 +282,7 @@
         self.back, self.mine, self.yours, self.carry, self.gains = back, mine, yours, carry, decays.gains
         self.core_sems, self.sems, self.decays = core_sems, sems, decays
         self.core, self.me, self.chip = decays.core, decays.me, decays.chip
-        self.other = {"seq_2": 1 - self.core}
+        self.other = {SEQ[2]: 1 - self.core}
         self.width = out.shape[2]
         self.cols = pl.ds(left, self.width)
 
@@ -549,45 +551,45 @@
     wx_ref, wbc_ref, total_ref = refs_out
     block = wx_ref.shape[0]
     heads = raw_ref.shape[0]
-    x, dy, li, dx, lt = s["x"], s["dy"], s["li"], s["dx"], s["lt"]
-    work, got_sems = s["work"], s["core_sems"]
+    x, dy, li, dx, lt = s.x, s.dy, s.li, s.dx, s.lt
+    work, got_sems = s.work, s.core_sems
     chunks = work.shape[1]
-    core = lax.axis_index("seq_2")
+    core = lax.axis_index(SEQ[2])
     mp = lax.axis_index("mp")
-    other = {"seq_2": 1 - core}
+    other = {SEQ[2]: 1 - core}
 
     loads = []
     for n, (source, target) in enumerate(((x_hbm, x), (dy_hbm, dy), (li_hbm, li))):
-        load = pltpu.make_async_copy(source, target, s["load_sems"].at[n])
+        load = pltpu.make_async_copy(source, target, s.load_sems.at[n])
         load.start()
         loads.append(load)
 
-    decays = Decays(s["tile"], s["tile_pair"], s["tile_chip"], s["tile_got"], s["gains"], heads, s["tile_sems"])
+    decays = Decays(s.tile, s.tile_pair, s.tile_chip, s.tile_got, s.gains, heads, s.tile_sems)
     carries = []
     for n, (left, right) in enumerate(parts_of(heads * HEAD_DIM)):
-        buffers = [s[f"{name}{n}"] for name in ("pair", "out", "got", "scanned", "back", "mine", "yours")]
-        carries.append(Carry(decays, left, s["ends"], s["carry"], *buffers, s["pair_sems"].at[n], s["chip_sems"].at[n]))
+        buffers = s.carry_parts[n]
+        carries.append(Carry(decays, left, s.ends, s.carry, *buffers, s.pair_sems.at[n], s.chip_sems.at[n]))
     partners = [other] + [decays.chip(k)[1] for k in range(1, 16)] + [around("mp", k) for k in (1, 2, 3)]
     barrier = pltpu.get_barrier_semaphore()
     for partner in partners:
         pl.semaphore_signal(barrier, inc=1, device_id=partner, device_id_type=MESH)
 
-    scalars(raw_ref, bias_ref, log_ref, s["dt"], s["slope"], s["a"])
+    scalars(raw_ref, bias_ref, log_ref, s.dt, s.slope, s.a)
+    block_decay(s.a, s.within, s.last, s.tile)
+    pl.semaphore_wait(barrier, len(partners))
+    decays.give_pair()
     loads[0].wait()
     loads[1].wait()
-    states(x, dy, b_ref, c_ref, s["dt"], s["a"], s["within"], s["last"], s["decay"], s["spread"], s["parts"],
-           s["ends"], s["tile"])
-    pl.semaphore_wait(barrier, len(partners))
-    decays.give_pair()
+    states(x, dy, b_ref, c_ref, s.dt, s.within, s.last, s.decay, s.spread, s.parts, s.ends)
     for one in carries:
         one.give_pair()
 
     def intra_part(j):
-        intra(j, x, dy, s["cols"], s["rows"], s["cross"], s["v"], s["mix"], dx, s["flow"], heads)
+        intra(j, x, dy, s.cols, s.rows, s.cross, s.v, s.mix, dx, s.flow, heads)
 
     def combine_part(j):
-        combine(j, x, dy, b_ref, c_ref, s["dt"], s["within"], s["last"], s["decay"], s["spread"], s["skip"],
-                s["parts"], s["carry"], s["sp"], s["gp"], dx, s["dbc"], s["sums"], s["inner"])
+        combine(j, x, dy, b_ref, c_ref, s.dt, s.within, s.last, s.decay, s.spread, s.skip,
+                s.parts, s.carry, s.sp, s.gp, dx, s.dbc, s.sums, s.inner)
 
     decays.give_chips()
     for one in carries:
@@ -624,20 +626,20 @@
 
         lax.fori_loop(0, 2, body, 0)
 
-    w_work = s["w_work"]
-    dbc_in, packed = s["dbc_in"], s["packed"]
+    w_work = s.w_work
+    dbc_in, packed = s.dbc_in, s.packed
 
     def narrow(kind, i, cols):
         start = pl.multiple_of(i * 4 * block, 16)
         res = dot(lt[kind, pl.ds(start, 4 * block), :], cols).reshape(4, block, 64)
         grads = jnp.concatenate([res[:, 0 : block // 2], res[:, block // 2 : block]], axis=2)
-        stats = jnp.broadcast_to(s["stats"][...][None], (4, 8, 128))
+        stats = jnp.broadcast_to(s.stats[...][None], (4, 8, 128))
         return jnp.concatenate([grads, stats], axis=1)
 
     quarter = packed.shape[1] // 2
-    mp_ring = RingSum("mp", lambda d, h: packed.at[d, pl.ds(h * quarter, quarter)], lambda h: s["mp_relay"].at[h],
+    mp_ring = RingSum("mp", lambda d, h: packed.at[d, pl.ds(h * quarter, quarter)], lambda h: s.mp_relay.at[h],
                       lambda w, h: dbc_in.at[w, pl.ds(h * quarter, quarter)],
-                      lambda k: s["mp_sems"].at[0, k], lambda k: s["mp_sems"].at[1, k], 0)
+                      lambda k: s.mp_sems.at[0, k], lambda k: s.mp_sems.at[1, k], 0)
 
     def owned_cols():
         owned = jnp.concatenate([mp_ring.result(0), mp_ring.result(1)], axis=0)
@@ -674,22 +676,20 @@
     def store_narrow(half, value):
         w_work[0, 0, 0, half * (W_ROWS // 2) : (half + 1) * (W_ROWS // 2)] = value
 
-    send, recv = s["ring_send"], s["ring_recv"]
+    send, recv = s.ring_send, s.ring_recv
 
     def stream(j, side):
-        axes = ("seq_0", "seq_1") if side == 0 else ("seq_1", "seq_0")
+        axes = SEQ[:2] if side == 0 else SEQ[1::-1]
         n = 2 * j + side
-        return PlaneSum(*axes, side == 1, own.at[j, side], s["relay"].at[:, j, side], s["final"].at[:, j, side],
-                        s["mid"].at[j, side], s["relay2"].at[:, j, side], s["final2"].at[:, j, side],
+        return PlaneSum(*axes, side == 1, own.at[j, side], s.relay.at[:, j, side], s.final.at[:, j, side],
+                        s.mid.at[j, side], s.relay2.at[:, j, side], s.final2.at[:, j, side],
                         lambda k: send.at[n, k], lambda k: recv.at[n, k], store_wide(j, side))
 
     streams = [[stream(j, 0), stream(j, 1)] for j in range(chunks)]
     end = 2 * chunks
-    streams.append([PlaneSum("seq_0", "seq_1", False, w_work.at[2], s["w_relay"], s["w_final"], s["w_mid"],
-                             s["w_relay2"], s["w_final2"],
+    streams.append([PlaneSum(*SEQ[:2], False, w_work.at[2], s.w_relay, s.w_final, s.w_mid,
+                             s.w_relay2, s.w_final2,
                              lambda k: send.at[end, k], lambda k: recv.at[end, k], store_narrow)])
-
-    cols_low = []
 
     def ring(j, stage):
         if stage == 4 and j == chunks:
@@ -698,38 +698,81 @@
             one.run(stage)
 
     def stats_part(n):
-        statistics(s["dt"], s["slope"], log_ref, s["within"], s["last"], s["cols"], s["sums"], s["inner"],
-                   s["flow"], s["stats"])
+        statistics(s.dt, s.slope, log_ref, s.within, s.last, s.cols, s.sums, s.inner,
+                   s.flow, s.stats)
 
     def flip_part(n):
-        s["mix"][:, GROUP // 2 : GROUP, 0 : GROUP // 2] = jnp.zeros((2, GROUP // 2, GROUP // 2), BF16)
-        s["v"][:, GROUP // 2 : GROUP, 0 : GROUP // 2] = jnp.zeros((s["v"].shape[0], GROUP // 2, GROUP // 2), F32)
-        s["inner"][...] = jnp.zeros_like(s["inner"])
+        s.mix[:, GROUP // 2 : GROUP, 0 : GROUP // 2] = jnp.zeros((2, GROUP // 2, GROUP // 2), BF16)
+        s.v[:, GROUP // 2 : GROUP, 0 : GROUP // 2] = jnp.zeros((s.v.shape[0], GROUP // 2, GROUP // 2), F32)
+        s.inner[...] = jnp.zeros_like(s.inner)
         flip(li, lt, block)
-        tables(b_ref, c_ref, s["dt"], s["slope"], s["within"], s["cols"], s["rows"], s["cross"], skip_ref, s["skip"])
+        tables(b_ref, c_ref, s.dt, s.slope, s.within, s.cols, s.rows, s.cross, skip_ref, s.skip)
         decays.take()
 
-    steps = {
-        "F": flip_part,
-        "S": lambda n: carries[n].scan(),
-        "B": lambda n: carries[n].give_back(),
-        "E": lambda n: carries[n].finish(),
-        "I": intra_part,
-        "C": combine_part,
-        "G": give,
-        "K": keep,
-        "M": lambda n: mixed_grads(b_ref, c_ref, s["v"], s["dbc"], packed),
-        "P": lambda n: mp_ring.first() if n == 0 else mp_ring.second(),
-        "T": stats_part,
-        "O": lambda n: cols_low.append(owned_cols()),
-        "g": lambda n: give_narrow(cols_low[0]),
-        "k": lambda n: keep_narrow(cols_low[0]),
-    }
-    for step in ORDER:
-        if step[0] == "r":
-            ring(int(step[1]), int(step[2]))
-        else:
-            steps[step[0]](int(step[1:] or 0))
+    flip_part(0)
+    carries[0].scan()
+    intra_part(0)
+    carries[1].scan()
+    intra_part(1)
+    carries[0].give_back()
+    intra_part(2)
+    carries[0].finish()
+    combine_part(0)
+    give(0)
+    combine_part(1)
+    give(1)
+    carries[1].give_back()
+    keep(0)
+    ring(0, 0)
+    keep(1)
+    ring(1, 0)
+    carries[1].finish()
+    combine_part(2)
+    ring(0, 1)
+    give(2)
+    intra_part(3)
+    keep(2)
+    ring(2, 0)
+    ring(1, 1)
+    combine_part(3)
+    give(3)
+    ring(0, 2)
+    intra_part(4)
+    keep(3)
+    ring(3, 0)
+    ring(2, 1)
+    combine_part(4)
+    give(4)
+    mixed_grads(b_ref, c_ref, s.v, s.dbc, packed)
+    mp_ring.first()
+    ring(1, 2)
+    ring(0, 3)
+    keep(4)
+    ring(4, 0)
+    stats_part(0)
+    ring(3, 1)
+    mp_ring.second()
+    ring(2, 2)
+    ring(1, 3)
+    owned = owned_cols()
+    give_narrow(owned)
+    ring(4, 1)
+    keep_narrow(owned)
+    ring(5, 0)
+    ring(0, 4)
+    ring(3, 2)
+    ring(2, 3)
+    ring(5, 1)
+    ring(1, 4)
+    ring(4, 2)
+    ring(3, 3)
+    ring(5, 2)
+    ring(2, 4)
+    ring(4, 3)
+    ring(3, 4)
+    ring(5, 3)
+    ring(4, 4)
+    ring(5, 4)
 
     half = block // 2
     turned = jnp.transpose(w_work[0, 0, 0, 0:half, :])
@@ -752,15 +795,9 @@
     return ((0, cut), (cut, width))
 
 
-def carry_buffers(width):
-    found = {}
-    for n, (left, right) in enumerate(parts_of(width)):
-        wide = right - left
-        for name in ("out", "got", "scanned", "back"):
-            found[f"{name}{n}"] = VMEM((16, 8, wide), F32)
-        for name in ("pair", "mine", "yours"):
-            found[f"{name}{n}"] = VMEM((2, STATE // 2, wide), F32)
-    return found
+def carry_buffers(left, right):
+    rows, tiles = VMEM((2, STATE // 2, right - left), F32), VMEM((16, 8, right - left), F32)
+    return (rows, tiles, tiles, tiles, tiles, rows, rows)
 
 
 def finish_kernel(wx_in, wbc_in, totals, wx_ref, wbc_ref, log_ref, bias_ref, skip_ref):
@@ -776,33 +813,33 @@
     groups = tokens // GROUP
     half = STATE // 2
     dma = pltpu.SemaphoreType.DMA
-    return {
-        "x": VMEM((tokens, width), BF16), "dy": VMEM((tokens, width), BF16), "li": VMEM((tokens, wide), BF16),
-        "dx": VMEM((tokens, width), BF16), "lt": VMEM((2, wide // 2, tokens), BF16),
-        "dt": VMEM((tokens, heads), F32), "slope": VMEM((tokens, heads), F32), "a": VMEM((tokens, heads), F32),
-        "within": VMEM((tokens, heads), F32), "last": VMEM((8, heads), F32), "cols": VMEM((tokens, 3 * heads), F32),
-        "rows": VMEM((groups, 3 * heads, GROUP), F32), "cross": VMEM((groups, GROUP, GROUP), F32),
-        "decay": VMEM((8, width), F32), "spread": VMEM((2 * heads, width), BF16),
-        "parts": VMEM((2 * groups - 2, STATE, width), F32), "ends": VMEM((2 * STATE, width), F32),
-        **carry_buffers(width), "tile": VMEM((8, 128), F32), "tile_pair": VMEM((8, 128), F32),
-        "tile_chip": VMEM((8, 128), F32), "tile_got": VMEM((16, 8, 128), F32), "skip": VMEM((8, width), F32),
-        "tile_sems": dma((2, 16)),
-        "carry": VMEM((2 * STATE, width), F32), "gains": VMEM((32, width), F32),
-        "v": VMEM((groups, GROUP, GROUP), F32), "mix": VMEM((2, GROUP, GROUP), BF16),
-        "flow": VMEM((groups, 2 * heads, GROUP), F32), "sp": VMEM((groups, STATE, 256), F32),
-        "gp": VMEM((groups, STATE, 256), F32), "dbc": VMEM((tokens, 2 * STATE), F32),
-        "sums": VMEM((tokens, 128), F32), "inner": VMEM((8, width), F32), "stats": VMEM((8, 128), F32),
-        "packed": VMEM((4, tokens // 2, 128), F32), "dbc_in": VMEM((2, tokens // 2, 128), F32),
-        "work": VMEM((3, chunks, 2, 4, 4, block, 128), F32), "relay": VMEM((2, chunks, 2, 2, block, 128), F32),
-        "final": VMEM((2, chunks, 2, 4, block, 128), F32), "mid": VMEM((chunks, 2, 4, block, 128), F32),
-        "relay2": VMEM((2, chunks, 2, block // 2, 128), F32), "final2": VMEM((2, chunks, 2, block, 128), F32),
-        "w_work": VMEM((3, 4, 4, W_ROWS, 128), F32), "w_relay": VMEM((2, 2, W_ROWS, 128), F32),
-        "w_final": VMEM((2, 4, W_ROWS, 128), F32), "w_mid": VMEM((4, W_ROWS, 128), F32),
-        "w_relay2": VMEM((2, W_ROWS // 2, 128), F32), "w_final2": VMEM((2, W_ROWS, 128), F32),
-        "load_sems": dma((3,)), "pair_sems": dma((2, 2, 3)), "chip_sems": dma((2, 4, 16)),
-        "core_sems": dma((2, chunks + 1)), "mp_sems": dma((2, 6)), "mp_relay": VMEM((2, tokens // 4, 128), F32),
-        "ring_send": dma((2 * chunks + 1, 12)), "ring_recv": dma((2 * chunks + 1, 12)),
-    }
+    return dict(
+        x=VMEM((tokens, width), BF16), dy=VMEM((tokens, width), BF16), li=VMEM((tokens, wide), BF16),
+        dx=VMEM((tokens, width), BF16), lt=VMEM((2, wide // 2, tokens), BF16),
+        dt=VMEM((tokens, heads), F32), slope=VMEM((tokens, heads), F32), a=VMEM((tokens, heads), F32),
+        within=VMEM((tokens, heads), F32), last=VMEM((8, heads), F32), cols=VMEM((tokens, 3 * heads), F32),
+        rows=VMEM((groups, 3 * heads, GROUP), F32), cross=VMEM((groups, GROUP, GROUP), F32),
+        decay=VMEM((8, width), F32), spread=VMEM((2 * heads, width), BF16),
+        parts=VMEM((2 * groups - 2, STATE, width), F32), ends=VMEM((2 * STATE, width), F32),
+        tile=VMEM((8, 128), F32), tile_pair=VMEM((8, 128), F32),
+        tile_chip=VMEM((8, 128), F32), tile_got=VMEM((16, 8, 128), F32), skip=VMEM((8, width), F32),
+        tile_sems=dma((2, 16)),
+        carry=VMEM((2 * STATE, width), F32), gains=VMEM((32, width), F32),
+        v=VMEM((groups, GROUP, GROUP), F32), mix=VMEM((2, GROUP, GROUP), BF16),
+        flow=VMEM((groups, 2 * heads, GROUP), F32), sp=VMEM((groups, STATE, 256), F32),
+        gp=VMEM((groups, STATE, 256), F32), dbc=VMEM((tokens, 2 * STATE), F32),
+        sums=VMEM((tokens, 128), F32), inner=VMEM((8, width), F32), stats=VMEM((8, 128), F32),
+        packed=VMEM((4, tokens // 2, 128), F32), dbc_in=VMEM((2, tokens // 2, 128), F32),
+        work=VMEM((3, chunks, 2, 4, 4, block, 128), F32), relay=VMEM((2, chunks, 2, 2, block, 128), F32),
+        final=VMEM((2, chunks, 2, 4, block, 128), F32), mid=VMEM((chunks, 2, 4, block, 128), F32),
+        relay2=VMEM((2, chunks, 2, block // 2, 128), F32), final2=VMEM((2, chunks, 2, block, 128), F32),
+        w_work=VMEM((3, 4, 4, W_ROWS, 128), F32), w_relay=VMEM((2, 2, W_ROWS, 128), F32),
+        w_final=VMEM((2, 4, W_ROWS, 128), F32), w_mid=VMEM((4, W_ROWS, 128), F32),
+        w_relay2=VMEM((2, W_ROWS // 2, 128), F32), w_final2=VMEM((2, W_ROWS, 128), F32),
+        load_sems=dma((3,)), pair_sems=dma((2, 2, 3)), chip_sems=dma((2, 4, 16)),
+        core_sems=dma((2, chunks + 1)), mp_sems=dma((2, 6)), mp_relay=VMEM((2, tokens // 4, 128), F32),
+        ring_send=dma((2 * chunks + 1, 12)), ring_recv=dma((2 * chunks + 1, 12)),
+    )
 
 
 def on_device(layer_in, ssm_input, b_matrix, c_matrix, dt_raw, dt_bias, a_log, d_skip, grad_out):
@@ -813,8 +850,14 @@
     sds = jax.ShapeDtypeStruct
     shapes = scratch(tokens, heads, block, wide)
 
+    held = [carry_buffers(*part) for part in parts_of(width)]
+    count = len(held[0])
+
     def kernel(*refs):
-        whole_kernel(refs[:9], refs[9:12], dict(zip(shapes, refs[12:])))
+        space = SimpleNamespace(**dict(zip(shapes, refs[12:])))
+        rest = refs[12 + len(shapes) :]
+        space.carry_parts = [rest[n * count : (n + 1) * count] for n in range(len(held))]
+        whole_kernel(refs[:9], refs[9:12], space)
 
     anywhere, local = pl.BlockSpec(memory_space=pl.ANY), pl.BlockSpec(memory_space=VMEM)
     grad_wx, grad_wbc, totals = pl.pallas_call(
@@ -822,7 +865,7 @@
         out_shape=(sds((block, width), F32), sds((64, block), F32), sds((8, 128), F32)),
         in_specs=[anywhere] * 3 + [local] * 6,
         out_specs=(local,) * 3,
-        scratch_shapes=list(shapes.values()),
+        scratch_shapes=list(shapes.values()) + [one for part in held for one in part],
         name="whole",
         cost_estimate=pl.CostEstimate(flops=4 * 10**10, bytes_accessed=10**7, transcendentals=0),
         compiler_params=pltpu.CompilerParams(

time: 93.4 us -> 91.8 us (0.983)
  Pallas kernels: 92.6 us -> 91.1 us
    pallas_call x1, Pallas kernels: 90.8 us -> 89.2 us  [on_device(): pl.pallas_call(kernel, out_shape=(sds((block, width), F32), sds((64, bloc...]
where the time goes in v6:
time: 91.8 us; the launch traced here: 91.7 us
  Pallas kernels  91.1 us (99%)
    pallas_call x1, Pallas kernels, on_device(): pl.pallas_call(kernel, out_shape=(sds((block, width), F32), sds((64, bloc...  89.2 us

profile of v6, /device:TPU:0, one launch (start us, length us, event | category | flops | bytes accessed | tf_op | source)
XLA Modules:
  0.0 91.7 jit_solution(15723539159103943923)
XLA Ops:
  0.6 89.2 %whole.1 = (f32[80,1280]{1,0:T(8,128)}, f32[64,80]{1,0:T(8,128)}, f32[8,128]{1,0:T(8,128)}) custom-call(bf16[768,1280]{1,0:T(8,128)(2,1)} %refs_0_.1, bf16[768,1280]{1,0:T(8,128)(2,1)} %refs_1_.1, bf16[768,2560]{1,0:T(8,128)(2,1)} %refs_2_.1, bf16[768,128]{1,0:T(8,128)(2,1)} %refs_3_.1, bf16[768,128]{1,0:T(8,128)(2,1)} %refs_4_.1, f32[20,768]{1,0:T(8,128)} %bitcast.8, ...), custom_call_target="tpu_custom_call" | custom-call | flops 40000000000 | bytes 10000000 | tf_op jit(solution)/shard_map/whole/pallas_call | solution.py:863
  89.9 1.8 %finish.1 = (f32[80,1280]{1,0:T(8,128)}, f32[64,80]{1,0:T(8,128)}, f32[1,20]{1,0:T(1,128)}, f32[1,20]{1,0:T(1,128)}, f32[1,20]{1,0:T(1,128)}) custom-call(f32[80,1280]{1,0:T(8,128)} %get-tuple-element.13.wx_in, f32[64,80]{1,0:T(8,128)} %get-tuple-element.14.wbc_in, f32[8,128]{1,0:T(8,128)} %get-tuple-element.15.totals), custom_call_target="tpu_custom_call" | custom-call | flops 1000000 | bytes 1000000 | tf_op jit(solution)/shard_map/finish/pallas_call | solution.py:876
